TPU v7x, 16 devices: a whole 2x2x2 slice. The times are simulated.
16 devices in a mesh: dp: 4 (over z, y), cp: 4 (over x, core).
Axes of the slice: x: 2, y: 2, z: 2, core: 2. Of those that a mesh axis runs over, the one named last changes fastest.
Arguments:
- q_tokens: bfloat16 [4096, 32, 128], P(('dp', 'cp')), parts along dimension 0
- k_tokens: bfloat16 [4096, 8, 128], P(('dp', 'cp')), parts along dimension 0
- v_tokens: bfloat16 [4096, 8, 128], P(('dp', 'cp')), parts along dimension 0
- d_out: bfloat16 [4096, 32, 128], P(('dp', 'cp')), parts along dimension 0
- key_valid: int32 [4096], P(('dp', 'cp')), parts along dimension 0
- cu_seqlens: int32 [12], P('dp'), parts along dimension 0
Outputs:
- output 1: bfloat16 [4096, 32, 128], P(('dp', 'cp')), parts along dimension 0
- output 2: float32 [4096, 32], P(('dp', 'cp')), parts along dimension 0
- output 3: bfloat16 [4096, 32, 128], P(('dp', 'cp')), parts along dimension 0
- output 4: bfloat16 [4096, 8, 128], P(('dp', 'cp')), parts along dimension 0
- output 5: bfloat16 [4096, 8, 128], P(('dp', 'cp')), parts along dimension 0
There are 4 independent parts. A program takes and returns all parts, laid end to end along the dimension named above; each array names one.
All inputs are finite; a program needn't handle non-finite values.
Results may differ from a plain program's by a relative error of at most 0.00877425.
Values are sent between devices in bfloat16 or wider.
A program may use at most 1 GiB of HBM per device.

v0:
```python
import jax
import jax.numpy as jnp
from jax import lax
from jax.sharding import PartitionSpec as P

MASK_FILL = -1.0e30


def token_coords(cu_seqlens, rank_ids, local_ids, cp_size):
    starts = cu_seqlens[:-1] // cp_size
    doc_id = jnp.sum((local_ids[..., None] >= starts).astype(jnp.int32), axis=-1) - 1
    seg_start = cu_seqlens[doc_id]
    piece_len = (cu_seqlens[doc_id + 1] - seg_start) // (2 * cp_size)
    within = local_ids - seg_start // cp_size
    in_upper = (within >= piece_len).astype(jnp.int32)
    piece_idx = rank_ids + in_upper * (2 * cp_size - 1 - 2 * rank_ids)
    position = seg_start + piece_idx * piece_len + within - in_upper * piece_len
    return doc_id, position


def solution(mesh):
    cp_size = mesh.shape['cp']
    tok_spec = P(('dp', 'cp'), None, None)
    lse_spec = P(('dp', 'cp'), None)
    row_spec = P(('dp', 'cp'))
    bound_spec = P('dp')

    def local_attention(q_loc, k_loc, v_loc, do_loc, valid_loc, cu_loc):
        tok_count, n_heads, head_dim = q_loc.shape
        kv_heads = k_loc.shape[1]
        group_size = n_heads // kv_heads
        score_scale = head_dim ** -0.5
        my_rank = lax.axis_index('cp')
        local_ids = jnp.arange(tok_count)
        doc_q, pos_q = token_coords(cu_loc, my_rank, local_ids, cp_size)
        rank_grid = jnp.broadcast_to(jnp.arange(cp_size)[:, None], (cp_size, tok_count))
        local_grid = jnp.broadcast_to(local_ids[None, :], (cp_size, tok_count))
        doc_all, pos_all = token_coords(cu_loc, rank_grid, local_grid, cp_size)
        k_all = lax.all_gather(k_loc, 'cp')
        v_all = lax.all_gather(v_loc, 'cp')
        ok_all = lax.all_gather(valid_loc, 'cp') > 0
        q_grouped = q_loc.reshape(tok_count, kv_heads, group_size, head_dim)
        do_grouped = do_loc.reshape(tok_count, kv_heads, group_size, head_dim)
        key_xs = (k_all, v_all, doc_all, pos_all, ok_all)

        def block_scores(k_blk, doc_k, pos_k, ok_k):
            allowed = (doc_q[:, None] == doc_k[None, :]) & (pos_k[None, :] <= pos_q[:, None]) & ok_k[None, :]
            scores = jnp.einsum('qhgd,khd->hgqk', q_grouped, k_blk, preferred_element_type=jnp.float32) * score_scale
            return jnp.where(allowed, scores, MASK_FILL), allowed

        def fwd_step(run_state, blk_data):
            m_run, l_run, acc_run = run_state
            k_blk, v_blk, doc_k, pos_k, ok_k = blk_data
            scores, allowed = block_scores(k_blk, doc_k, pos_k, ok_k)
            m_new = jnp.maximum(m_run, jnp.max(scores, axis=-1))
            weights = jnp.where(allowed, jnp.exp(scores - m_new[..., None]), 0.0)
            rescale = jnp.exp(m_run - m_new)
            l_new = rescale * l_run + jnp.sum(weights, axis=-1)
            acc_new = acc_run * rescale[..., None] + jnp.einsum('hgqk,khd->hgqd', weights.astype(jnp.bfloat16), v_blk, preferred_element_type=jnp.float32)
            return (m_new, l_new, acc_new), None

        m_init = jnp.full((kv_heads, group_size, tok_count), MASK_FILL, jnp.float32)
        l_init = jnp.zeros((kv_heads, group_size, tok_count), jnp.float32)
        acc_init = jnp.zeros((kv_heads, group_size, tok_count, head_dim), jnp.float32)
        m_fin, l_fin, acc_fin = lax.scan(fwd_step, (m_init, l_init, acc_init), key_xs)[0]
        has_key = l_fin > 0
        safe_den = jnp.where(has_key, l_fin, 1.0)
        out_hgqd = jnp.where(has_key[..., None], acc_fin / safe_den[..., None], 0.0)
        out_grouped = jnp.transpose(out_hgqd, (2, 0, 1, 3)).astype(jnp.bfloat16)
        lse_hgq = jnp.where(has_key, m_fin + jnp.log(safe_den), 0.0)
        row_delta = jnp.einsum('qhgd,qhgd->hgq', do_grouped, out_grouped, preferred_element_type=jnp.float32)

        def bwd_step(dq_run, blk_data):
            k_blk, v_blk, doc_k, pos_k, ok_k = blk_data
            scores, allowed = block_scores(k_blk, doc_k, pos_k, ok_k)
            weights = jnp.where(allowed, jnp.exp(scores - lse_hgq[..., None]), 0.0)
            d_prob = jnp.einsum('qhgd,khd->hgqk', do_grouped, v_blk, preferred_element_type=jnp.float32)
            d_score = (weights * (d_prob - row_delta[..., None])).astype(jnp.bfloat16)
            dq_new = dq_run + jnp.einsum('hgqk,khd->qhgd', d_score, k_blk, preferred_element_type=jnp.float32)
            dk_blk = jnp.einsum('hgqk,qhgd->khd', d_score, q_grouped, preferred_element_type=jnp.float32)
            dv_blk = jnp.einsum('hgqk,qhgd->khd', weights.astype(jnp.bfloat16), do_grouped, preferred_element_type=jnp.float32)
            return dq_new, (dk_blk, dv_blk)

        dq_init = jnp.zeros((tok_count, kv_heads, group_size, head_dim), jnp.float32)
        dq_fin, kv_parts = lax.scan(bwd_step, dq_init, key_xs)
        dk_own = lax.psum_scatter(kv_parts[0], 'cp', scatter_dimension=0, tiled=False)
        dv_own = lax.psum_scatter(kv_parts[1], 'cp', scatter_dimension=0, tiled=False)
        attn_out = out_grouped.reshape(tok_count, n_heads, head_dim)
        log_sumexp = jnp.transpose(lse_hgq, (2, 0, 1)).reshape(tok_count, n_heads)
        d_query = (dq_fin * score_scale).astype(jnp.bfloat16).reshape(tok_count, n_heads, head_dim)
        d_key = (dk_own * score_scale).astype(jnp.bfloat16)
        d_value = dv_own.astype(jnp.bfloat16)
        return attn_out, log_sumexp, d_query, d_key, d_value

    return jax.shard_map(local_attention, mesh=mesh, in_specs=(tok_spec, tok_spec, tok_spec, tok_spec, row_spec, bound_spec), out_specs=(tok_spec, lse_spec, tok_spec, tok_spec, tok_spec), check_vma=False)
```

profile of v0, /device:TPU:0, one launch (start us, length us, event | category | flops | bytes accessed | tf_op | source)
XLA Modules:
  0.0 308.8 jit_solution(7115190216428728233)
XLA Ops:
  9.5 5.9 %gather_fusion = s32[1024]{0:T(1024)S(1)} fusion(s32[3]{0:T(128)} %param.15, s32[1024]{0:T(1024)S(1)} %broadcast_clamp_fusion.1), kind=kCustom, calls=%fused_computation | custom fusion | bytes 12288 | tf_op jit(solution)/shard_map/gather | solution.py:12
  15.5 6.6 %gather_fusion.1 = s32[1024]{0:T(1024)S(1)} fusion(s32[3]{0:T(128)S(1)} %copy-done, s32[1024]{0:T(1024)S(1)} %broadcast_clamp_fusion), kind=kCustom, calls=%fused_computation.1 | custom fusion | bytes 12288 | tf_op jit(solution)/shard_map/gather | solution.py:13
  24.5 6.3 %all-gather.3 = s32[4,1,256]{2,1,0:T(1,128)S(1)} all-gather(s32[1,1,256]{2,1,0:T(1,128)S(1)} %bitcast.207), channel_id=2, replica_groups=mesh['dp'=4,'cp'=4] {'cp'}, dimensions={0}, use_global_device_ids=true | all-gather | bytes 5120 | tf_op jit(solution)/shard_map/all_gather | solution.py:41
  40.7 14.2 %all-gather.9.cloned.1.call-done = bf16[1024,8,128]{2,1,0:T(8,128)(2,1)} async-done(((bf16[256,8,128]{2,1,0:T(8,128)(2,1)}), bf16[1024,8,128]{2,1,0:T(8,128)(2,1)}) %all-gather.9.cloned.1.call-update) | async-done | bytes 2097168 | tf_op jit(solution)/shard_map/all_gather | solution.py:40
  58.3 73.5 %while.30 = (s32[]{:T(128)}, f32[8,4,256]{2,1,0:T(4,128)S(1)}, f32[8,4,256]{2,1,0:T(4,128)S(1)}, f32[8,4,256,128]{3,2,1,0:T(8,128)}, s32[256]{0:T(256)S(1)}, /*i...) while((s32[]{:T(128)}, f32[8,4,256]{2,1,0:T(4,128)S(1)}, ...), condition=%wide.region_5.6_spmd.clone, body=%wide.region_2.5_spmd.clone.sunk | while | flops 1104453632 | bytes 71051192 | solution.py:65
  58.5 5.6 %fusion.90 = (f32[8,4,256]{2,1,0:T(4,128)S(1)}, f32[8,256,256,4]{2,1,3,0:T(8,128)}) fusion(pred[256,256]{0,1:T(8,128)(4,1)S(1)} %and_and_fusion.4, bf16[256,8,4,128]{3,0,2,1:T(8,128)(2,1)S(1)} %get-tuple-element.644, bf16[4,256,8,128]{3,1,2,0:T(8,128)(2,1)} %get-tuple-element.643, s32[]{:T(128)} %get-tuple-element.620), kind=kOutput, calls=%fused_computation.4.clone.1 | convolution fusion | flops 543154176 | bytes 11108864 | tf_op jit(solution)/shard_map/while/body/eval_jaxpr/qhgd,khd->hgqk/dot_general | solution.py:48
  64.1 4.7 %fusion.91 = f32[8,4,256]{2,1,0:T(4,128)S(1)} fusion(f32[8,256,256,4]{2,1,3,0:T(8,128)} %get-tuple-element.586, f32[8,4,256]{2,1,0:T(4,128)S(1)} %select_maximum_fusion.2, pred[256,256]{0,1:T(8,128)(4,1)S(1)} %and_and_fusion.4), kind=kLoop, calls=%fused_computation.6.clone.1 | loop fusion | flops 10477568 | bytes 8519680 | tf_op jit(solution)/shard_map/while/body/eval_jaxpr/reduce_sum | solution.py:58
  70.0 5.9 %fusion.93 = f32[8,4,256,128]{3,2,1,0:T(8,128)} fusion(f32[8,4,256,128]{3,2,1,0:T(8,128)} %get-tuple-element.623, f32[8,4,256]{2,1,0:T(4,128)S(1)} %get-tuple-element.588, pred[]{:T(512)S(6)} %compare.36, f32[8,256,256,4]{2,1,3,0:T(8,128)S(1)} %copy-done.1, f32[8,4,256]{2,1,0:T(4,128)S(1)} %select_maximum_fusion.2, ...), kind=kOutput, calls=%fused_computation.9.clone.1 | convolution fusion | flops 550502400 | bytes 17433088 | tf_op jit(solution)/shard_map/while/body/eval_jaxpr/hgqk,khd->hgqd/dot_general | solution.py:59
  76.1 5.6 %fusion.90 = (f32[8,4,256]{2,1,0:T(4,128)S(1)}, f32[8,256,256,4]{2,1,3,0:T(8,128)}) fusion(pred[256,256]{0,1:T(8,128)(4,1)S(1)} %and_and_fusion.4, bf16[256,8,4,128]{3,0,2,1:T(8,128)(2,1)S(1)} %get-tuple-element.644, bf16[4,256,8,128]{3,1,2,0:T(8,128)(2,1)} %get-tuple-element.643, s32[]{:T(128)} %get-tuple-element.620), kind=kOutput, calls=%fused_computation.4.clone.1 | convolution fusion | flops 543154176 | bytes 11108864 | tf_op jit(solution)/shard_map/while/body/eval_jaxpr/qhgd,khd->hgqk/dot_general | solution.py:48
  81.8 4.7 %fusion.91 = f32[8,4,256]{2,1,0:T(4,128)S(1)} fusion(f32[8,256,256,4]{2,1,3,0:T(8,128)} %get-tuple-element.586, f32[8,4,256]{2,1,0:T(4,128)S(1)} %select_maximum_fusion.2, pred[256,256]{0,1:T(8,128)(4,1)S(1)} %and_and_fusion.4), kind=kLoop, calls=%fused_computation.6.clone.1 | loop fusion | flops 10477568 | bytes 8519680 | tf_op jit(solution)/shard_map/while/body/eval_jaxpr/reduce_sum | solution.py:58
  87.6 7.0 %fusion.93 = f32[8,4,256,128]{3,2,1,0:T(8,128)} fusion(f32[8,4,256,128]{3,2,1,0:T(8,128)} %get-tuple-element.623, f32[8,4,256]{2,1,0:T(4,128)S(1)} %get-tuple-element.588, pred[]{:T(512)S(6)} %compare.36, f32[8,256,256,4]{2,1,3,0:T(8,128)S(1)} %copy-done.1, f32[8,4,256]{2,1,0:T(4,128)S(1)} %select_maximum_fusion.2, ...), kind=kOutput, calls=%fused_computation.9.clone.1 | convolution fusion | flops 550502400 | bytes 17433088 | tf_op jit(solution)/shard_map/while/body/eval_jaxpr/hgqk,khd->hgqd/dot_general | solution.py:59
  94.8 5.6 %fusion.90 = (f32[8,4,256]{2,1,0:T(4,128)S(1)}, f32[8,256,256,4]{2,1,3,0:T(8,128)}) fusion(pred[256,256]{0,1:T(8,128)(4,1)S(1)} %and_and_fusion.4, bf16[256,8,4,128]{3,0,2,1:T(8,128)(2,1)S(1)} %get-tuple-element.644, bf16[4,256,8,128]{3,1,2,0:T(8,128)(2,1)} %get-tuple-element.643, s32[]{:T(128)} %get-tuple-element.620), kind=kOutput, calls=%fused_computation.4.clone.1 | convolution fusion | flops 543154176 | bytes 11108864 | tf_op jit(solution)/shard_map/while/body/eval_jaxpr/qhgd,khd->hgqk/dot_general | solution.py:48
  106.2 7.0 %fusion.93 = f32[8,4,256,128]{3,2,1,0:T(8,128)} fusion(f32[8,4,256,128]{3,2,1,0:T(8,128)} %get-tuple-element.623, f32[8,4,256]{2,1,0:T(4,128)S(1)} %get-tuple-element.588, pred[]{:T(512)S(6)} %compare.36, f32[8,256,256,4]{2,1,3,0:T(8,128)S(1)} %copy-done.1, f32[8,4,256]{2,1,0:T(4,128)S(1)} %select_maximum_fusion.2, ...), kind=kOutput, calls=%fused_computation.9.clone.1 | convolution fusion | flops 550502400 | bytes 17433088 | tf_op jit(solution)/shard_map/while/body/eval_jaxpr/hgqk,khd->hgqd/dot_general | solution.py:59
  113.4 5.6 %fusion.90 = (f32[8,4,256]{2,1,0:T(4,128)S(1)}, f32[8,256,256,4]{2,1,3,0:T(8,128)}) fusion(pred[256,256]{0,1:T(8,128)(4,1)S(1)} %and_and_fusion.4, bf16[256,8,4,128]{3,0,2,1:T(8,128)(2,1)S(1)} %get-tuple-element.644, bf16[4,256,8,128]{3,1,2,0:T(8,128)(2,1)} %get-tuple-element.643, s32[]{:T(128)} %get-tuple-element.620), kind=kOutput, calls=%fused_computation.4.clone.1 | convolution fusion | flops 543154176 | bytes 11108864 | tf_op jit(solution)/shard_map/while/body/eval_jaxpr/qhgd,khd->hgqk/dot_general | solution.py:48
  119.0 4.7 %fusion.91 = f32[8,4,256]{2,1,0:T(4,128)S(1)} fusion(f32[8,256,256,4]{2,1,3,0:T(8,128)} %get-tuple-element.586, f32[8,4,256]{2,1,0:T(4,128)S(1)} %select_maximum_fusion.2, pred[256,256]{0,1:T(8,128)(4,1)S(1)} %and_and_fusion.4), kind=kLoop, calls=%fused_computation.6.clone.1 | loop fusion | flops 10477568 | bytes 8519680 | tf_op jit(solution)/shard_map/while/body/eval_jaxpr/reduce_sum | solution.py:58
  124.9 7.0 %fusion.93 = f32[8,4,256,128]{3,2,1,0:T(8,128)} fusion(f32[8,4,256,128]{3,2,1,0:T(8,128)} %get-tuple-element.623, f32[8,4,256]{2,1,0:T(4,128)S(1)} %get-tuple-element.588, pred[]{:T(512)S(6)} %compare.36, f32[8,256,256,4]{2,1,3,0:T(8,128)S(1)} %copy-done.1, f32[8,4,256]{2,1,0:T(4,128)S(1)} %select_maximum_fusion.2, ...), kind=kOutput, calls=%fused_computation.9.clone.1 | convolution fusion | flops 550502400 | bytes 17433088 | tf_op jit(solution)/shard_map/while/body/eval_jaxpr/hgqk,khd->hgqd/dot_general | solution.py:59
  131.9 8.0 %fusion.49 = (f32[8,4,256]{2,1,0:T(4,128)S(1)}, bf16[8,4,256,128]{3,2,1,0:T(8,128)(2,1)}) fusion(bf16[8,4,256,128]{3,2,1,0:T(8,128)(2,1)} %bitcast.189, f32[8,4,256,128]{3,2,1,0:T(8,128)} %get-tuple-element.149, f32[8,4,256]{2,1,0:T(4,128)S(1)} %broadcast_select_fusion, pred[8,4,256]{2,1,0:T(4,128)(4,1)S(1)} %get-tuple-element.408), kind=kLoop, calls=%fused_computation.66 | loop fusion | flops 7331840 | bytes 8462336 | tf_op jit(solution)/shard_map/qhgd,qhgd->hgq/dot_general | solution.py:71
  139.8 77.6 %while.31 = (s32[]{:T(128)}, f32[256,8,4,128]{0,3,2,1:T(8,128)}, f32[4,256,8,128]{3,2,1,0:T(8,128)}, f32[4,256,8,128]{3,2,1,0:T(8,128)}, bf16[4,256,8,128]{3,1,2...) while((s32[]{:T(128)}, f32[256,8,4,128]{0,3,2,1:T(8,128)}, ...), condition=%wide.region_7.8_spmd.clone, body=%wide.region_6.7_spmd.clone.sunk | while | flops 2711879680 | bytes 87862248 | solution.py:85
  153.3 5.1 %bitcast_add_fusion.4 = f32[256,8,4,128]{0,3,2,1:T(8,128)} fusion(f32[256,8,4,128]{0,3,2,1:T(8,128)} %get-tuple-element.666, bf16[8,4,256,256]{2,3,1,0:T(8,128)(2,1)} %copy-done.2, pred[]{:T(512)S(6)} %compare.37, bf16[4,256,8,128]{3,1,2,0:T(8,128)(2,1)} %get-tuple-element.686, s32[]{:T(128)} %get-tuple-element.665), kind=kOutput, calls=%fused_computation.41.clone.1 | convolution fusion | flops 538968064 | bytes 13107713 | tf_op jit(solution)/shard_map/while/body/eval_jaxpr/hgqk,khd->qhgd/dot_general | solution.py:79
  171.7 6.4 %bitcast_add_fusion.4 = f32[256,8,4,128]{0,3,2,1:T(8,128)} fusion(f32[256,8,4,128]{0,3,2,1:T(8,128)} %get-tuple-element.666, bf16[8,4,256,256]{2,3,1,0:T(8,128)(2,1)} %copy-done.2, pred[]{:T(512)S(6)} %compare.37, bf16[4,256,8,128]{3,1,2,0:T(8,128)(2,1)} %get-tuple-element.686, s32[]{:T(128)} %get-tuple-element.665), kind=kOutput, calls=%fused_computation.41.clone.1 | convolution fusion | flops 538968064 | bytes 13107713 | tf_op jit(solution)/shard_map/while/body/eval_jaxpr/hgqk,khd->qhgd/dot_general | solution.py:79
  191.4 6.4 %bitcast_add_fusion.4 = f32[256,8,4,128]{0,3,2,1:T(8,128)} fusion(f32[256,8,4,128]{0,3,2,1:T(8,128)} %get-tuple-element.666, bf16[8,4,256,256]{2,3,1,0:T(8,128)(2,1)} %copy-done.2, pred[]{:T(512)S(6)} %compare.37, bf16[4,256,8,128]{3,1,2,0:T(8,128)(2,1)} %get-tuple-element.686, s32[]{:T(128)} %get-tuple-element.665), kind=kOutput, calls=%fused_computation.41.clone.1 | convolution fusion | flops 538968064 | bytes 13107713 | tf_op jit(solution)/shard_map/while/body/eval_jaxpr/hgqk,khd->qhgd/dot_general | solution.py:79
  211.0 6.4 %bitcast_add_fusion.4 = f32[256,8,4,128]{0,3,2,1:T(8,128)} fusion(f32[256,8,4,128]{0,3,2,1:T(8,128)} %get-tuple-element.666, bf16[8,4,256,256]{2,3,1,0:T(8,128)(2,1)} %copy-done.2, pred[]{:T(512)S(6)} %compare.37, bf16[4,256,8,128]{3,1,2,0:T(8,128)(2,1)} %get-tuple-element.686, s32[]{:T(128)} %get-tuple-element.665), kind=kOutput, calls=%fused_computation.41.clone.1 | convolution fusion | flops 538968064 | bytes 13107713 | tf_op jit(solution)/shard_map/while/body/eval_jaxpr/hgqk,khd->qhgd/dot_general | solution.py:79
  230.3 27.3 %reduce-scatter.5.cloned.1.call-done = f32[1,256,8,128]{3,2,1,0:T(8,128)} async-done(((f32[4,256,8,128]{3,2,1,0:T(8,128)}), f32[1,256,8,128]{3,2,1,0:T(8,128)}) %reduce-scatter.5.cloned.1.call-update) | async-done | bytes 1048592 | tf_op jit(solution)/shard_map/reduce_scatter | solution.py:87
  259.8 40.4 %reduce-scatter.3.cloned.1.call-done = f32[1,256,8,128]{3,2,1,0:T(8,128)} async-done(((f32[4,256,8,128]{3,2,1,0:T(8,128)}), f32[1,256,8,128]{3,2,1,0:T(8,128)}) %reduce-scatter.3.cloned.1.call-update) | async-done | bytes 1048592 | tf_op jit(solution)/shard_map/reduce_scatter | solution.py:86
  (135 shorter events, 98.1 us)
Async XLA Ops:
  7.2 8.3 %copy-start = (s32[3]{0:T(128)S(1)}, s32[3]{0:T(128)}, u32[]{:S(2)}) copy-start(s32[3]{0:T(128)} %param.15) | copy-start | bytes 40
  7.2 30.1 %all-gather.7.cloned.1.call-start = ((), (), s32[]{:S(2)}) async-start(), calls=%async_computation.4 | async-start | bytes 2621440 | tf_op jit(solution)/shard_map/all_gather | solution.py:39
  7.9 47.0 %all-gather.9.cloned.1.call-start = ((), (), s32[]{:S(2)}) async-start(), calls=%async_computation.5 | async-start | bytes 2621440 | tf_op jit(solution)/shard_map/all_gather | solution.py:40
  8.7 249.0 %reduce-scatter.5.cloned.1.call-start = ((), (), s32[]{:S(2)}) async-start(), calls=%async_computation.3 | async-start | bytes 5242880 | tf_op jit(solution)/shard_map/reduce_scatter | solution.py:87
  15.4 9.0 %copy-start.5 = (s32[256]{0:T(256)S(1)}, s32[256]{0:T(256)}, u32[]{:S(2)}) copy-start(s32[256]{0:T(256)} %param.14) | copy-start | bytes 3076
  64.1 5.8 %copy-start.1 = (f32[8,256,256,4]{2,1,3,0:T(8,128)S(1)}, f32[8,256,256,4]{2,1,3,0:T(8,128)}, u32[]{:S(2)}) copy-start(f32[8,256,256,4]{2,1,3,0:T(8,128)} %get-tuple-element.586) | copy-start | bytes 25165828 | tf_op jit(solution)/shard_map/while
  81.8 5.8 %copy-start.1 = (f32[8,256,256,4]{2,1,3,0:T(8,128)S(1)}, f32[8,256,256,4]{2,1,3,0:T(8,128)}, u32[]{:S(2)}) copy-start(f32[8,256,256,4]{2,1,3,0:T(8,128)} %get-tuple-element.586) | copy-start | bytes 25165828 | tf_op jit(solution)/shard_map/while
  100.4 5.8 %copy-start.1 = (f32[8,256,256,4]{2,1,3,0:T(8,128)S(1)}, f32[8,256,256,4]{2,1,3,0:T(8,128)}, u32[]{:S(2)}) copy-start(f32[8,256,256,4]{2,1,3,0:T(8,128)} %get-tuple-element.586) | copy-start | bytes 25165828 | tf_op jit(solution)/shard_map/while
  119.0 5.8 %copy-start.1 = (f32[8,256,256,4]{2,1,3,0:T(8,128)S(1)}, f32[8,256,256,4]{2,1,3,0:T(8,128)}, u32[]{:S(2)}) copy-start(f32[8,256,256,4]{2,1,3,0:T(8,128)} %get-tuple-element.586) | copy-start | bytes 25165828 | tf_op jit(solution)/shard_map/while
  140.3 2.5 copy-start.3
  146.6 1.9 copy-start.2
  158.7 2.5 copy-start.3
  165.0 1.9 copy-start.2
  178.4 2.5 copy-start.3
  184.7 1.9 copy-start.2
  198.0 2.5 copy-start.3
  204.3 1.9 copy-start.2
  217.5 82.7 %reduce-scatter.3.cloned.1.call-start = ((), (), s32[]{:S(2)}) async-start(), calls=%async_computation.2 | async-start | bytes 5242880 | tf_op jit(solution)/shard_map/reduce_scatter | solution.py:86
  218.1 8.7 %copy-start.4 = (bf16[8,4,256,128]{3,2,1,0:T(8,128)(2,1)S(1)}, bf16[8,4,256,128]{3,2,1,0:T(8,128)(2,1)}, u32[]{:S(2)}) copy-start(bf16[8,4,256,128]{3,2,1,0:T(8,128)(2,1)} %get-tuple-element.406) | copy-start | bytes 6291460
Sparse Core Ops, SparseCore 0:
  9.5 23.2 all-gather.6
  34.4 20.4 all-gather.8
  217.6 40.0 reduce-scatter.4
  260.1 40.0 reduce-scatter.2
where the time goes:
time: 310 us; the launch traced here: 309 us
  matrix products  112 us (36%)
  waiting for transfers between devices  83.9 us (27%)
  local copies, waits for them, and re-layouts  51.9 us (17%)
  other arithmetic  39.6 us (13%)
  between operations  13.9 us (4%)
  blocking collectives  6.31 us (2%)
    reduce_scatter x1, waiting for transfers between devices, local_attention(): lax.psum_scatter(kv_parts[0], 'cp', scatter_dimension=0, tiled=False)  40.4 us
    dot_general x8, matrix products, block_scores(): jnp.einsum('qhgd,khd->hgqk', q_grouped, k_blk, preferred_element_type=jnp...  32.2 us
    reduce_scatter x1, waiting for transfers between devices, local_attention(): lax.psum_scatter(kv_parts[1], 'cp', scatter_dimension=0, tiled=False)  27.3 us
    dot_general x4, matrix products, fwd_step(): jnp.einsum('hgqk,khd->hgqd', weights.astype(jnp.bfloat16), v_blk, preferr...  26.8 us
    dot_general x4, matrix products, bwd_step(): jnp.einsum('hgqk,khd->qhgd', d_score, k_blk, preferred_element_type=jnp.f...  24.3 us
    reduce_sum x4, other arithmetic, fwd_step(): l_new = rescale * l_run + jnp.sum(weights, axis=-1)  18.7 us
    dot_general x4, matrix products, bwd_step(): jnp.einsum('qhgd,khd->hgqk', do_grouped, v_blk, preferred_element_type=jn...  15.3 us
    all_gather x1, waiting for transfers between devices, local_attention(): v_all = lax.all_gather(v_loc, 'cp')  14.2 us
  transfers between devices with their start and end apart: 4, of which 3 were waited for; matrix products, arithmetic and copies ran while one was open for 13% of the time, Pallas kernels for 0%

commit v1 on v0

v1 whole, which is shorter than its diff:
```python
import functools
import math

import jax
import jax.numpy as jnp
from jax import lax
from jax.experimental import pallas as pl
from jax.experimental.pallas import tpu as pltpu
from jax.sharding import PartitionSpec as P

MESH = pl.DeviceIdType.MESH
FILL = -1.0e30
BIG = 3.0e38
HEAD = 128
SLOT = 128
TILE = 512
GROUP = 4
HC = 4
SCALE = HEAD ** -0.5
C2 = SCALE * math.log2(math.e)
NT = (((1,), (1,)), ((), ()))
NN = (((1,), (0,)), ((), ()))
F32 = jnp.float32
BF16 = jnp.bfloat16

TILES = ((0, 0), (1, 0), (1, 1), (0, 1))


def slot_of(chip, ti):
    oc, up = TILES[ti]
    r = 2 * chip + oc
    return 7 - r if up else r


def mm(a, b, dims):
    return lax.dot_general(a, b, dims, preferred_element_type=F32)


def src_row(up, t, l0):
    if up:
        return jnp.where(t < l0, t + l0, t + SLOT)
    return jnp.where(t < l0, t, t + l0)


def attn_kernel(cu, valid, q, k, v, do, o_out, dq_out, dkv_out, lse_out,
                raw_q, raw_do, far_q, far_do, raw_k, raw_v, kv_hm, kv_all, kt, vt, qh, doh, st, pb, db,
                dkv_acc, dkv_in, o_st, dq_st, dkv_st, lse_st, caps, valid_all,
                in_sem, raw_ssem, raw_rsem, val_ssem, val_rsem, kv_ssem, kv_rsem,
                part_ssem, part_rsem, out_sem, out_rsem, lse_sem, lse_rsem):
    r = lax.axis_index("cp")
    chip = r // 2
    c = r % 2
    pc = 1 - c
    partner = chip * 2 + pc
    cross = (1 - chip) * 2 + c
    cross_o = (1 - chip) * 2 + pc
    l0 = lax.shift_right_logical(cu[1], 3)

    def remote(src, dst, ssem, rsem, dev):
        return pltpu.make_async_remote_copy(src_ref=src, dst_ref=dst, send_sem=ssem, recv_sem=rsem,
                                            device_id={"cp": dev}, device_id_type=MESH)

    own_heads = pl.ds(pl.multiple_of(16 * c, 16), 16)
    oth_heads = pl.ds(pl.multiple_of(16 * pc, 16), 16)
    ld_k = pltpu.make_async_copy(k, raw_k, in_sem.at[0])
    ld_v = pltpu.make_async_copy(v, raw_v, in_sem.at[1])
    ld_q = pltpu.make_async_copy(q.at[:, own_heads, :], raw_q, in_sem.at[2])
    ld_do = pltpu.make_async_copy(do.at[:, own_heads, :], raw_do, in_sem.at[3])
    ld_val = pltpu.make_async_copy(valid, valid_all.at[r], in_sem.at[4])
    for cp in (ld_k, ld_v, ld_q, ld_do, ld_val):
        cp.start()

    barrier = pltpu.get_barrier_semaphore()
    for dev in (partner, cross, cross_o):
        pl.semaphore_signal(barrier, inc=1, device_id={"cp": dev}, device_id_type=MESH)
    pl.semaphore_wait(barrier, 3)

    peers = (partner, cross, cross_o)
    push_q = remote(q.at[:, oth_heads, :], far_q, raw_ssem.at[0], raw_rsem.at[0], partner)
    push_do = remote(do.at[:, oth_heads, :], far_do, raw_ssem.at[1], raw_rsem.at[1], partner)
    push_val = [remote(valid, valid_all.at[r], val_ssem.at[i], val_rsem.at[r], dev) for i, dev in enumerate(peers)]

    def kv_relayout(up):
        def body(i, _):
            t0 = i * 16
            for which, raw in ((0, raw_k), (1, raw_v)):
                rows = jnp.stack([raw[src_row(up, t0 + j, l0)] for j in range(16)])
                kv_hm[:, up, which, pl.ds(pl.multiple_of(t0, 16), 16), :] = jnp.transpose(rows, (1, 0, 2))
            return 0
        lax.fori_loop(0, SLOT // 16, body, 0)

    my_slot = (r, 7 - r)

    def kv_push(h, up, to):
        head = (4 * c if to == 1 else 4 * pc) + h
        dev = (partner, cross, cross_o)[to]
        return remote(kv_hm.at[head, up], kv_all.at[h, my_slot[up]], kv_ssem.at[to, h, up],
                      kv_rsem.at[h, my_slot[up]], dev)

    ld_k.wait()
    ld_v.wait()
    kv_relayout(0)
    for h in range(HC):
        kv_push(h, 0, 1).start()
        kv_push(h, 0, 2).start()
    kv_relayout(1)

    @pl.when(chip == 1)
    def _():
        for h in range(HC):
            kv_push(h, 1, 1).start()
            kv_push(h, 1, 2).start()

    for h in range(HC):
        kv_push(h, 0, 0).start()
        kv_push(h, 1, 0).start()
    push_q.start()
    push_do.start()
    ld_val.wait()
    for cp in push_val:
        cp.start()

    def copy_own(h, _):
        for up in range(2):
            kv_all[h, my_slot[up]] = kv_hm[4 * c + h, up]
        return 0
    lax.fori_loop(0, HC, copy_own, 0)

    def q_relayout(oc, from_q, from_do):
        for up, ti in ((0, oc), (1, 3 - oc)):
            def body(i, _):
                t0 = i * 16
                at = pl.ds(pl.multiple_of(t0, 16), 16)
                for raw, dst in ((from_q, qh), (from_do, doh)):
                    rows = jnp.stack([raw[src_row(up, t0 + j, l0)] for j in range(16)])
                    dst[:, ti, :, at, :] = jnp.transpose(rows, (1, 0, 2)).reshape(HC, GROUP, 16, HEAD)
                return 0
            lax.fori_loop(0, SLOT // 16, body, 0)

    ld_q.wait()
    ld_do.wait()
    q_relayout(c, raw_q, raw_do)

    for i in range(3):
        remote(valid, valid_all.at[peers[i]], val_ssem.at[i], val_rsem.at[peers[i]], peers[i]).wait_recv()
    lane = lax.broadcasted_iota(jnp.int32, (SLOT, SLOT), 1)
    sub = lax.broadcasted_iota(jnp.int32, (SLOT, SLOT), 0)
    lane2 = lax.broadcasted_iota(jnp.int32, (SLOT, 2 * SLOT), 1)
    sub2 = lax.broadcasted_iota(jnp.int32, (SLOT, 2 * SLOT), 0)
    same_doc = (lane < l0) == (sub < l0)
    doc_f = jnp.where(lane < l0, 1.0, 0.0)
    doc_s = jnp.where(sub < l0, 1.0, 0.0)
    same_f = jnp.where(doc_f == doc_s, 1.0, 0.0)
    del same_doc

    def cap_body(s, _):
        owner = jnp.where(s < 4, s, 7 - s)
        off = jnp.where(s < 4, 0, 1)
        src_lo = jnp.where(sub2 < l0, sub2, sub2 + l0)
        src_hi = jnp.where(sub2 < l0, sub2 + l0, sub2 + SLOT)
        src = jnp.where(off == 1, src_hi, src_lo)
        row = jnp.broadcast_to(valid_all[owner].astype(F32), (SLOT, 2 * SLOT))
        ok = jnp.sum(jnp.where(src == lane2, row, 0.0), axis=1, keepdims=True)
        caps[s] = jnp.where(same_f * ok > 0.5, BIG, FILL)
        return 0
    lax.fori_loop(0, 8, cap_body, 0)
    for ti in range(4):
        oc, up = TILES[ti]
        s = (7 - (2 * chip + oc)) if up else 2 * chip + oc
        caps[8 + ti] = jnp.where(sub <= lane, caps[s], FILL)

    push_q.wait_recv()
    push_do.wait_recv()
    q_relayout(pc, far_q, far_do)

    def part_copy(h, i, slot):
        return remote(dkv_acc.at[h, slot], dkv_in.at[h, i], part_ssem.at[h, i], part_rsem.at[h, i], cross)

    def out_copies(h, ti, which):
        stage, out = ((o_st, o_out), (dq_st, dq_out), (dkv_st, dkv_out))[which]
        oc, up = TILES[ti]
        dst = out.at[4 * c + h, up]
        src = stage.at[h, ti]
        return (pltpu.make_async_copy(src, dst, out_sem.at[which, h, ti]),
                remote(src, dst, out_sem.at[which, h, ti], out_rsem.at[which, h, up], partner))

    def out_start(h, ti, which):
        local, far = out_copies(h, ti, which)
        oc = TILES[ti][0]

        @pl.when(c == oc)
        def _():
            local.start()

        @pl.when(c != oc)
        def _():
            far.start()

    lse_local = pltpu.make_async_copy(lse_st.at[c], lse_out.at[:, own_heads, :], lse_sem.at[0])
    lse_far = remote(lse_st.at[pc], lse_out.at[:, own_heads, :], lse_sem.at[1], lse_rsem, partner)

    def run_chip(ch):
        slots = [slot_of(ch, ti) for ti in range(4)]
        sent = [0, 1] if ch == 1 else [2, 3, 4, 5]
        kept = [0, 1] if ch == 0 else [2, 3, 4, 5]
        order = [0, 1, 2, 3]

        def transposes(s):
            for src, dst in ((0, kt), (1, vt)):
                dst[:, s * SLOT:(s + 1) * SLOT] = jnp.transpose(kv_all[h_ref[0], s, src])

        h_ref = [None]

        def head(h, _):
            h_ref[0] = h
            seen = set()
            ready = set()

            def wait_slot(s):
                if s in ready:
                    return
                ready.add(s)
                if s in slots:
                    @pl.when(jnp.logical_and(r != s, 7 - r != s))
                    def _():
                        remote(kv_hm.at[0, 0], kv_all.at[h, s], kv_ssem.at[0, h, 0], kv_rsem.at[h, s], partner).wait_recv()
                else:
                    remote(kv_hm.at[0, 0], kv_all.at[h, s], kv_ssem.at[0, h, 0], kv_rsem.at[h, s], partner).wait_recv()
                transposes(s)

            for ti in order:
                s = slots[ti]
                nk = s + 1
                for u in range(nk):
                    wait_slot(u)
                qt = qh[h, ti].reshape(TILE, HEAD)
                dt = doh[h, ti].reshape(TILE, HEAD)
                m8 = [None] * GROUP
                for a in range(0, nk, 2):
                    n = min(2, nk - a)
                    kb = kv_all[h, a:a + n, 0].reshape(n * SLOT, HEAD)
                    sc = mm(kb, qt, NT)
                    for j in range(n):
                        cap = caps[8 + ti] if a + j == s else caps[a + j]
                        for g in range(GROUP):
                            x = jnp.minimum(sc[j * SLOT:(j + 1) * SLOT, g * SLOT:(g + 1) * SLOT], cap)
                            st[(a + j) * SLOT:(a + j + 1) * SLOT, g * SLOT:(g + 1) * SLOT] = x
                            top = jnp.max(x.reshape(SLOT // 8, 8, SLOT), axis=0)
                            m8[g] = top if m8[g] is None else jnp.maximum(m8[g], top)
                m = [jnp.max(x, axis=0, keepdims=True) for x in m8]
                mc = [x * C2 for x in m]
                l8 = [None] * GROUP
                for a in range(nk):
                    for g in range(GROUP):
                        at = (slice(a * SLOT, (a + 1) * SLOT), slice(g * SLOT, (g + 1) * SLOT))
                        e = jnp.exp2(st[at] * C2 - mc[g])
                        st[at] = e
                        pb[at] = e.astype(BF16)
                        tot = jnp.sum(e.reshape(SLOT // 8, 8, SLOT), axis=0)
                        l8[g] = tot if l8[g] is None else l8[g] + tot
                ot = mm(vt[:, :nk * SLOT], pb[:nk * SLOT, :], NN)
                inv, dd = [], []
                oc, up = TILES[ti]
                for g in range(GROUP):
                    l = jnp.sum(l8[g], axis=0, keepdims=True)
                    has = m[g] > 0.5 * FILL
                    safe = jnp.where(has, l, 1.0)
                    i_l = jnp.where(has, 1.0 / safe, 0.0)
                    lse = jnp.where(has, m[g] * SCALE + jnp.log(safe), 0.0)
                    lse_st[oc, up, pl.ds(h * GROUP + g, 1), :] = lse
                    og = (ot[:, g * SLOT:(g + 1) * SLOT] * i_l).astype(BF16)
                    dog = jnp.transpose(dt[g * SLOT:(g + 1) * SLOT, :])
                    dd.append(jnp.sum(og.astype(F32) * dog.astype(F32), axis=0, keepdims=True))
                    inv.append(i_l)
                    o_st[h, ti, g * SLOT:(g + 1) * SLOT, :] = jnp.transpose(og)
                out_start(h, ti, 0)

                first = [u for u in range(nk) if u in sent] if (ch == 0 and ti >= 2) else []
                rest = [u for u in range(nk) if u not in first]
                dqt = None
                for part in (first, rest):
                    runs = []
                    for u in part:
                        if runs and runs[-1][1] == u and u - runs[-1][0] < 2:
                            runs[-1][1] = u + 1
                        else:
                            runs.append([u, u + 1])
                    for a, b in runs:
                        n = b - a
                        vb = kv_all[h, a:b, 1].reshape(n * SLOT, HEAD)
                        dp = mm(vb, dt, NT)
                        for j in range(n):
                            for g in range(GROUP):
                                at = (slice((a + j) * SLOT, (a + j + 1) * SLOT), slice(g * SLOT, (g + 1) * SLOT))
                                p = st[at] * inv[g]
                                pb[at] = p.astype(BF16)
                                ds = p * (dp[j * SLOT:(j + 1) * SLOT, g * SLOT:(g + 1) * SLOT] - dd[g])
                                db[at] = ds.astype(BF16)
                        dsb = db[a * SLOT:b * SLOT, :]
                        dv = mm(pb[a * SLOT:b * SLOT, :], dt, NN)
                        dk = mm(dsb, qt, NN) * SCALE
                        dq = mm(kt[:, a * SLOT:b * SLOT], dsb, NN)
                        dqt = dq if dqt is None else dqt + dq
                        for j in range(n):
                            u = a + j
                            new = (dk[j * SLOT:(j + 1) * SLOT], dv[j * SLOT:(j + 1) * SLOT])
                            for w in range(2):
                                dkv_acc[h, u, w] = dkv_acc[h, u, w] + new[w] if u in seen else new[w]
                            seen.add(u)
                    if part is first and ti == 3 and ch == 0:
                        for i, u in enumerate(sent):
                            part_copy(h, i, u).start()
                for g in range(GROUP):
                    dqg = (dqt[:, g * SLOT:(g + 1) * SLOT] * SCALE).astype(BF16)
                    dq_st[h, ti, g * SLOT:(g + 1) * SLOT, :] = jnp.transpose(dqg)
                out_start(h, ti, 1)
            if ch == 1:
                for i, u in enumerate(sent):
                    part_copy(h, i, u).start()
            else:
                for ti in (2, 3):
                    for w in range(2):
                        dkv_st[h, ti, w] = dkv_acc[h, slots[ti], w].astype(BF16)
                    out_start(h, ti, 2)
            return 0

        lax.fori_loop(0, HC, head, 0)

        lse_local.start()
        lse_far.start()

        def tail(h, _):
            for i, u in enumerate(kept):
                ti = slots.index(u)
                part_copy(h, i, u).wait_recv()
                for w in range(2):
                    dkv_st[h, ti, w] = (dkv_acc[h, u, w] + dkv_in[h, i, w]).astype(BF16)
                out_start(h, ti, 2)
            return 0
        lax.fori_loop(0, HC, tail, 0)

        def drain(h, _):
            for i, u in enumerate(sent):
                part_copy(h, i, u).wait_send()
            return 0
        lax.fori_loop(0, HC, drain, 0)

    pl.when(chip == 0)(functools.partial(run_chip, 0))
    pl.when(chip == 1)(functools.partial(run_chip, 1))

    push_q.wait_send()
    push_do.wait_send()
    for cp in push_val:
        cp.wait_send()

    def drain(h, _):
        for up in range(2):
            kv_push(h, up, 0).wait_send()
        for to in (1, 2):
            kv_push(h, 0, to).wait_send()

        @pl.when(chip == 1)
        def _():
            for to in (1, 2):
                kv_push(h, 1, to).wait_send()
        for which in range(3):
            for ti in range(4):
                local, far = out_copies(h, ti, which)
                oc = TILES[ti][0]

                @pl.when(c == oc)
                def _():
                    local.wait()

                @pl.when(c != oc)
                def _():
                    far.wait_send()
            for up in range(2):
                stage, out = ((o_st, o_out), (dq_st, dq_out), (dkv_st, dkv_out))[which]
                remote(stage.at[h, 0], out.at[4 * pc + h, up], out_sem.at[which, h, 0],
                       out_rsem.at[which, h, up], partner).wait_recv()
        return 0
    lax.fori_loop(0, HC, drain, 0)
    lse_local.wait()
    lse_far.wait_send()
    remote(lse_st.at[0], lse_out.at[:, oth_heads, :], lse_sem.at[1], lse_rsem, partner).wait_recv()


def attn_call(cu, valid, q, k, v, do):
    any_spec = pl.BlockSpec(memory_space=pl.ANY)
    dma = pltpu.SemaphoreType.DMA
    return pl.pallas_call(
        attn_kernel,
        out_shape=(
            jax.ShapeDtypeStruct((8, 2, GROUP * SLOT, HEAD), BF16),
            jax.ShapeDtypeStruct((8, 2, GROUP * SLOT, HEAD), BF16),
            jax.ShapeDtypeStruct((8, 2, 2, SLOT, HEAD), BF16),
            jax.ShapeDtypeStruct((2, 32, SLOT), F32),
        ),
        in_specs=[pl.BlockSpec(memory_space=pltpu.SMEM)] + [any_spec] * 5,
        out_specs=(any_spec,) * 4,
        scratch_shapes=[
            pltpu.VMEM((256, 16, HEAD), BF16),
            pltpu.VMEM((256, 16, HEAD), BF16),
            pltpu.VMEM((256, 16, HEAD), BF16),
            pltpu.VMEM((256, 16, HEAD), BF16),
            pltpu.VMEM((256, 8, HEAD), BF16),
            pltpu.VMEM((256, 8, HEAD), BF16),
            pltpu.VMEM((8, 2, 2, SLOT, HEAD), BF16),
            pltpu.VMEM((HC, 8, 2, SLOT, HEAD), BF16),
            pltpu.VMEM((HEAD, 8 * SLOT), BF16),
            pltpu.VMEM((HEAD, 8 * SLOT), BF16),
            pltpu.VMEM((HC, 4, GROUP, SLOT, HEAD), BF16),
            pltpu.VMEM((HC, 4, GROUP, SLOT, HEAD), BF16),
            pltpu.VMEM((8 * SLOT, TILE), F32),
            pltpu.VMEM((8 * SLOT, TILE), BF16),
            pltpu.VMEM((8 * SLOT, TILE), BF16),
            pltpu.VMEM((HC, 8, 2, SLOT, HEAD), F32),
            pltpu.VMEM((HC, 4, 2, SLOT, HEAD), F32),
            pltpu.VMEM((HC, 4, TILE, HEAD), BF16),
            pltpu.VMEM((HC, 4, TILE, HEAD), BF16),
            pltpu.VMEM((HC, 4, 2, SLOT, HEAD), BF16),
            pltpu.VMEM((2, 2, 16, SLOT), F32),
            pltpu.VMEM((12, SLOT, SLOT), F32),
            pltpu.VMEM((4, 1, 2 * SLOT), jnp.int32),
            dma((5,)),
            dma((2,)), dma((2,)),
            dma((3,)), dma((4,)),
            dma((3, HC, 2)), dma((HC, 8)),
            dma((HC, 4)), dma((HC, 4)),
            dma((3, HC, 4)), dma((3, HC, 2)),
            dma((2,)), dma,
        ],
        compiler_params=pltpu.CompilerParams(collective_id=0, has_side_effects=True, vmem_limit_bytes=60 * 1024 * 1024),
        name="attn",
    )(cu, valid, q, k, v, do)


def finish_kernel(cu, o_in, dq_in, dkv_in, lse_in, o_out, dq_out, dk_out, dv_out, lse_out):
    l0 = lax.shift_right_logical(cu[1], 3)

    def put(get, out):
        for up in range(2):
            def body(i, _):
                t0 = i * 16
                x = get(up, pl.ds(pl.multiple_of(t0, 16), 16))
                y = jnp.transpose(x, (1, 0, 2))
                for j in range(16):
                    out[src_row(up, t0 + j, l0)] = y[j]
                return 0
            lax.fori_loop(0, SLOT // 16, body, 0)

    put(lambda up, at: o_in[:, up, :, at, :].reshape(8, 16, HEAD), o_out)
    put(lambda up, at: dq_in[:, up, :, at, :].reshape(8, 16, HEAD), dq_out)

    @pl.when(pl.program_id(0) == 0)
    def _():
        put(lambda up, at: dkv_in[:, up, 0, at, :], dk_out)
        put(lambda up, at: dkv_in[:, up, 1, at, :], dv_out)
        row = lax.broadcasted_iota(jnp.int32, (2 * SLOT, SLOT), 0)
        col = lax.broadcasted_iota(jnp.int32, (2 * SLOT, SLOT), 1)
        acc = None
        for up in range(2):
            if up:
                src = jnp.where(col < l0, col + l0, col + SLOT)
            else:
                src = jnp.where(col < l0, col, col + l0)
            pick = jnp.where(row == src, 1.0, 0.0)
            part = lax.dot_general(pick, lse_in[up], NT, precision=lax.Precision.HIGHEST, preferred_element_type=F32)
            acc = part if acc is None else acc + part
        lse_out[...] = acc


def finish_call(cu, o_hm, dq_hm, dkv_hm, lse_hm):
    return pl.pallas_call(
        finish_kernel,
        grid=(4,),
        out_shape=(
            jax.ShapeDtypeStruct((256, 32, HEAD), BF16),
            jax.ShapeDtypeStruct((256, 32, HEAD), BF16),
            jax.ShapeDtypeStruct((256, 8, HEAD), BF16),
            jax.ShapeDtypeStruct((256, 8, HEAD), BF16),
            jax.ShapeDtypeStruct((256, 32), F32),
        ),
        in_specs=[
            pl.BlockSpec(memory_space=pltpu.SMEM),
            pl.BlockSpec((2, 2, GROUP, SLOT, HEAD), lambda i: (i, 0, 0, 0, 0)),
            pl.BlockSpec((2, 2, GROUP, SLOT, HEAD), lambda i: (i, 0, 0, 0, 0)),
            pl.BlockSpec((8, 2, 2, SLOT, HEAD), lambda i: (0, 0, 0, 0, 0)),
            pl.BlockSpec((2, 32, SLOT), lambda i: (0, 0, 0)),
        ],
        out_specs=(
            pl.BlockSpec((256, 8, HEAD), lambda i: (0, i, 0)),
            pl.BlockSpec((256, 8, HEAD), lambda i: (0, i, 0)),
            pl.BlockSpec((256, 8, HEAD), lambda i: (0, 0, 0)),
            pl.BlockSpec((256, 8, HEAD), lambda i: (0, 0, 0)),
            pl.BlockSpec((256, 32), lambda i: (0, 0)),
        ),
        compiler_params=pltpu.CompilerParams(dimension_semantics=("arbitrary",), vmem_limit_bytes=40 * 1024 * 1024),
        name="finish",
    )(cu, o_hm.reshape(8, 2, GROUP, SLOT, HEAD), dq_hm.reshape(8, 2, GROUP, SLOT, HEAD), dkv_hm, lse_hm)


def solution(mesh):
    tok_spec = P(("dp", "cp"), None, None)
    lse_spec = P(("dp", "cp"), None)

    def local(q, k, v, do, valid, cu):
        o_hm, dq_hm, dkv_hm, lse_hm = attn_call(cu, valid.reshape(1, 256), q, k, v, do)
        o, dq, dk, dv, lse = finish_call(cu, o_hm, dq_hm, dkv_hm, lse_hm)
        return o, lse, dq, dk, dv

    return jax.shard_map(local, mesh=mesh, in_specs=(tok_spec,) * 4 + (P(("dp", "cp")), P("dp")),
                         out_specs=(tok_spec, lse_spec, tok_spec, tok_spec, tok_spec), check_vma=False)
```

time: 310 us -> 99.1 us (0.32)
  matrix products: 112 us -> 0 us
  Pallas kernels: 0 us -> 92.3 us
  waiting for transfers between devices: 83.9 us -> 0 us
  local copies, waits for them, and re-layouts: 51.9 us -> 5.85 us
  other arithmetic: 39.6 us -> 0 us
  between operations: 13.9 us -> 0.67 us
  blocking collectives: 6.31 us -> 0 us
    dot_general x28 -> x0, matrix products: 112 us -> none  [the longest x8 32.2 us: block_scores(): jnp.einsum('qhgd,khd->hgqk', q_grouped, k_blk, preferred_element_type=jnp...]
    pallas_call x0 -> x2, Pallas kernels: none -> 92.3 us  [the longest x1 84.6 us: attn_call(): pl.pallas_call(attn_kernel, out_shape=(jax.ShapeDtypeStruct((8, 2, GROUP...]
    reduce_scatter x2 -> x0, waiting for transfers between devices: 67.8 us -> none  [the longest x1 40.4 us: local_attention(): lax.psum_scatter(kv_parts[0], 'cp', scatter_dimension=0, tiled=False)]
    reduce_sum x6 -> x0, other arithmetic: 18.9 us -> none  [the longest x4 18.7 us: fwd_step(): l_new = rescale * l_run + jnp.sum(weights, axis=-1)]
    all_gather x2 -> x0, waiting for transfers between devices: 14.2 us -> none  [the longest x1 14.2 us: local_attention(): v_all = lax.all_gather(v_loc, 'cp')]
    gather x5 -> x0, local copies, waits for them, and re-layouts: 13 us -> none  [the longest x2 6.58 us: token_coords(): piece_len = (cu_seqlens[doc_id + 1] - seg_start) // (2 * cp_size)]
    dynamic_update_slice x4 -> x0, local copies, waits for them, and re-layouts: 10.4 us -> none  [local_attention(): dq_fin, kv_parts = lax.scan(bwd_step, dq_init, key_xs)]
    convert_element_type x3 -> x0, other arithmetic: 8.39 us -> none  [the longest x1 4.22 us: local_attention(): (dq_fin * score_scale).astype(jnp.bfloat16)]
  transfers between devices with their start and end apart: 4 -> 0, of which waited for: 3 -> 0; matrix products, arithmetic and copies ran while one was open for 13% -> 0% of each run, Pallas kernels for 0% -> 0%
where the time goes in v1:
time: 99.1 us; the launch traced here: 98.8 us
  Pallas kernels  92.3 us (93%)
  local copies, waits for them, and re-layouts  5.85 us (6%)
    pallas_call x1, Pallas kernels, attn_call(): pl.pallas_call(attn_kernel, out_shape=(jax.ShapeDtypeStruct((8, 2, GROUP...  84.6 us
    pallas_call x1, Pallas kernels, finish_call(): pl.pallas_call(finish_kernel, grid=(4,), out_shape=(jax.ShapeDtypeStruct(...  7.66 us
    unnamed x11, local copies, waits for them, and re-layouts  5.85 us

profile of v1, /device:TPU:0, one launch (start us, length us, event | category | flops | bytes accessed | tf_op | source)
XLA Modules:
  0.0 98.8 jit_solution(3862104851881539252)
XLA Ops:
  0.6 0.0 copy-start.4
  0.6 84.6 %attn.1 = (bf16[8,2,512,128]{3,2,1,0:T(8,128)(2,1)}, bf16[8,2,512,128]{3,2,1,0:T(8,128)(2,1)}, bf16[8,2,2,128,128]{4,3,2,1,0:T(8,128)(2,1)}, f32[2,32,128]{2,1,0:T(8,128)}) custom-call(s32[3]{0:T(128)} %cu.3, s32[1,256]{1,0:T(1,128)} %bitcast.5, bf16[256,32,128]{2,1,0:T(8,128)(2,1)} %q.1, bf16[256,8,128]{2,1,0:T(8,128)(2,1)} %k.1, bf16[256,8,128]{2,1,0:T(8,128)(2,1)} %v.1, ...), custom_call_target="tpu_custom_call" | custom-call | tf_op jit(solution)/shard_map/attn/pallas_call | solution.py:392
  85.3 0.0 copy-done.4
  85.3 0.0 copy-start
  85.3 1.6 %copy-done = bf16[8,2,512,128]{3,2,1,0:T(8,128)(2,1)S(1)} copy-done((bf16[8,2,512,128]{3,2,1,0:T(8,128)(2,1)S(1)}, bf16[8,2,512,128]{3,2,1,0:T(8,128)(2,1)}, u32[]{:S(2)}) %copy-start) | copy-done | bytes 2097176
  86.9 0.0 copy-start.1
  86.9 1.6 %copy-done.1 = bf16[8,2,512,128]{3,2,1,0:T(8,128)(2,1)S(1)} copy-done((bf16[8,2,512,128]{3,2,1,0:T(8,128)(2,1)S(1)}, bf16[8,2,512,128]{3,2,1,0:T(8,128)(2,1)}, u32[]{:S(2)}) %copy-start.1) | copy-done | bytes 2097176
  88.5 0.0 copy-start.2
  88.5 1.2 %copy-done.2 = bf16[8,2,2,128,128]{4,3,2,1,0:T(8,128)(2,1)S(1)} copy-done((bf16[8,2,2,128,128]{4,3,2,1,0:T(8,128)(2,1)S(1)}, bf16[8,2,2,128,128]{4,3,2,1,0:T(8,128)(2,1)}, u32[]{:S(2)}) %copy-start.2) | copy-done | bytes 1048600
  89.7 0.0 copy-start.3
  89.7 0.8 copy-done.3
  90.5 7.7 %finish.1 = (bf16[256,32,128]{2,1,0:T(8,128)(2,1)}, bf16[256,32,128]{2,1,0:T(8,128)(2,1)}, bf16[256,8,128]{2,1,0:T(8,128)(2,1)}, bf16[256,8,128]{2,1,0:T(8,128)(2,1)}, f32[256,32]{1,0:T(8,128)S(1)}) custom-call(s32[3]{0:T(128)S(1)} %copy-done.4, bf16[8,2,4,128,128]{4,3,2,1,0:T(8,128)(2,1)S(1)} %bitcast.3, bf16[8,2,4,128,128]{4,3,2,1,0:T(8,128)(2,1)S(1)} %bitcast.4, ...), custom_call_target="tpu_custom_call" | custom-call | tf_op jit(solution)/shard_map/finish/pallas_call | solution.py:475
  98.1 0.7 copy.11
Async XLA Ops:
  0.6 84.6 %copy-start.4 = (s32[3]{0:T(128)S(1)}, s32[3]{0:T(128)}, u32[]{:S(2)}) copy-start(s32[3]{0:T(128)} %cu.3) | copy-start | bytes 40
  85.3 1.6 %copy-start = (bf16[8,2,512,128]{3,2,1,0:T(8,128)(2,1)S(1)}, bf16[8,2,512,128]{3,2,1,0:T(8,128)(2,1)}, u32[]{:S(2)}) copy-start(bf16[8,2,512,128]{3,2,1,0:T(8,128)(2,1)} %get-tuple-element.14) | copy-start | bytes 6291460
  86.9 1.6 %copy-start.1 = (bf16[8,2,512,128]{3,2,1,0:T(8,128)(2,1)S(1)}, bf16[8,2,512,128]{3,2,1,0:T(8,128)(2,1)}, u32[]{:S(2)}) copy-start(bf16[8,2,512,128]{3,2,1,0:T(8,128)(2,1)} %get-tuple-element.15) | copy-start | bytes 6291460
  88.5 1.2 %copy-start.2 = (bf16[8,2,2,128,128]{4,3,2,1,0:T(8,128)(2,1)S(1)}, bf16[8,2,2,128,128]{4,3,2,1,0:T(8,128)(2,1)}, u32[]{:S(2)}) copy-start(bf16[8,2,2,128,128]{4,3,2,1,0:T(8,128)(2,1)} %get-tuple-element.16.dkv_in) | copy-start | bytes 3145732
  89.7 0.8 copy-start.3

commit v2 on v1

--- a/solution.py
+++ b/solution.py
@@ -89,31 +89,36 @@
             return 0
         lax.fori_loop(0, SLOT // 16, body, 0)
 
-    my_slot = (r, 7 - r)
-
-    def kv_push(h, up, to):
+    def kv_push(h, to, both):
         head = (4 * c if to == 1 else 4 * pc) + h
         dev = (partner, cross, cross_o)[to]
-        return remote(kv_hm.at[head, up], kv_all.at[h, my_slot[up]], kv_ssem.at[to, h, up],
-                      kv_rsem.at[h, my_slot[up]], dev)
+        ups = pl.ds(0, 2 if both else 1)
+        return remote(kv_hm.at[head, ups], kv_all.at[h, r, ups], kv_ssem.at[to, h], kv_rsem.at[h, r], dev)
+
+    def kv_wait(h, owner, both):
+        ups = pl.ds(0, 2 if both else 1)
+        remote(kv_hm.at[0, ups], kv_all.at[h, owner, ups], kv_ssem.at[0, h], kv_rsem.at[h, owner], partner).wait_recv()
 
     ld_k.wait()
     ld_v.wait()
     kv_relayout(0)
-    for h in range(HC):
-        kv_push(h, 0, 1).start()
-        kv_push(h, 0, 2).start()
+
+    @pl.when(chip == 0)
+    def _():
+        for h in range(HC):
+            kv_push(h, 1, False).start()
+            kv_push(h, 2, False).start()
+
     kv_relayout(1)
 
     @pl.when(chip == 1)
     def _():
         for h in range(HC):
-            kv_push(h, 1, 1).start()
-            kv_push(h, 1, 2).start()
+            kv_push(h, 1, True).start()
+            kv_push(h, 2, True).start()
 
     for h in range(HC):
-        kv_push(h, 0, 0).start()
-        kv_push(h, 1, 0).start()
+        kv_push(h, 0, True).start()
     push_q.start()
     push_do.start()
     ld_val.wait()
@@ -122,7 +127,7 @@
 
     def copy_own(h, _):
         for up in range(2):
-            kv_all[h, my_slot[up]] = kv_hm[4 * c + h, up]
+            kv_all[h, r, up] = kv_hm[4 * c + h, up]
         return 0
     lax.fori_loop(0, HC, copy_own, 0)
 
@@ -173,8 +178,8 @@
     push_do.wait_recv()
     q_relayout(pc, far_q, far_do)
 
-    def part_copy(h, i, slot):
-        return remote(dkv_acc.at[h, slot], dkv_in.at[h, i], part_ssem.at[h, i], part_rsem.at[h, i], cross)
+    def part_copy(h, i, n):
+        return remote(dkv_acc.at[h, pl.ds(i, n)], dkv_in.at[h, pl.ds(0, n)], part_ssem.at[h], part_rsem.at[h], cross)
 
     def out_copies(h, ti, which):
         stage, out = ((o_st, o_out), (dq_st, dq_out), (dkv_st, dkv_out))[which]
@@ -199,6 +204,12 @@
     lse_local = pltpu.make_async_copy(lse_st.at[c], lse_out.at[:, own_heads, :], lse_sem.at[0])
     lse_far = remote(lse_st.at[pc], lse_out.at[:, own_heads, :], lse_sem.at[1], lse_rsem, partner)
 
+    def kv_slot(h, s, which):
+        return kv_all[h, min(s, 7 - s), int(s > 3), which]
+
+    def kv_slots(h, a, b, which):
+        return jnp.concatenate([kv_slot(h, s, which) for s in range(a, b)], axis=0)
+
     def run_chip(ch):
         slots = [slot_of(ch, ti) for ti in range(4)]
         sent = [0, 1] if ch == 1 else [2, 3, 4, 5]
@@ -207,7 +218,7 @@
 
         def transposes(s):
             for src, dst in ((0, kt), (1, vt)):
-                dst[:, s * SLOT:(s + 1) * SLOT] = jnp.transpose(kv_all[h_ref[0], s, src])
+                dst[:, s * SLOT:(s + 1) * SLOT] = jnp.transpose(kv_slot(h_ref[0], s, src))
 
         h_ref = [None]
 
@@ -219,14 +230,20 @@
             def wait_slot(s):
                 if s in ready:
                     return
-                ready.add(s)
                 if s in slots:
-                    @pl.when(jnp.logical_and(r != s, 7 - r != s))
-                    def _():
-                        remote(kv_hm.at[0, 0], kv_all.at[h, s], kv_ssem.at[0, h, 0], kv_rsem.at[h, s], partner).wait_recv()
+                    kv_wait(h, partner, True)
+                    new = slots
+                elif ch == 1:
+                    for owner in (0, 1):
+                        kv_wait(h, owner, False)
+                    new = [0, 1]
                 else:
-                    remote(kv_hm.at[0, 0], kv_all.at[h, s], kv_ssem.at[0, h, 0], kv_rsem.at[h, s], partner).wait_recv()
-                transposes(s)
+                    for owner in (2, 3):
+                        kv_wait(h, owner, True)
+                    new = [2, 3, 4, 5]
+                for u in new:
+                    ready.add(u)
+                    transposes(u)
 
             for ti in order:
                 s = slots[ti]
@@ -238,7 +255,7 @@
                 m8 = [None] * GROUP
                 for a in range(0, nk, 2):
                     n = min(2, nk - a)
-                    kb = kv_all[h, a:a + n, 0].reshape(n * SLOT, HEAD)
+                    kb = kv_slots(h, a, a + n, 0)
                     sc = mm(kb, qt, NT)
                     for j in range(n):
                         cap = caps[8 + ti] if a + j == s else caps[a + j]
@@ -287,7 +304,7 @@
                             runs.append([u, u + 1])
                     for a, b in runs:
                         n = b - a
-                        vb = kv_all[h, a:b, 1].reshape(n * SLOT, HEAD)
+                        vb = kv_slots(h, a, b, 1)
                         dp = mm(vb, dt, NT)
                         for j in range(n):
                             for g in range(GROUP):
@@ -308,15 +325,13 @@
                                 dkv_acc[h, u, w] = dkv_acc[h, u, w] + new[w] if u in seen else new[w]
                             seen.add(u)
                     if part is first and ti == 3 and ch == 0:
-                        for i, u in enumerate(sent):
-                            part_copy(h, i, u).start()
+                        part_copy(h, sent[0], len(sent)).start()
                 for g in range(GROUP):
                     dqg = (dqt[:, g * SLOT:(g + 1) * SLOT] * SCALE).astype(BF16)
                     dq_st[h, ti, g * SLOT:(g + 1) * SLOT, :] = jnp.transpose(dqg)
                 out_start(h, ti, 1)
             if ch == 1:
-                for i, u in enumerate(sent):
-                    part_copy(h, i, u).start()
+                part_copy(h, sent[0], len(sent)).start()
             else:
                 for ti in (2, 3):
                     for w in range(2):
@@ -330,9 +345,9 @@
         lse_far.start()
 
         def tail(h, _):
+            part_copy(h, kept[0], len(kept)).wait_recv()
             for i, u in enumerate(kept):
                 ti = slots.index(u)
-                part_copy(h, i, u).wait_recv()
                 for w in range(2):
                     dkv_st[h, ti, w] = (dkv_acc[h, u, w] + dkv_in[h, i, w]).astype(BF16)
                 out_start(h, ti, 2)
@@ -340,8 +355,7 @@
         lax.fori_loop(0, HC, tail, 0)
 
         def drain(h, _):
-            for i, u in enumerate(sent):
-                part_copy(h, i, u).wait_send()
+            part_copy(h, sent[0], len(sent)).wait_send()
             return 0
         lax.fori_loop(0, HC, drain, 0)
 
@@ -354,15 +368,12 @@
         cp.wait_send()
 
     def drain(h, _):
-        for up in range(2):
-            kv_push(h, up, 0).wait_send()
-        for to in (1, 2):
-            kv_push(h, 0, to).wait_send()
-
-        @pl.when(chip == 1)
-        def _():
-            for to in (1, 2):
-                kv_push(h, 1, to).wait_send()
+        kv_push(h, 0, True).wait_send()
+        for ch in range(2):
+            @pl.when(chip == ch)
+            def _():
+                for to in (1, 2):
+                    kv_push(h, to, ch == 1).wait_send()
         for which in range(3):
             for ti in range(4):
                 local, far = out_copies(h, ti, which)
@@ -407,7 +418,7 @@
             pltpu.VMEM((256, 8, HEAD), BF16),
             pltpu.VMEM((256, 8, HEAD), BF16),
             pltpu.VMEM((8, 2, 2, SLOT, HEAD), BF16),
-            pltpu.VMEM((HC, 8, 2, SLOT, HEAD), BF16),
+            pltpu.VMEM((HC, 4, 2, 2, SLOT, HEAD), BF16),
             pltpu.VMEM((HEAD, 8 * SLOT), BF16),
             pltpu.VMEM((HEAD, 8 * SLOT), BF16),
             pltpu.VMEM((HC, 4, GROUP, SLOT, HEAD), BF16),
@@ -426,8 +437,8 @@
             dma((5,)),
             dma((2,)), dma((2,)),
             dma((3,)), dma((4,)),
-            dma((3, HC, 2)), dma((HC, 8)),
-            dma((HC, 4)), dma((HC, 4)),
+            dma((3, HC)), dma((HC, 4)),
+            dma((HC,)), dma((HC,)),
             dma((3, HC, 4)), dma((3, HC, 2)),
             dma((2,)), dma,
         ],

time: 99.1 us -> 99.7 us (level)
  no operation moved by 1% of the time
where the time goes in v2:
time: 99.7 us; the launch traced here: 98.8 us
  Pallas kernels  92.3 us (93%)
  local copies, waits for them, and re-layouts  5.85 us (6%)
    pallas_call x1, Pallas kernels, attn_call(): pl.pallas_call(attn_kernel, out_shape=(jax.ShapeDtypeStruct((8, 2, GROUP...  84.6 us
    pallas_call x1, Pallas kernels, finish_call(): pl.pallas_call(finish_kernel, grid=(4,), out_shape=(jax.ShapeDtypeStruct(...  7.66 us
    unnamed x11, local copies, waits for them, and re-layouts  5.85 us

profile of v2, /device:TPU:0, one launch (start us, length us, event | category | flops | bytes accessed | tf_op | source)
XLA Modules:
  0.0 98.8 jit_solution(7067424072953359778)
XLA Ops:
  0.6 0.0 copy-start.4
  0.6 84.6 %attn.1 = (bf16[8,2,512,128]{3,2,1,0:T(8,128)(2,1)}, bf16[8,2,512,128]{3,2,1,0:T(8,128)(2,1)}, bf16[8,2,2,128,128]{4,3,2,1,0:T(8,128)(2,1)}, f32[2,32,128]{2,1,0:T(8,128)}) custom-call(s32[3]{0:T(128)} %cu.3, s32[1,256]{1,0:T(1,128)} %bitcast.5, bf16[256,32,128]{2,1,0:T(8,128)(2,1)} %q.1, bf16[256,8,128]{2,1,0:T(8,128)(2,1)} %k.1, bf16[256,8,128]{2,1,0:T(8,128)(2,1)} %v.1, ...), custom_call_target="tpu_custom_call" | custom-call | tf_op jit(solution)/shard_map/attn/pallas_call | solution.py:403
  85.3 0.0 copy-done.4
  85.3 0.0 copy-start
  85.3 1.6 %copy-done = bf16[8,2,512,128]{3,2,1,0:T(8,128)(2,1)S(1)} copy-done((bf16[8,2,512,128]{3,2,1,0:T(8,128)(2,1)S(1)}, bf16[8,2,512,128]{3,2,1,0:T(8,128)(2,1)}, u32[]{:S(2)}) %copy-start) | copy-done | bytes 2097176
  86.9 0.0 copy-start.1
  86.9 1.6 %copy-done.1 = bf16[8,2,512,128]{3,2,1,0:T(8,128)(2,1)S(1)} copy-done((bf16[8,2,512,128]{3,2,1,0:T(8,128)(2,1)S(1)}, bf16[8,2,512,128]{3,2,1,0:T(8,128)(2,1)}, u32[]{:S(2)}) %copy-start.1) | copy-done | bytes 2097176
  88.5 0.0 copy-start.2
  88.5 1.2 %copy-done.2 = bf16[8,2,2,128,128]{4,3,2,1,0:T(8,128)(2,1)S(1)} copy-done((bf16[8,2,2,128,128]{4,3,2,1,0:T(8,128)(2,1)S(1)}, bf16[8,2,2,128,128]{4,3,2,1,0:T(8,128)(2,1)}, u32[]{:S(2)}) %copy-start.2) | copy-done | bytes 1048600
  89.7 0.0 copy-start.3
  89.7 0.8 copy-done.3
  90.5 7.7 %finish.1 = (bf16[256,32,128]{2,1,0:T(8,128)(2,1)}, bf16[256,32,128]{2,1,0:T(8,128)(2,1)}, bf16[256,8,128]{2,1,0:T(8,128)(2,1)}, bf16[256,8,128]{2,1,0:T(8,128)(2,1)}, f32[256,32]{1,0:T(8,128)S(1)}) custom-call(s32[3]{0:T(128)S(1)} %copy-done.4, bf16[8,2,4,128,128]{4,3,2,1,0:T(8,128)(2,1)S(1)} %bitcast.3, bf16[8,2,4,128,128]{4,3,2,1,0:T(8,128)(2,1)S(1)} %bitcast.4, ...), custom_call_target="tpu_custom_call" | custom-call | tf_op jit(solution)/shard_map/finish/pallas_call | solution.py:486
  98.1 0.7 copy.11
Async XLA Ops:
  0.6 84.6 %copy-start.4 = (s32[3]{0:T(128)S(1)}, s32[3]{0:T(128)}, u32[]{:S(2)}) copy-start(s32[3]{0:T(128)} %cu.3) | copy-start | bytes 40
  85.3 1.6 %copy-start = (bf16[8,2,512,128]{3,2,1,0:T(8,128)(2,1)S(1)}, bf16[8,2,512,128]{3,2,1,0:T(8,128)(2,1)}, u32[]{:S(2)}) copy-start(bf16[8,2,512,128]{3,2,1,0:T(8,128)(2,1)} %get-tuple-element.14) | copy-start | bytes 6291460
  86.9 1.6 %copy-start.1 = (bf16[8,2,512,128]{3,2,1,0:T(8,128)(2,1)S(1)}, bf16[8,2,512,128]{3,2,1,0:T(8,128)(2,1)}, u32[]{:S(2)}) copy-start(bf16[8,2,512,128]{3,2,1,0:T(8,128)(2,1)} %get-tuple-element.15) | copy-start | bytes 6291460
  88.5 1.2 %copy-start.2 = (bf16[8,2,2,128,128]{4,3,2,1,0:T(8,128)(2,1)S(1)}, bf16[8,2,2,128,128]{4,3,2,1,0:T(8,128)(2,1)}, u32[]{:S(2)}) copy-start(bf16[8,2,2,128,128]{4,3,2,1,0:T(8,128)(2,1)} %get-tuple-element.16.dkv_in) | copy-start | bytes 3145732
  89.7 0.8 copy-start.3

commit v3 on v2

--- a/solution.py
+++ b/solution.py
@@ -80,6 +80,9 @@
     push_do = remote(do.at[:, oth_heads, :], far_do, raw_ssem.at[1], raw_rsem.at[1], partner)
     push_val = [remote(valid, valid_all.at[r], val_ssem.at[i], val_rsem.at[r], dev) for i, dev in enumerate(peers)]
 
+    push_q.start()
+    push_do.start()
+
     def kv_relayout(up):
         def body(i, _):
             t0 = i * 16
@@ -119,8 +122,6 @@
 
     for h in range(HC):
         kv_push(h, 0, True).start()
-    push_q.start()
-    push_do.start()
     ld_val.wait()
     for cp in push_val:
         cp.start()

time: 99.7 us -> 99.7 us (level)
  no operation moved by 1% of the time
where the time goes in v3:
time: 99.7 us; the launch traced here: 98.8 us
  Pallas kernels  92.3 us (93%)
  local copies, waits for them, and re-layouts  5.85 us (6%)
    pallas_call x1, Pallas kernels, attn_call(): pl.pallas_call(attn_kernel, out_shape=(jax.ShapeDtypeStruct((8, 2, GROUP...  84.6 us
    pallas_call x1, Pallas kernels, finish_call(): pl.pallas_call(finish_kernel, grid=(4,), out_shape=(jax.ShapeDtypeStruct(...  7.66 us
    unnamed x11, local copies, waits for them, and re-layouts  5.85 us

profile of v3, /device:TPU:0, one launch (start us, length us, event | category | flops | bytes accessed | tf_op | source)
XLA Modules:
  0.0 98.8 jit_solution(7920237856844981296)
XLA Ops:
  0.6 0.0 copy-start.4
  0.6 84.6 %attn.1 = (bf16[8,2,512,128]{3,2,1,0:T(8,128)(2,1)}, bf16[8,2,512,128]{3,2,1,0:T(8,128)(2,1)}, bf16[8,2,2,128,128]{4,3,2,1,0:T(8,128)(2,1)}, f32[2,32,128]{2,1,0:T(8,128)}) custom-call(s32[3]{0:T(128)} %cu.3, s32[1,256]{1,0:T(1,128)} %bitcast.5, bf16[256,32,128]{2,1,0:T(8,128)(2,1)} %q.1, bf16[256,8,128]{2,1,0:T(8,128)(2,1)} %k.1, bf16[256,8,128]{2,1,0:T(8,128)(2,1)} %v.1, ...), custom_call_target="tpu_custom_call" | custom-call | tf_op jit(solution)/shard_map/attn/pallas_call | solution.py:404
  85.3 0.0 copy-done.4
  85.3 0.0 copy-start
  85.3 1.6 %copy-done = bf16[8,2,512,128]{3,2,1,0:T(8,128)(2,1)S(1)} copy-done((bf16[8,2,512,128]{3,2,1,0:T(8,128)(2,1)S(1)}, bf16[8,2,512,128]{3,2,1,0:T(8,128)(2,1)}, u32[]{:S(2)}) %copy-start) | copy-done | bytes 2097176
  86.9 0.0 copy-start.1
  86.9 1.6 %copy-done.1 = bf16[8,2,512,128]{3,2,1,0:T(8,128)(2,1)S(1)} copy-done((bf16[8,2,512,128]{3,2,1,0:T(8,128)(2,1)S(1)}, bf16[8,2,512,128]{3,2,1,0:T(8,128)(2,1)}, u32[]{:S(2)}) %copy-start.1) | copy-done | bytes 2097176
  88.5 0.0 copy-start.2
  88.5 1.2 %copy-done.2 = bf16[8,2,2,128,128]{4,3,2,1,0:T(8,128)(2,1)S(1)} copy-done((bf16[8,2,2,128,128]{4,3,2,1,0:T(8,128)(2,1)S(1)}, bf16[8,2,2,128,128]{4,3,2,1,0:T(8,128)(2,1)}, u32[]{:S(2)}) %copy-start.2) | copy-done | bytes 1048600
  89.7 0.0 copy-start.3
  89.7 0.8 copy-done.3
  90.5 7.7 %finish.1 = (bf16[256,32,128]{2,1,0:T(8,128)(2,1)}, bf16[256,32,128]{2,1,0:T(8,128)(2,1)}, bf16[256,8,128]{2,1,0:T(8,128)(2,1)}, bf16[256,8,128]{2,1,0:T(8,128)(2,1)}, f32[256,32]{1,0:T(8,128)S(1)}) custom-call(s32[3]{0:T(128)S(1)} %copy-done.4, bf16[8,2,4,128,128]{4,3,2,1,0:T(8,128)(2,1)S(1)} %bitcast.3, bf16[8,2,4,128,128]{4,3,2,1,0:T(8,128)(2,1)S(1)} %bitcast.4, ...), custom_call_target="tpu_custom_call" | custom-call | tf_op jit(solution)/shard_map/finish/pallas_call | solution.py:487
  98.1 0.7 copy.11
Async XLA Ops:
  0.6 84.6 %copy-start.4 = (s32[3]{0:T(128)S(1)}, s32[3]{0:T(128)}, u32[]{:S(2)}) copy-start(s32[3]{0:T(128)} %cu.3) | copy-start | bytes 40
  85.3 1.6 %copy-start = (bf16[8,2,512,128]{3,2,1,0:T(8,128)(2,1)S(1)}, bf16[8,2,512,128]{3,2,1,0:T(8,128)(2,1)}, u32[]{:S(2)}) copy-start(bf16[8,2,512,128]{3,2,1,0:T(8,128)(2,1)} %get-tuple-element.14) | copy-start | bytes 6291460
  86.9 1.6 %copy-start.1 = (bf16[8,2,512,128]{3,2,1,0:T(8,128)(2,1)S(1)}, bf16[8,2,512,128]{3,2,1,0:T(8,128)(2,1)}, u32[]{:S(2)}) copy-start(bf16[8,2,512,128]{3,2,1,0:T(8,128)(2,1)} %get-tuple-element.15) | copy-start | bytes 6291460
  88.5 1.2 %copy-start.2 = (bf16[8,2,2,128,128]{4,3,2,1,0:T(8,128)(2,1)S(1)}, bf16[8,2,2,128,128]{4,3,2,1,0:T(8,128)(2,1)}, u32[]{:S(2)}) copy-start(bf16[8,2,2,128,128]{4,3,2,1,0:T(8,128)(2,1)} %get-tuple-element.16.dkv_in) | copy-start | bytes 3145732
  89.7 0.8 copy-start.3

commit v4 on v3

--- a/solution.py
+++ b/solution.py
@@ -106,20 +106,18 @@
     ld_v.wait()
     kv_relayout(0)
 
-    @pl.when(chip == 0)
-    def _():
-        for h in range(HC):
-            kv_push(h, 1, False).start()
-            kv_push(h, 2, False).start()
-
+    def cross_next(ch, h):
+        @pl.when(chip == ch)
+        def _():
+            for to in (1, 2):
+                if h > 0:
+                    kv_push(h - 1, to, ch == 1).wait_send()
+            for to in (1, 2):
+                kv_push(h, to, ch == 1).start()
+
+    cross_next(0, 0)
     kv_relayout(1)
-
-    @pl.when(chip == 1)
-    def _():
-        for h in range(HC):
-            kv_push(h, 1, True).start()
-            kv_push(h, 2, True).start()
-
+    cross_next(1, 0)
     for h in range(HC):
         kv_push(h, 0, True).start()
     ld_val.wait()
@@ -145,8 +143,10 @@
 
     ld_q.wait()
     ld_do.wait()
+    cross_next(0, 1)
     q_relayout(c, raw_q, raw_do)
 
+    cross_next(0, 2)
     for i in range(3):
         remote(valid, valid_all.at[peers[i]], val_ssem.at[i], val_rsem.at[peers[i]], peers[i]).wait_recv()
     lane = lax.broadcasted_iota(jnp.int32, (SLOT, SLOT), 1)
@@ -175,6 +175,8 @@
         s = (7 - (2 * chip + oc)) if up else 2 * chip + oc
         caps[8 + ti] = jnp.where(sub <= lane, caps[s], FILL)
 
+    cross_next(0, 3)
+    cross_next(1, 1)
     push_q.wait_recv()
     push_do.wait_recv()
     q_relayout(pc, far_q, far_do)
@@ -249,6 +251,9 @@
             for ti in order:
                 s = slots[ti]
                 nk = s + 1
+                if ch == 1 and ti == 1:
+                    for nxt in (2, 3):
+                        pl.when(h == nxt - 2)(functools.partial(cross_next, 1, nxt))
                 for u in range(nk):
                     wait_slot(u)
                 qt = qh[h, ti].reshape(TILE, HEAD)
@@ -374,7 +379,7 @@
             @pl.when(chip == ch)
             def _():
                 for to in (1, 2):
-                    kv_push(h, to, ch == 1).wait_send()
+                    pl.when(h == HC - 1)(kv_push(h, to, ch == 1).wait_send)
         for which in range(3):
             for ti in range(4):
                 local, far = out_copies(h, ti, which)

time: 99.7 us -> 82.5 us (0.83)
  Pallas kernels: 92.3 us -> 75.1 us
    pallas_call x1, Pallas kernels: 84.6 us -> 67.4 us  [attn_call(): pl.pallas_call(attn_kernel, out_shape=(jax.ShapeDtypeStruct((8, 2, GROUP...]
where the time goes in v4:
time: 82.5 us; the launch traced here: 81.6 us
  Pallas kernels  75.1 us (91%)
  local copies, waits for them, and re-layouts  5.85 us (7%)
    pallas_call x1, Pallas kernels, attn_call(): pl.pallas_call(attn_kernel, out_shape=(jax.ShapeDtypeStruct((8, 2, GROUP...  67.4 us
    pallas_call x1, Pallas kernels, finish_call(): pl.pallas_call(finish_kernel, grid=(4,), out_shape=(jax.ShapeDtypeStruct(...  7.66 us
    unnamed x11, local copies, waits for them, and re-layouts  5.85 us

profile of v4, /device:TPU:0, one launch (start us, length us, event | category | flops | bytes accessed | tf_op | source)
XLA Modules:
  0.0 81.6 jit_solution(10377397143190056309)
XLA Ops:
  0.6 0.0 copy-start.4
  0.6 67.4 %attn.1 = (bf16[8,2,512,128]{3,2,1,0:T(8,128)(2,1)}, bf16[8,2,512,128]{3,2,1,0:T(8,128)(2,1)}, bf16[8,2,2,128,128]{4,3,2,1,0:T(8,128)(2,1)}, f32[2,32,128]{2,1,0:T(8,128)}) custom-call(s32[3]{0:T(128)} %cu.3, s32[1,256]{1,0:T(1,128)} %bitcast.5, bf16[256,32,128]{2,1,0:T(8,128)(2,1)} %q.1, bf16[256,8,128]{2,1,0:T(8,128)(2,1)} %k.1, bf16[256,8,128]{2,1,0:T(8,128)(2,1)} %v.1, ...), custom_call_target="tpu_custom_call" | custom-call | tf_op jit(solution)/shard_map/attn/pallas_call | solution.py:409
  68.1 0.0 copy-done.4
  68.1 0.0 copy-start
  68.1 1.6 %copy-done = bf16[8,2,512,128]{3,2,1,0:T(8,128)(2,1)S(1)} copy-done((bf16[8,2,512,128]{3,2,1,0:T(8,128)(2,1)S(1)}, bf16[8,2,512,128]{3,2,1,0:T(8,128)(2,1)}, u32[]{:S(2)}) %copy-start) | copy-done | bytes 2097176
  69.7 0.0 copy-start.1
  69.7 1.6 %copy-done.1 = bf16[8,2,512,128]{3,2,1,0:T(8,128)(2,1)S(1)} copy-done((bf16[8,2,512,128]{3,2,1,0:T(8,128)(2,1)S(1)}, bf16[8,2,512,128]{3,2,1,0:T(8,128)(2,1)}, u32[]{:S(2)}) %copy-start.1) | copy-done | bytes 2097176
  71.3 0.0 copy-start.2
  71.3 1.2 %copy-done.2 = bf16[8,2,2,128,128]{4,3,2,1,0:T(8,128)(2,1)S(1)} copy-done((bf16[8,2,2,128,128]{4,3,2,1,0:T(8,128)(2,1)S(1)}, bf16[8,2,2,128,128]{4,3,2,1,0:T(8,128)(2,1)}, u32[]{:S(2)}) %copy-start.2) | copy-done | bytes 1048600
  72.5 0.0 copy-start.3
  72.5 0.8 copy-done.3
  73.2 7.7 %finish.1 = (bf16[256,32,128]{2,1,0:T(8,128)(2,1)}, bf16[256,32,128]{2,1,0:T(8,128)(2,1)}, bf16[256,8,128]{2,1,0:T(8,128)(2,1)}, bf16[256,8,128]{2,1,0:T(8,128)(2,1)}, f32[256,32]{1,0:T(8,128)S(1)}) custom-call(s32[3]{0:T(128)S(1)} %copy-done.4, bf16[8,2,4,128,128]{4,3,2,1,0:T(8,128)(2,1)S(1)} %bitcast.3, bf16[8,2,4,128,128]{4,3,2,1,0:T(8,128)(2,1)S(1)} %bitcast.4, ...), custom_call_target="tpu_custom_call" | custom-call | tf_op jit(solution)/shard_map/finish/pallas_call | solution.py:492
  80.9 0.7 copy.11
Async XLA Ops:
  0.6 67.4 %copy-start.4 = (s32[3]{0:T(128)S(1)}, s32[3]{0:T(128)}, u32[]{:S(2)}) copy-start(s32[3]{0:T(128)} %cu.3) | copy-start | bytes 40
  68.1 1.6 %copy-start = (bf16[8,2,512,128]{3,2,1,0:T(8,128)(2,1)S(1)}, bf16[8,2,512,128]{3,2,1,0:T(8,128)(2,1)}, u32[]{:S(2)}) copy-start(bf16[8,2,512,128]{3,2,1,0:T(8,128)(2,1)} %get-tuple-element.14) | copy-start | bytes 6291460
  69.7 1.6 %copy-start.1 = (bf16[8,2,512,128]{3,2,1,0:T(8,128)(2,1)S(1)}, bf16[8,2,512,128]{3,2,1,0:T(8,128)(2,1)}, u32[]{:S(2)}) copy-start(bf16[8,2,512,128]{3,2,1,0:T(8,128)(2,1)} %get-tuple-element.15) | copy-start | bytes 6291460
  71.3 1.2 %copy-start.2 = (bf16[8,2,2,128,128]{4,3,2,1,0:T(8,128)(2,1)S(1)}, bf16[8,2,2,128,128]{4,3,2,1,0:T(8,128)(2,1)}, u32[]{:S(2)}) copy-start(bf16[8,2,2,128,128]{4,3,2,1,0:T(8,128)(2,1)} %get-tuple-element.16.dkv_in) | copy-start | bytes 3145732
  72.5 0.8 copy-start.3

commit v5 on v4

--- a/solution.py
+++ b/solution.py
@@ -44,9 +44,9 @@
 
 def attn_kernel(cu, valid, q, k, v, do, o_out, dq_out, dkv_out, lse_out,
                 raw_q, raw_do, far_q, far_do, raw_k, raw_v, kv_hm, kv_all, kt, vt, qh, doh, st, pb, db,
-                dkv_acc, dkv_in, o_st, dq_st, dkv_st, lse_st, caps, valid_all,
+                dkv_acc, dkv_in, o_st, dq_st, o_far, dq_far, dkv_st, lse_st, caps, valid_all,
                 in_sem, raw_ssem, raw_rsem, val_ssem, val_rsem, kv_ssem, kv_rsem,
-                part_ssem, part_rsem, out_sem, out_rsem, lse_sem, lse_rsem):
+                part_ssem, part_rsem, res_ssem, res_rsem, dkv_ssem, dkv_rsem, lse_sem, lse_rsem):
     r = lax.axis_index("cp")
     chip = r // 2
     c = r % 2
@@ -184,28 +184,55 @@
     def part_copy(h, i, n):
         return remote(dkv_acc.at[h, pl.ds(i, n)], dkv_in.at[h, pl.ds(0, n)], part_ssem.at[h], part_rsem.at[h], cross)
 
-    def out_copies(h, ti, which):
-        stage, out = ((o_st, o_out), (dq_st, dq_out), (dkv_st, dkv_out))[which]
+    def res_copy(p, ti, which):
+        stage, out = ((o_far, o_out), (dq_far, dq_out))[which]
+        dst = out.at[TILES[ti][1], :, pl.ds(pl.multiple_of(16 * c + 8 * p, 8), 8), :]
+        return remote(stage.at[p, ti], dst, res_ssem.at[which, p, ti], res_rsem.at[which, p, TILES[ti][1]], partner)
+
+    def dkv_copy(h, ti):
+        up = TILES[ti][1]
+        return remote(dkv_st.at[h, ti], dkv_out.at[4 * c + h, up], dkv_ssem.at[h, ti], dkv_rsem.at[h, up], partner)
+
+    def res_put(p):
+        heads = pl.ds(pl.multiple_of(16 * c + 8 * p, 8), 8)
+        for ti, (oc, up) in enumerate(TILES):
+            def body(i, _, keep):
+                at = pl.ds(pl.multiple_of(i * 16, 16), 16)
+                for stage, far, out in ((o_st, o_far, o_out), (dq_st, dq_far, dq_out)):
+                    x = jnp.concatenate([stage[e, ti, pl.ds(pl.multiple_of(g * SLOT + i * 16, 16), 16), :][None]
+                                         for e in range(2) for g in range(GROUP)], axis=0)
+                    y = jnp.transpose(x, (1, 0, 2))
+                    if keep:
+                        out[up, at, heads, :] = y
+                    else:
+                        far[p, ti, at, :, :] = y
+                return 0
+
+            @pl.when(c == oc)
+            def _():
+                lax.fori_loop(0, SLOT // 16, functools.partial(body, keep=True), 0)
+
+            @pl.when(c != oc)
+            def _():
+                lax.fori_loop(0, SLOT // 16, functools.partial(body, keep=False), 0)
+                for which in range(2):
+                    res_copy(p, ti, which).start()
+
+    def dkv_put(h, ti, parts):
         oc, up = TILES[ti]
-        dst = out.at[4 * c + h, up]
-        src = stage.at[h, ti]
-        return (pltpu.make_async_copy(src, dst, out_sem.at[which, h, ti]),
-                remote(src, dst, out_sem.at[which, h, ti], out_rsem.at[which, h, up], partner))
-
-    def out_start(h, ti, which):
-        local, far = out_copies(h, ti, which)
-        oc = TILES[ti][0]
 
         @pl.when(c == oc)
         def _():
-            local.start()
+            for w in range(2):
+                dkv_out[4 * c + h, up, w] = parts(w).astype(BF16)
 
         @pl.when(c != oc)
         def _():
-            far.start()
-
-    lse_local = pltpu.make_async_copy(lse_st.at[c], lse_out.at[:, own_heads, :], lse_sem.at[0])
-    lse_far = remote(lse_st.at[pc], lse_out.at[:, own_heads, :], lse_sem.at[1], lse_rsem, partner)
+            for w in range(2):
+                dkv_st[h, ti, w] = parts(w).astype(BF16)
+            dkv_copy(h, ti).start()
+
+    lse_far = remote(lse_st.at[pc], lse_out.at[:, own_heads, :], lse_sem, lse_rsem, partner)
 
     def kv_slot(h, s, which):
         return kv_all[h, min(s, 7 - s), int(s > 3), which]
@@ -295,8 +322,7 @@
                     dog = jnp.transpose(dt[g * SLOT:(g + 1) * SLOT, :])
                     dd.append(jnp.sum(og.astype(F32) * dog.astype(F32), axis=0, keepdims=True))
                     inv.append(i_l)
-                    o_st[h, ti, g * SLOT:(g + 1) * SLOT, :] = jnp.transpose(og)
-                out_start(h, ti, 0)
+                    o_st[h % 2, ti, g * SLOT:(g + 1) * SLOT, :] = jnp.transpose(og)
 
                 first = [u for u in range(nk) if u in sent] if (ch == 0 and ti >= 2) else []
                 rest = [u for u in range(nk) if u not in first]
@@ -334,29 +360,25 @@
                         part_copy(h, sent[0], len(sent)).start()
                 for g in range(GROUP):
                     dqg = (dqt[:, g * SLOT:(g + 1) * SLOT] * SCALE).astype(BF16)
-                    dq_st[h, ti, g * SLOT:(g + 1) * SLOT, :] = jnp.transpose(dqg)
-                out_start(h, ti, 1)
+                    dq_st[h % 2, ti, g * SLOT:(g + 1) * SLOT, :] = jnp.transpose(dqg)
             if ch == 1:
                 part_copy(h, sent[0], len(sent)).start()
             else:
                 for ti in (2, 3):
-                    for w in range(2):
-                        dkv_st[h, ti, w] = dkv_acc[h, slots[ti], w].astype(BF16)
-                    out_start(h, ti, 2)
+                    dkv_put(h, ti, lambda w, ti=ti: dkv_acc[h, slots[ti], w])
+            pl.when(h % 2 == 1)(lambda: res_put(h // 2))
             return 0
 
         lax.fori_loop(0, HC, head, 0)
 
-        lse_local.start()
+        lse_out[:, own_heads, :] = lse_st[c]
         lse_far.start()
 
         def tail(h, _):
             part_copy(h, kept[0], len(kept)).wait_recv()
             for i, u in enumerate(kept):
                 ti = slots.index(u)
-                for w in range(2):
-                    dkv_st[h, ti, w] = (dkv_acc[h, u, w] + dkv_in[h, i, w]).astype(BF16)
-                out_start(h, ti, 2)
+                dkv_put(h, ti, lambda w, u=u, i=i: dkv_acc[h, u, w] + dkv_in[h, i, w])
             return 0
         lax.fori_loop(0, HC, tail, 0)
 
@@ -380,27 +402,23 @@
             def _():
                 for to in (1, 2):
                     pl.when(h == HC - 1)(kv_push(h, to, ch == 1).wait_send)
-        for which in range(3):
-            for ti in range(4):
-                local, far = out_copies(h, ti, which)
-                oc = TILES[ti][0]
-
-                @pl.when(c == oc)
-                def _():
-                    local.wait()
-
-                @pl.when(c != oc)
-                def _():
-                    far.wait_send()
-            for up in range(2):
-                stage, out = ((o_st, o_out), (dq_st, dq_out), (dkv_st, dkv_out))[which]
-                remote(stage.at[h, 0], out.at[4 * pc + h, up], out_sem.at[which, h, 0],
-                       out_rsem.at[which, h, up], partner).wait_recv()
+        for ti in range(4):
+            pl.when(c != TILES[ti][0])(dkv_copy(h, ti).wait_send)
+        for up in range(2):
+            remote(dkv_st.at[h, 0], dkv_out.at[4 * pc + h, up], dkv_ssem.at[h, 0], dkv_rsem.at[h, up], partner).wait_recv()
         return 0
     lax.fori_loop(0, HC, drain, 0)
-    lse_local.wait()
+
+    for p in range(2):
+        for which in range(2):
+            stage, out = ((o_far, o_out), (dq_far, dq_out))[which]
+            for ti in range(4):
+                pl.when(c != TILES[ti][0])(res_copy(p, ti, which).wait_send)
+            for up in range(2):
+                dst = out.at[up, :, pl.ds(pl.multiple_of(16 * pc + 8 * p, 8), 8), :]
+                remote(stage.at[p, 0], dst, res_ssem.at[which, p, 0], res_rsem.at[which, p, up], partner).wait_recv()
     lse_far.wait_send()
-    remote(lse_st.at[0], lse_out.at[:, oth_heads, :], lse_sem.at[1], lse_rsem, partner).wait_recv()
+    remote(lse_st.at[0], lse_out.at[:, oth_heads, :], lse_sem, lse_rsem, partner).wait_recv()
 
 
 def attn_call(cu, valid, q, k, v, do):
@@ -409,13 +427,13 @@
     return pl.pallas_call(
         attn_kernel,
         out_shape=(
-            jax.ShapeDtypeStruct((8, 2, GROUP * SLOT, HEAD), BF16),
-            jax.ShapeDtypeStruct((8, 2, GROUP * SLOT, HEAD), BF16),
-            jax.ShapeDtypeStruct((8, 2, 2, SLOT, HEAD), BF16),
-            jax.ShapeDtypeStruct((2, 32, SLOT), F32),
+            pltpu.VMEM((2, SLOT, 32, HEAD), BF16),
+            pltpu.VMEM((2, SLOT, 32, HEAD), BF16),
+            pltpu.VMEM((8, 2, 2, SLOT, HEAD), BF16),
+            pltpu.VMEM((2, 32, SLOT), F32),
         ),
         in_specs=[pl.BlockSpec(memory_space=pltpu.SMEM)] + [any_spec] * 5,
-        out_specs=(any_spec,) * 4,
+        out_specs=(pl.BlockSpec(memory_space=pltpu.VMEM),) * 4,
         scratch_shapes=[
             pltpu.VMEM((256, 16, HEAD), BF16),
             pltpu.VMEM((256, 16, HEAD), BF16),
@@ -434,8 +452,10 @@
             pltpu.VMEM((8 * SLOT, TILE), BF16),
             pltpu.VMEM((HC, 8, 2, SLOT, HEAD), F32),
             pltpu.VMEM((HC, 4, 2, SLOT, HEAD), F32),
-            pltpu.VMEM((HC, 4, TILE, HEAD), BF16),
-            pltpu.VMEM((HC, 4, TILE, HEAD), BF16),
+            pltpu.VMEM((2, 4, TILE, HEAD), BF16),
+            pltpu.VMEM((2, 4, TILE, HEAD), BF16),
+            pltpu.VMEM((2, 4, SLOT, 8, HEAD), BF16),
+            pltpu.VMEM((2, 4, SLOT, 8, HEAD), BF16),
             pltpu.VMEM((HC, 4, 2, SLOT, HEAD), BF16),
             pltpu.VMEM((2, 2, 16, SLOT), F32),
             pltpu.VMEM((12, SLOT, SLOT), F32),
@@ -445,77 +465,78 @@
             dma((3,)), dma((4,)),
             dma((3, HC)), dma((HC, 4)),
             dma((HC,)), dma((HC,)),
-            dma((3, HC, 4)), dma((3, HC, 2)),
-            dma((2,)), dma,
+            dma((2, 2, 4)), dma((2, 2, 2)),
+            dma((HC, 4)), dma((HC, 2)),
+            dma, dma,
         ],
-        compiler_params=pltpu.CompilerParams(collective_id=0, has_side_effects=True, vmem_limit_bytes=60 * 1024 * 1024),
+        compiler_params=pltpu.CompilerParams(collective_id=0, has_side_effects=True, vmem_limit_bytes=44 * 1024 * 1024),
         name="attn",
     )(cu, valid, q, k, v, do)
 
 
-def finish_kernel(cu, o_in, dq_in, dkv_in, lse_in, o_out, dq_out, dk_out, dv_out, lse_out):
+def finish_kernel(cu, o_in, dq_in, dkv_in, lse_in, o_out, dq_out, dk_out, dv_out, lse_out, dk_t, dv_t, sem):
     l0 = lax.shift_right_logical(cu[1], 3)
-
-    def put(get, out):
+    rest = SLOT - l0
+
+    def copies(i, x, out):
+        runs = ((0, 0, 0, l0), (1, 0, l0, l0), (0, l0, 2 * l0, rest), (1, l0, SLOT + l0, rest))
+        return [pltpu.make_async_copy(x.at[up, pl.ds(at, n)], out.at[pl.ds(to, n)], sem.at[i, j])
+                for j, (up, at, to, n) in enumerate(runs)]
+
+    moves = copies(0, o_in, o_out) + copies(1, dq_in, dq_out)
+    for cp in moves:
+        cp.start()
+
+    for w, dst in ((0, dk_t), (1, dv_t)):
         for up in range(2):
             def body(i, _):
-                t0 = i * 16
-                x = get(up, pl.ds(pl.multiple_of(t0, 16), 16))
-                y = jnp.transpose(x, (1, 0, 2))
-                for j in range(16):
-                    out[src_row(up, t0 + j, l0)] = y[j]
+                at = pl.ds(pl.multiple_of(i * 16, 16), 16)
+                dst[up, at] = jnp.transpose(dkv_in[:, up, w, at, :], (1, 0, 2))
                 return 0
             lax.fori_loop(0, SLOT // 16, body, 0)
-
-    put(lambda up, at: o_in[:, up, :, at, :].reshape(8, 16, HEAD), o_out)
-    put(lambda up, at: dq_in[:, up, :, at, :].reshape(8, 16, HEAD), dq_out)
-
-    @pl.when(pl.program_id(0) == 0)
-    def _():
-        put(lambda up, at: dkv_in[:, up, 0, at, :], dk_out)
-        put(lambda up, at: dkv_in[:, up, 1, at, :], dv_out)
-        row = lax.broadcasted_iota(jnp.int32, (2 * SLOT, SLOT), 0)
-        col = lax.broadcasted_iota(jnp.int32, (2 * SLOT, SLOT), 1)
-        acc = None
-        for up in range(2):
-            if up:
-                src = jnp.where(col < l0, col + l0, col + SLOT)
-            else:
-                src = jnp.where(col < l0, col, col + l0)
-            pick = jnp.where(row == src, 1.0, 0.0)
-            part = lax.dot_general(pick, lse_in[up], NT, precision=lax.Precision.HIGHEST, preferred_element_type=F32)
-            acc = part if acc is None else acc + part
-        lse_out[...] = acc
-
-
-def finish_call(cu, o_hm, dq_hm, dkv_hm, lse_hm):
+        more = copies(2 + w, dst, (dk_out, dv_out)[w])
+        for cp in more:
+            cp.start()
+        moves += more
+
+    row = lax.broadcasted_iota(jnp.int32, (2 * SLOT, SLOT), 0)
+    col = lax.broadcasted_iota(jnp.int32, (2 * SLOT, SLOT), 1)
+    acc = None
+    for up in range(2):
+        if up:
+            src = jnp.where(col < l0, col + l0, col + SLOT)
+        else:
+            src = jnp.where(col < l0, col, col + l0)
+        pick = jnp.where(row == src, 1.0, 0.0)
+        part = lax.dot_general(lse_in[up], pick, NT, precision=lax.Precision.HIGHEST, preferred_element_type=F32)
+        acc = part if acc is None else acc + part
+    lse_out[...] = acc
+    for cp in moves:
+        cp.wait()
+
+
+def finish_call(cu, o_t, dq_t, dkv_hm, lse_hm):
+    any_spec = pl.BlockSpec(memory_space=pl.ANY)
+    vmem = pl.BlockSpec(memory_space=pltpu.VMEM)
     return pl.pallas_call(
         finish_kernel,
-        grid=(4,),
         out_shape=(
             jax.ShapeDtypeStruct((256, 32, HEAD), BF16),
             jax.ShapeDtypeStruct((256, 32, HEAD), BF16),
             jax.ShapeDtypeStruct((256, 8, HEAD), BF16),
             jax.ShapeDtypeStruct((256, 8, HEAD), BF16),
-            jax.ShapeDtypeStruct((256, 32), F32),
+            jax.ShapeDtypeStruct((32, 256), F32),
         ),
-        in_specs=[
-            pl.BlockSpec(memory_space=pltpu.SMEM),
-            pl.BlockSpec((2, 2, GROUP, SLOT, HEAD), lambda i: (i, 0, 0, 0, 0)),
-            pl.BlockSpec((2, 2, GROUP, SLOT, HEAD), lambda i: (i, 0, 0, 0, 0)),
-            pl.BlockSpec((8, 2, 2, SLOT, HEAD), lambda i: (0, 0, 0, 0, 0)),
-            pl.BlockSpec((2, 32, SLOT), lambda i: (0, 0, 0)),
+        in_specs=[pl.BlockSpec(memory_space=pltpu.SMEM)] + [vmem] * 4,
+        out_specs=(any_spec,) * 4 + (vmem,),
+        scratch_shapes=[
+            pltpu.VMEM((2, SLOT, 8, HEAD), BF16),
+            pltpu.VMEM((2, SLOT, 8, HEAD), BF16),
+            pltpu.SemaphoreType.DMA((4, 4)),
         ],
-        out_specs=(
-            pl.BlockSpec((256, 8, HEAD), lambda i: (0, i, 0)),
-            pl.BlockSpec((256, 8, HEAD), lambda i: (0, i, 0)),
-            pl.BlockSpec((256, 8, HEAD), lambda i: (0, 0, 0)),
-            pl.BlockSpec((256, 8, HEAD), lambda i: (0, 0, 0)),
-            pl.BlockSpec((256, 32), lambda i: (0, 0)),
-        ),
-        compiler_params=pltpu.CompilerParams(dimension_semantics=("arbitrary",), vmem_limit_bytes=40 * 1024 * 1024),
+        compiler_params=pltpu.CompilerParams(vmem_limit_bytes=16 * 1024 * 1024),
         name="finish",
-    )(cu, o_hm.reshape(8, 2, GROUP, SLOT, HEAD), dq_hm.reshape(8, 2, GROUP, SLOT, HEAD), dkv_hm, lse_hm)
+    )(cu, o_t, dq_t, dkv_hm, lse_hm)
 
 
 def solution(mesh):
@@ -523,9 +544,9 @@
     lse_spec = P(("dp", "cp"), None)
 
     def local(q, k, v, do, valid, cu):
-        o_hm, dq_hm, dkv_hm, lse_hm = attn_call(cu, valid.reshape(1, 256), q, k, v, do)
-        o, dq, dk, dv, lse = finish_call(cu, o_hm, dq_hm, dkv_hm, lse_hm)
-        return o, lse, dq, dk, dv
+        res = attn_call(cu, valid.reshape(1, 256), q, k, v, do)
+        o, dq, dk, dv, lse = finish_call(cu, *res)
+        return o, lse.T, dq, dk, dv
 
     return jax.shard_map(local, mesh=mesh, in_specs=(tok_spec,) * 4 + (P(("dp", "cp")), P("dp")),
                          out_specs=(tok_spec, lse_spec, tok_spec, tok_spec, tok_spec), check_vma=False)

time: 82.5 us -> 76.2 us (0.924)
  Pallas kernels: 75.1 us -> 69.2 us
  local copies, waits for them, and re-layouts: 5.85 us -> 5 us
    pallas_call x2, Pallas kernels: 75.1 us -> 69.2 us  [the longest x1 65.6 us: attn_call(): pl.pallas_call(attn_kernel, out_shape=(pltpu.VMEM((2, SLOT, 32, HEAD), BF...]
    unnamed x11 -> x10, local copies, waits for them, and re-layouts: 5.85 us -> 5 us
where the time goes in v5:
time: 76.2 us; the launch traced here: 75 us
  Pallas kernels  69.2 us (91%)
  local copies, waits for them, and re-layouts  5 us (7%)
  between operations  0.81 us (1%)
    pallas_call x1, Pallas kernels, attn_call(): pl.pallas_call(attn_kernel, out_shape=(pltpu.VMEM((2, SLOT, 32, HEAD), BF...  65.6 us
    unnamed x10, local copies, waits for them, and re-layouts  5 us
    pallas_call x1, Pallas kernels, finish_call(): pl.pallas_call(finish_kernel, out_shape=(jax.ShapeDtypeStruct((256, 32, H...  3.61 us

profile of v5, /device:TPU:0, one launch (start us, length us, event | category | flops | bytes accessed | tf_op | source)
XLA Modules:
  0.0 75.0 jit_solution(14865181334471469499)
XLA Ops:
  0.6 0.0 copy-start
  0.6 1.6 %copy-done = bf16[256,32,128]{2,1,0:T(8,128)(2,1)S(1)} copy-done((bf16[256,32,128]{2,1,0:T(8,128)(2,1)S(1)}, bf16[256,32,128]{2,1,0:T(8,128)(2,1)}, u32[]{:S(2)}) %copy-start) | copy-done | bytes 2097176
  2.2 0.0 copy-start.1
  2.2 1.0 %copy-done.1 = bf16[256,8,128]{2,1,0:T(8,128)(2,1)S(1)} copy-done((bf16[256,8,128]{2,1,0:T(8,128)(2,1)S(1)}, bf16[256,8,128]{2,1,0:T(8,128)(2,1)}, u32[]{:S(2)}) %copy-start.1) | copy-done | bytes 524312
  3.3 0.0 copy-start.2
  3.3 1.0 %copy-done.2 = bf16[256,8,128]{2,1,0:T(8,128)(2,1)S(1)} copy-done((bf16[256,8,128]{2,1,0:T(8,128)(2,1)S(1)}, bf16[256,8,128]{2,1,0:T(8,128)(2,1)}, u32[]{:S(2)}) %copy-start.2) | copy-done | bytes 524312
  4.3 0.0 copy-start.3
  4.3 0.7 copy-done.3
  5.0 0.0 copy-start.4
  5.0 0.7 copy-done.4
  5.6 65.6 %attn.1 = (bf16[2,128,32,128]{3,2,1,0:T(8,128)(2,1)S(1)}, bf16[2,128,32,128]{3,2,1,0:T(8,128)(2,1)S(1)}, bf16[8,2,2,128,128]{4,3,2,1,0:T(8,128)(2,1)S(1)}, f32[2,32,128]{2,1,0:T(8,128)S(1)}) custom-call(s32[3]{0:T(128)S(1)} %copy-done.3, s32[1,256]{1,0:T(1,128)S(1)} %bitcast.2, bf16[256,32,128]{2,1,0:T(8,128)(2,1)S(1)} %copy-done, ...), custom_call_target="tpu_custom_call" | custom-call | tf_op jit(solution)/shard_map/attn/pallas_call | solution.py:427
  71.2 3.6 %finish.1 = (bf16[256,32,128]{2,1,0:T(8,128)(2,1)}, bf16[256,32,128]{2,1,0:T(8,128)(2,1)}, bf16[256,8,128]{2,1,0:T(8,128)(2,1)}, bf16[256,8,128]{2,1,0:T(8,128)(2,1)}, f32[32,256]{1,0:T(8,128)}) custom-call(s32[3]{0:T(128)S(1)} %copy-done.3, bf16[2,128,32,128]{3,2,1,0:T(8,128)(2,1)S(1)} %get-tuple-element.14.o_in, ...), custom_call_target="tpu_custom_call" | custom-call | tf_op jit(solution)/shard_map/finish/pallas_call | solution.py:521
Async XLA Ops:
  0.6 1.6 %copy-start = (bf16[256,32,128]{2,1,0:T(8,128)(2,1)S(1)}, bf16[256,32,128]{2,1,0:T(8,128)(2,1)}, u32[]{:S(2)}) copy-start(bf16[256,32,128]{2,1,0:T(8,128)(2,1)} %q.1) | copy-start | bytes 6291460
  2.2 1.0 %copy-start.1 = (bf16[256,8,128]{2,1,0:T(8,128)(2,1)S(1)}, bf16[256,8,128]{2,1,0:T(8,128)(2,1)}, u32[]{:S(2)}) copy-start(bf16[256,8,128]{2,1,0:T(8,128)(2,1)} %k.1) | copy-start | bytes 1572868
  3.3 1.0 %copy-start.2 = (bf16[256,8,128]{2,1,0:T(8,128)(2,1)S(1)}, bf16[256,8,128]{2,1,0:T(8,128)(2,1)}, u32[]{:S(2)}) copy-start(bf16[256,8,128]{2,1,0:T(8,128)(2,1)} %v.1) | copy-start | bytes 1572868
  4.3 0.7 copy-start.3
  5.0 0.7 copy-start.4

commit v6 on v5

--- a/solution.py
+++ b/solution.py
@@ -469,7 +469,7 @@
             dma((HC, 4)), dma((HC, 2)),
             dma, dma,
         ],
-        compiler_params=pltpu.CompilerParams(collective_id=0, has_side_effects=True, vmem_limit_bytes=44 * 1024 * 1024),
+        compiler_params=pltpu.CompilerParams(collective_id=0, has_side_effects=True, vmem_limit_bytes=61300000),
         name="attn",
     )(cu, valid, q, k, v, do)
 

time: 76.2 us -> 71.5 us (0.938)
  local copies, waits for them, and re-layouts: 5 us -> 0.01 us
    unnamed x10 -> x2, local copies, waits for them, and re-layouts: 5 us -> 0.01 us
where the time goes in v6:
time: 71.5 us; the launch traced here: 70.6 us
  Pallas kernels  69.8 us (98%)
  between operations  0.82 us (1%)
    pallas_call x1, Pallas kernels, attn_call(): pl.pallas_call(attn_kernel, out_shape=(pltpu.VMEM((2, SLOT, 32, HEAD), BF...  66.2 us
    pallas_call x1, Pallas kernels, finish_call(): pl.pallas_call(finish_kernel, out_shape=(jax.ShapeDtypeStruct((256, 32, H...  3.61 us

profile of v6, /device:TPU:0, one launch (start us, length us, event | category | flops | bytes accessed | tf_op | source)
XLA Modules:
  0.0 70.6 jit_solution(12268296248095871097)
XLA Ops:
  0.6 0.0 copy-start
  0.6 66.2 %attn.1 = (bf16[2,128,32,128]{3,2,1,0:T(8,128)(2,1)S(1)}, bf16[2,128,32,128]{3,2,1,0:T(8,128)(2,1)S(1)}, bf16[8,2,2,128,128]{4,3,2,1,0:T(8,128)(2,1)S(1)}, f32[2,32,128]{2,1,0:T(8,128)S(1)}) custom-call(s32[3]{0:T(128)} %cu.3, s32[1,256]{1,0:T(1,128)} %bitcast.2, bf16[256,32,128]{2,1,0:T(8,128)(2,1)} %q.1, bf16[256,8,128]{2,1,0:T(8,128)(2,1)} %k.1, ...), custom_call_target="tpu_custom_call" | custom-call | tf_op jit(solution)/shard_map/attn/pallas_call | solution.py:427
  66.8 0.0 copy-done
  66.9 3.6 %finish.1 = (bf16[256,32,128]{2,1,0:T(8,128)(2,1)}, bf16[256,32,128]{2,1,0:T(8,128)(2,1)}, bf16[256,8,128]{2,1,0:T(8,128)(2,1)}, bf16[256,8,128]{2,1,0:T(8,128)(2,1)}, f32[32,256]{1,0:T(8,128)}) custom-call(s32[3]{0:T(128)S(1)} %copy-done, bf16[2,128,32,128]{3,2,1,0:T(8,128)(2,1)S(1)} %get-tuple-element.14.o_in, ...), custom_call_target="tpu_custom_call" | custom-call | tf_op jit(solution)/shard_map/finish/pallas_call | solution.py:521
Async XLA Ops:
  0.6 66.2 %copy-start = (s32[3]{0:T(128)S(1)}, s32[3]{0:T(128)}, u32[]{:S(2)}) copy-start(s32[3]{0:T(128)} %cu.3) | copy-start | bytes 40

commit v7 on v6

--- a/solution.py
+++ b/solution.py
@@ -16,6 +16,7 @@
 TILE = 512
 GROUP = 4
 HC = 4
+SWAP = 2
 SCALE = HEAD ** -0.5
 C2 = SCALE * math.log2(math.e)
 NT = (((1,), (1,)), ((), ()))
@@ -44,9 +45,9 @@
 
 def attn_kernel(cu, valid, q, k, v, do, o_out, dq_out, dkv_out, lse_out,
                 raw_q, raw_do, far_q, far_do, raw_k, raw_v, kv_hm, kv_all, kt, vt, qh, doh, st, pb, db,
-                dkv_acc, dkv_in, o_st, dq_st, o_far, dq_far, dkv_st, lse_st, caps, valid_all,
+                dkv_acc, dkv_in, o_st, dq_st, o_far, dq_far, dkv_st, back_st, lse_st, caps, valid_all,
                 in_sem, raw_ssem, raw_rsem, val_ssem, val_rsem, kv_ssem, kv_rsem,
-                part_ssem, part_rsem, res_ssem, res_rsem, dkv_ssem, dkv_rsem, lse_sem, lse_rsem):
+                part_ssem, part_rsem, swap_ssem, swap_rsem, back_ssem, back_rsem, res_ssem, res_rsem, dkv_ssem, dkv_rsem, lse_sem, lse_rsem):
     r = lax.axis_index("cp")
     chip = r // 2
     c = r % 2
@@ -106,14 +107,15 @@
     ld_v.wait()
     kv_relayout(0)
 
-    def cross_next(ch, h):
+    def cross_next(ch, h, upto=None):
         @pl.when(chip == ch)
         def _():
             for to in (1, 2):
                 if h > 0:
                     kv_push(h - 1, to, ch == 1).wait_send()
-            for to in (1, 2):
-                kv_push(h, to, ch == 1).start()
+            for e in range(h, upto or h + 1):
+                for to in (1, 2):
+                    kv_push(e, to, ch == 1).start()
 
     cross_next(0, 0)
     kv_relayout(1)
@@ -143,10 +145,9 @@
 
     ld_q.wait()
     ld_do.wait()
-    cross_next(0, 1)
+    cross_next(0, 1, HC)
     q_relayout(c, raw_q, raw_do)
 
-    cross_next(0, 2)
     for i in range(3):
         remote(valid, valid_all.at[peers[i]], val_ssem.at[i], val_rsem.at[peers[i]], peers[i]).wait_recv()
     lane = lax.broadcasted_iota(jnp.int32, (SLOT, SLOT), 1)
@@ -175,7 +176,6 @@
         s = (7 - (2 * chip + oc)) if up else 2 * chip + oc
         caps[8 + ti] = jnp.where(sub <= lane, caps[s], FILL)
 
-    cross_next(0, 3)
     cross_next(1, 1)
     push_q.wait_recv()
     push_do.wait_recv()
@@ -183,6 +183,19 @@
 
     def part_copy(h, i, n):
         return remote(dkv_acc.at[h, pl.ds(i, n)], dkv_in.at[h, pl.ds(0, n)], part_ssem.at[h], part_rsem.at[h], cross)
+
+    def part_run(ch, h, act):
+        if ch == 1:
+            act(part_copy(h, 0, 2))
+        else:
+            pl.when(h < SWAP)(lambda: act(part_copy(h, 2, 3)))
+            pl.when(h >= SWAP)(lambda: act(part_copy(h, 2, 4)))
+
+    def swap_copy(h):
+        return remote(dkv_acc.at[h, 5], dkv_in.at[h, 2], swap_ssem.at[h], swap_rsem.at[h], cross)
+
+    def swap_back(h):
+        return remote(back_st.at[h], dkv_out.at[4 * c + h, 1], back_ssem.at[h], back_rsem.at[4 * c + h], 2)
 
     def res_copy(p, ti, which):
         stage, out = ((o_far, o_out), (dq_far, dq_out))[which]
@@ -357,12 +370,13 @@
                                 dkv_acc[h, u, w] = dkv_acc[h, u, w] + new[w] if u in seen else new[w]
                             seen.add(u)
                     if part is first and ti == 3 and ch == 0:
-                        part_copy(h, sent[0], len(sent)).start()
+                        part_run(0, h, lambda cp: cp.start())
                 for g in range(GROUP):
                     dqg = (dqt[:, g * SLOT:(g + 1) * SLOT] * SCALE).astype(BF16)
                     dq_st[h % 2, ti, g * SLOT:(g + 1) * SLOT, :] = jnp.transpose(dqg)
             if ch == 1:
-                part_copy(h, sent[0], len(sent)).start()
+                part_run(1, h, lambda cp: cp.start())
+                pl.when(h < SWAP)(lambda: swap_copy(h).start())
             else:
                 for ti in (2, 3):
                     dkv_put(h, ti, lambda w, ti=ti: dkv_acc[h, slots[ti], w])
@@ -374,18 +388,46 @@
         lse_out[:, own_heads, :] = lse_st[c]
         lse_far.start()
 
+        if ch == 0:
+            def swapped(h, _):
+                swap_copy(h).wait_recv()
+                for w in range(2):
+                    back_st[h, w] = (dkv_in[h, 2, w] + dkv_acc[h, 5, w]).astype(BF16)
+                swap_back(h).start()
+                return 0
+            lax.fori_loop(0, SWAP, swapped, 0)
+
         def tail(h, _):
-            part_copy(h, kept[0], len(kept)).wait_recv()
+            part_run(1 - ch, h, lambda cp: cp.wait_recv())
             for i, u in enumerate(kept):
                 ti = slots.index(u)
-                dkv_put(h, ti, lambda w, u=u, i=i: dkv_acc[h, u, w] + dkv_in[h, i, w])
+                put = functools.partial(dkv_put, h, ti, lambda w, u=u, i=i: dkv_acc[h, u, w] + dkv_in[h, i, w])
+                if u == 5:
+                    pl.when(h >= SWAP)(put)
+                else:
+                    put()
             return 0
         lax.fori_loop(0, HC, tail, 0)
 
         def drain(h, _):
-            part_copy(h, sent[0], len(sent)).wait_send()
+            part_run(ch, h, lambda cp: cp.wait_send())
             return 0
         lax.fori_loop(0, HC, drain, 0)
+
+        def drain_swap(h, _):
+            if ch == 0:
+                swap_back(h).wait_send()
+            else:
+                swap_copy(h).wait_send()
+            return 0
+        lax.fori_loop(0, SWAP, drain_swap, 0)
+
+        if ch == 1:
+            @pl.when(c == 0)
+            def _():
+                for core in range(2):
+                    for h in range(SWAP):
+                        remote(back_st.at[h], dkv_out.at[4 * core + h, 1], back_ssem.at[h], back_rsem.at[4 * core + h], 2).wait_recv()
 
     pl.when(chip == 0)(functools.partial(run_chip, 0))
     pl.when(chip == 1)(functools.partial(run_chip, 1))
@@ -401,11 +443,17 @@
             @pl.when(chip == ch)
             def _():
                 for to in (1, 2):
-                    pl.when(h == HC - 1)(kv_push(h, to, ch == 1).wait_send)
+                    pl.when((h == HC - 1) if ch == 1 else (h > 0))(kv_push(h, to, ch == 1).wait_send)
+        far = jnp.logical_and(chip == 1, h < SWAP)
         for ti in range(4):
-            pl.when(c != TILES[ti][0])(dkv_copy(h, ti).wait_send)
+            sent = c != TILES[ti][0]
+            pl.when(jnp.logical_and(sent, jnp.logical_not(far)) if ti == 3 else sent)(dkv_copy(h, ti).wait_send)
         for up in range(2):
-            remote(dkv_st.at[h, 0], dkv_out.at[4 * pc + h, up], dkv_ssem.at[h, 0], dkv_rsem.at[h, up], partner).wait_recv()
+            come = remote(dkv_st.at[h, 0], dkv_out.at[4 * pc + h, up], dkv_ssem.at[h, 0], dkv_rsem.at[h, up], partner)
+            if up:
+                pl.when(jnp.logical_not(jnp.logical_and(far, c == 0)))(come.wait_recv)
+            else:
+                come.wait_recv()
         return 0
     lax.fori_loop(0, HC, drain, 0)
 
@@ -457,6 +505,7 @@
             pltpu.VMEM((2, 4, SLOT, 8, HEAD), BF16),
             pltpu.VMEM((2, 4, SLOT, 8, HEAD), BF16),
             pltpu.VMEM((HC, 4, 2, SLOT, HEAD), BF16),
+            pltpu.VMEM((HC, 2, SLOT, HEAD), BF16),
             pltpu.VMEM((2, 2, 16, SLOT), F32),
             pltpu.VMEM((12, SLOT, SLOT), F32),
             pltpu.VMEM((4, 1, 2 * SLOT), jnp.int32),
@@ -465,6 +514,7 @@
             dma((3,)), dma((4,)),
             dma((3, HC)), dma((HC, 4)),
             dma((HC,)), dma((HC,)),
+            dma((HC,)), dma((HC,)), dma((HC,)), dma((8,)),
             dma((2, 2, 4)), dma((2, 2, 2)),
             dma((HC, 4)), dma((HC, 2)),
             dma, dma,

time: 71.5 us -> 68.1 us (0.952); the launches traced: 70.6 us -> 68 us
  Pallas kernels: 69.8 us -> 67.2 us
    pallas_call x1, Pallas kernels: 66.2 us -> 63.6 us  [attn_call(): pl.pallas_call(attn_kernel, out_shape=(pltpu.VMEM((2, SLOT, 32, HEAD), BF...]
where the time goes in v7:
time: 68.1 us; the launch traced here: 68 us
  Pallas kernels  67.2 us (99%)
  between operations  0.82 us (1%)
    pallas_call x1, Pallas kernels, attn_call(): pl.pallas_call(attn_kernel, out_shape=(pltpu.VMEM((2, SLOT, 32, HEAD), BF...  63.6 us
    pallas_call x1, Pallas kernels, finish_call(): pl.pallas_call(finish_kernel, out_shape=(jax.ShapeDtypeStruct((256, 32, H...  3.6 us

profile of v7, /device:TPU:0, one launch (start us, length us, event | category | flops | bytes accessed | tf_op | source)
XLA Modules:
  0.0 68.0 jit_solution(11412010716593141332)
XLA Ops:
  0.6 0.0 copy-start
  0.6 63.6 %attn.1 = (bf16[2,128,32,128]{3,2,1,0:T(8,128)(2,1)S(1)}, bf16[2,128,32,128]{3,2,1,0:T(8,128)(2,1)S(1)}, bf16[8,2,2,128,128]{4,3,2,1,0:T(8,128)(2,1)S(1)}, f32[2,32,128]{2,1,0:T(8,128)S(1)}) custom-call(s32[3]{0:T(128)} %cu.3, s32[1,256]{1,0:T(1,128)} %bitcast.2, bf16[256,32,128]{2,1,0:T(8,128)(2,1)} %q.1, bf16[256,8,128]{2,1,0:T(8,128)(2,1)} %k.1, ...), custom_call_target="tpu_custom_call" | custom-call | tf_op jit(solution)/shard_map/attn/pallas_call | solution.py:475
  64.2 0.0 copy-done
  64.2 3.6 %finish.1 = (bf16[256,32,128]{2,1,0:T(8,128)(2,1)}, bf16[256,32,128]{2,1,0:T(8,128)(2,1)}, bf16[256,8,128]{2,1,0:T(8,128)(2,1)}, bf16[256,8,128]{2,1,0:T(8,128)(2,1)}, f32[32,256]{1,0:T(8,128)}) custom-call(s32[3]{0:T(128)S(1)} %copy-done, bf16[2,128,32,128]{3,2,1,0:T(8,128)(2,1)S(1)} %get-tuple-element.14.o_in, ...), custom_call_target="tpu_custom_call" | custom-call | tf_op jit(solution)/shard_map/finish/pallas_call | solution.py:571
Async XLA Ops:
  0.6 63.6 %copy-start = (s32[3]{0:T(128)S(1)}, s32[3]{0:T(128)}, u32[]{:S(2)}) copy-start(s32[3]{0:T(128)} %cu.3) | copy-start | bytes 40

commit v8 on v7

--- a/solution.py
+++ b/solution.py
@@ -16,7 +16,7 @@
 TILE = 512
 GROUP = 4
 HC = 4
-SWAP = 2
+SWAP = 3
 SCALE = HEAD ** -0.5
 C2 = SCALE * math.log2(math.e)
 NT = (((1,), (1,)), ((), ()))

time: 68.1 us -> 66.8 us (0.981)
  Pallas kernels: 67.2 us -> 65.8 us
    pallas_call x1, Pallas kernels: 63.6 us -> 62.2 us  [attn_call(): pl.pallas_call(attn_kernel, out_shape=(pltpu.VMEM((2, SLOT, 32, HEAD), BF...]
where the time goes in v8:
time: 66.8 us; the launch traced here: 66.6 us
  Pallas kernels  65.8 us (99%)
  between operations  0.82 us (1%)
    pallas_call x1, Pallas kernels, attn_call(): pl.pallas_call(attn_kernel, out_shape=(pltpu.VMEM((2, SLOT, 32, HEAD), BF...  62.2 us
    pallas_call x1, Pallas kernels, finish_call(): pl.pallas_call(finish_kernel, out_shape=(jax.ShapeDtypeStruct((256, 32, H...  3.61 us

profile of v8, /device:TPU:0, one launch (start us, length us, event | category | flops | bytes accessed | tf_op | source)
XLA Modules:
  0.0 66.6 jit_solution(18274660770107811930)
XLA Ops:
  0.6 0.0 copy-start
  0.6 62.2 %attn.1 = (bf16[2,128,32,128]{3,2,1,0:T(8,128)(2,1)S(1)}, bf16[2,128,32,128]{3,2,1,0:T(8,128)(2,1)S(1)}, bf16[8,2,2,128,128]{4,3,2,1,0:T(8,128)(2,1)S(1)}, f32[2,32,128]{2,1,0:T(8,128)S(1)}) custom-call(s32[3]{0:T(128)} %cu.3, s32[1,256]{1,0:T(1,128)} %bitcast.2, bf16[256,32,128]{2,1,0:T(8,128)(2,1)} %q.1, bf16[256,8,128]{2,1,0:T(8,128)(2,1)} %k.1, ...), custom_call_target="tpu_custom_call" | custom-call | tf_op jit(solution)/shard_map/attn/pallas_call | solution.py:475
  62.8 0.0 copy-done
  62.9 3.6 %finish.1 = (bf16[256,32,128]{2,1,0:T(8,128)(2,1)}, bf16[256,32,128]{2,1,0:T(8,128)(2,1)}, bf16[256,8,128]{2,1,0:T(8,128)(2,1)}, bf16[256,8,128]{2,1,0:T(8,128)(2,1)}, f32[32,256]{1,0:T(8,128)}) custom-call(s32[3]{0:T(128)S(1)} %copy-done, bf16[2,128,32,128]{3,2,1,0:T(8,128)(2,1)S(1)} %get-tuple-element.14.o_in, ...), custom_call_target="tpu_custom_call" | custom-call | tf_op jit(solution)/shard_map/finish/pallas_call | solution.py:571
Async XLA Ops:
  0.6 62.2 %copy-start = (s32[3]{0:T(128)S(1)}, s32[3]{0:T(128)}, u32[]{:S(2)}) copy-start(s32[3]{0:T(128)} %cu.3) | copy-start | bytes 40

commit v9 on v8

--- a/solution.py
+++ b/solution.py
@@ -43,7 +43,7 @@
     return jnp.where(t < l0, t, t + l0)
 
 
-def attn_kernel(cu, valid, q, k, v, do, o_out, dq_out, dkv_out, lse_out,
+def attn_kernel(cu_hbm, valid, q, k, v, do, o_out, dq_out, dkv_out, lse_out, cu,
                 raw_q, raw_do, far_q, far_do, raw_k, raw_v, kv_hm, kv_all, kt, vt, qh, doh, st, pb, db,
                 dkv_acc, dkv_in, o_st, dq_st, o_far, dq_far, dkv_st, back_st, lse_st, caps, valid_all,
                 in_sem, raw_ssem, raw_rsem, val_ssem, val_rsem, kv_ssem, kv_rsem,
@@ -55,7 +55,6 @@
     partner = chip * 2 + pc
     cross = (1 - chip) * 2 + c
     cross_o = (1 - chip) * 2 + pc
-    l0 = lax.shift_right_logical(cu[1], 3)
 
     def remote(src, dst, ssem, rsem, dev):
         return pltpu.make_async_remote_copy(src_ref=src, dst_ref=dst, send_sem=ssem, recv_sem=rsem,
@@ -68,13 +67,16 @@
     ld_q = pltpu.make_async_copy(q.at[:, own_heads, :], raw_q, in_sem.at[2])
     ld_do = pltpu.make_async_copy(do.at[:, own_heads, :], raw_do, in_sem.at[3])
     ld_val = pltpu.make_async_copy(valid, valid_all.at[r], in_sem.at[4])
-    for cp in (ld_k, ld_v, ld_q, ld_do, ld_val):
+    ld_cu = pltpu.make_async_copy(cu_hbm, cu, in_sem.at[5])
+    for cp in (ld_cu, ld_k, ld_v, ld_q, ld_do, ld_val):
         cp.start()
 
     barrier = pltpu.get_barrier_semaphore()
     for dev in (partner, cross, cross_o):
         pl.semaphore_signal(barrier, inc=1, device_id={"cp": dev}, device_id_type=MESH)
     pl.semaphore_wait(barrier, 3)
+    ld_cu.wait()
+    l0 = lax.shift_right_logical(cu[1], 3)
 
     peers = (partner, cross, cross_o)
     push_q = remote(q.at[:, oth_heads, :], far_q, raw_ssem.at[0], raw_rsem.at[0], partner)
@@ -107,19 +109,15 @@
     ld_v.wait()
     kv_relayout(0)
 
-    def cross_next(ch, h, upto=None):
+    def cross_send(ch, h):
         @pl.when(chip == ch)
         def _():
             for to in (1, 2):
-                if h > 0:
-                    kv_push(h - 1, to, ch == 1).wait_send()
-            for e in range(h, upto or h + 1):
-                for to in (1, 2):
-                    kv_push(e, to, ch == 1).start()
-
-    cross_next(0, 0)
+                kv_push(h, to, ch == 1).start()
+
+    cross_send(0, 0)
     kv_relayout(1)
-    cross_next(1, 0)
+    cross_send(1, 0)
     for h in range(HC):
         kv_push(h, 0, True).start()
     ld_val.wait()
@@ -145,9 +143,10 @@
 
     ld_q.wait()
     ld_do.wait()
-    cross_next(0, 1, HC)
+    cross_send(0, 1)
     q_relayout(c, raw_q, raw_do)
 
+    cross_send(0, 2)
     for i in range(3):
         remote(valid, valid_all.at[peers[i]], val_ssem.at[i], val_rsem.at[peers[i]], peers[i]).wait_recv()
     lane = lax.broadcasted_iota(jnp.int32, (SLOT, SLOT), 1)
@@ -176,7 +175,8 @@
         s = (7 - (2 * chip + oc)) if up else 2 * chip + oc
         caps[8 + ti] = jnp.where(sub <= lane, caps[s], FILL)
 
-    cross_next(1, 1)
+    cross_send(0, 3)
+    cross_send(1, 1)
     push_q.wait_recv()
     push_do.wait_recv()
     q_relayout(pc, far_q, far_do)
@@ -291,9 +291,6 @@
             for ti in order:
                 s = slots[ti]
                 nk = s + 1
-                if ch == 1 and ti == 1:
-                    for nxt in (2, 3):
-                        pl.when(h == nxt - 2)(functools.partial(cross_next, 1, nxt))
                 for u in range(nk):
                     wait_slot(u)
                 qt = qh[h, ti].reshape(TILE, HEAD)
@@ -375,8 +372,20 @@
                     dqg = (dqt[:, g * SLOT:(g + 1) * SLOT] * SCALE).astype(BF16)
                     dq_st[h % 2, ti, g * SLOT:(g + 1) * SLOT, :] = jnp.transpose(dqg)
             if ch == 1:
-                part_run(1, h, lambda cp: cp.start())
-                pl.when(h < SWAP)(lambda: swap_copy(h).start())
+                @pl.when(h < HC - 2)
+                def _():
+                    for to in (1, 2):
+                        kv_push(h + 2, to, True).start()
+
+                @pl.when(h == HC - 2)
+                def _():
+                    for e in range(SWAP):
+                        swap_copy(e).start()
+
+                @pl.when(h == HC - 1)
+                def _():
+                    for e in range(HC):
+                        part_copy(e, 0, 2).start()
             else:
                 for ti in (2, 3):
                     dkv_put(h, ti, lambda w, ti=ti: dkv_acc[h, slots[ti], w])
@@ -443,7 +452,7 @@
             @pl.when(chip == ch)
             def _():
                 for to in (1, 2):
-                    pl.when((h == HC - 1) if ch == 1 else (h > 0))(kv_push(h, to, ch == 1).wait_send)
+                    kv_push(h, to, ch == 1).wait_send()
         far = jnp.logical_and(chip == 1, h < SWAP)
         for ti in range(4):
             sent = c != TILES[ti][0]
@@ -479,9 +488,10 @@
             pltpu.VMEM((2, SLOT, 32, HEAD), BF16),
             pltpu.VMEM((8, 2, 2, SLOT, HEAD), BF16),
             pltpu.VMEM((2, 32, SLOT), F32),
+            pltpu.SMEM((3,), jnp.int32),
         ),
-        in_specs=[pl.BlockSpec(memory_space=pltpu.SMEM)] + [any_spec] * 5,
-        out_specs=(pl.BlockSpec(memory_space=pltpu.VMEM),) * 4,
+        in_specs=[any_spec] * 6,
+        out_specs=(pl.BlockSpec(memory_space=pltpu.VMEM),) * 4 + (pl.BlockSpec(memory_space=pltpu.SMEM),),
         scratch_shapes=[
             pltpu.VMEM((256, 16, HEAD), BF16),
             pltpu.VMEM((256, 16, HEAD), BF16),
@@ -509,7 +519,7 @@
             pltpu.VMEM((2, 2, 16, SLOT), F32),
             pltpu.VMEM((12, SLOT, SLOT), F32),
             pltpu.VMEM((4, 1, 2 * SLOT), jnp.int32),
-            dma((5,)),
+            dma((6,)),
             dma((2,)), dma((2,)),
             dma((3,)), dma((4,)),
             dma((3, HC)), dma((HC, 4)),
@@ -524,7 +534,7 @@
     )(cu, valid, q, k, v, do)
 
 
-def finish_kernel(cu, o_in, dq_in, dkv_in, lse_in, o_out, dq_out, dk_out, dv_out, lse_out, dk_t, dv_t, sem):
+def finish_kernel(o_in, dq_in, dkv_in, lse_in, cu, o_out, dq_out, dk_out, dv_out, lse_out, dk_t, dv_t, lse_t, sem, lse_sem):
     l0 = lax.shift_right_logical(cu[1], 3)
     rest = SLOT - l0
 
@@ -560,12 +570,14 @@
         pick = jnp.where(row == src, 1.0, 0.0)
         part = lax.dot_general(lse_in[up], pick, NT, precision=lax.Precision.HIGHEST, preferred_element_type=F32)
         acc = part if acc is None else acc + part
-    lse_out[...] = acc
-    for cp in moves:
+    lse_t[...] = acc
+    lse_move = pltpu.make_async_copy(lse_t, lse_out, lse_sem)
+    lse_move.start()
+    for cp in moves + [lse_move]:
         cp.wait()
 
 
-def finish_call(cu, o_t, dq_t, dkv_hm, lse_hm):
+def finish_call(o_t, dq_t, dkv_hm, lse_hm, cu):
     any_spec = pl.BlockSpec(memory_space=pl.ANY)
     vmem = pl.BlockSpec(memory_space=pltpu.VMEM)
     return pl.pallas_call(
@@ -577,16 +589,18 @@
             jax.ShapeDtypeStruct((256, 8, HEAD), BF16),
             jax.ShapeDtypeStruct((32, 256), F32),
         ),
-        in_specs=[pl.BlockSpec(memory_space=pltpu.SMEM)] + [vmem] * 4,
-        out_specs=(any_spec,) * 4 + (vmem,),
+        in_specs=[vmem] * 4 + [pl.BlockSpec(memory_space=pltpu.SMEM)],
+        out_specs=(any_spec,) * 5,
         scratch_shapes=[
             pltpu.VMEM((2, SLOT, 8, HEAD), BF16),
             pltpu.VMEM((2, SLOT, 8, HEAD), BF16),
+            pltpu.VMEM((32, 256), F32),
             pltpu.SemaphoreType.DMA((4, 4)),
+            pltpu.SemaphoreType.DMA,
         ],
         compiler_params=pltpu.CompilerParams(vmem_limit_bytes=16 * 1024 * 1024),
         name="finish",
-    )(cu, o_t, dq_t, dkv_hm, lse_hm)
+    )(o_t, dq_t, dkv_hm, lse_hm, cu)
 
 
 def solution(mesh):
@@ -595,7 +609,7 @@
 
     def local(q, k, v, do, valid, cu):
         res = attn_call(cu, valid.reshape(1, 256), q, k, v, do)
-        o, dq, dk, dv, lse = finish_call(cu, *res)
+        o, dq, dk, dv, lse = finish_call(*res)
         return o, lse.T, dq, dk, dv
 
     return jax.shard_map(local, mesh=mesh, in_specs=(tok_spec,) * 4 + (P(("dp", "cp")), P("dp")),

time: 66.8 us -> 69.4 us (1.039)
  Pallas kernels: 65.8 us -> 68.4 us
    pallas_call x1, Pallas kernels: 62.2 us -> 66 us  [attn_call(): pl.pallas_call(attn_kernel, out_shape=(pltpu.VMEM((2, SLOT, 32, HEAD), BF...]
    pallas_call x1, Pallas kernels: 3.61 us -> 2.46 us  [finish_call(): pl.pallas_call(finish_kernel, out_shape=(jax.ShapeDtypeStruct((256, 32, H...]
where the time goes in v9:
time: 69.4 us; the launch traced here: 69.2 us
  Pallas kernels  68.4 us (99%)
  between operations  0.8 us (1%)
    pallas_call x1, Pallas kernels, attn_call(): pl.pallas_call(attn_kernel, out_shape=(pltpu.VMEM((2, SLOT, 32, HEAD), BF...  66 us
    pallas_call x1, Pallas kernels, finish_call(): pl.pallas_call(finish_kernel, out_shape=(jax.ShapeDtypeStruct((256, 32, H...  2.46 us

profile of v9, /device:TPU:0, one launch (start us, length us, event | category | flops | bytes accessed | tf_op | source)
XLA Modules:
  0.0 69.2 jit_solution(14515622396529201783)
XLA Ops:
  0.6 66.0 %attn.1 = (bf16[2,128,32,128]{3,2,1,0:T(8,128)(2,1)S(1)}, bf16[2,128,32,128]{3,2,1,0:T(8,128)(2,1)S(1)}, bf16[8,2,2,128,128]{4,3,2,1,0:T(8,128)(2,1)S(1)}, f32[2,32,128]{2,1,0:T(8,128)S(1)}, s32[3]{0:T(128)S(4)}) custom-call(s32[3]{0:T(128)} %cu_hbm.1, s32[1,256]{1,0:T(1,128)} %bitcast.2, bf16[256,32,128]{2,1,0:T(8,128)(2,1)} %q.1, bf16[256,8,128]{2,1,0:T(8,128)(2,1)} %k.1, ...), custom_call_target="tpu_custom_call" | custom-call | tf_op jit(solution)/shard_map/attn/pallas_call | solution.py:484
  66.6 2.5 %finish.1 = (bf16[256,32,128]{2,1,0:T(8,128)(2,1)}, bf16[256,32,128]{2,1,0:T(8,128)(2,1)}, bf16[256,8,128]{2,1,0:T(8,128)(2,1)}, bf16[256,8,128]{2,1,0:T(8,128)(2,1)}, f32[32,256]{1,0:T(8,128)}) custom-call(bf16[2,128,32,128]{3,2,1,0:T(8,128)(2,1)S(1)} %get-tuple-element.15.o_in, bf16[2,128,32,128]{3,2,1,0:T(8,128)(2,1)S(1)} %get-tuple-element.16.dq_in, ...), custom_call_target="tpu_custom_call" | custom-call | tf_op jit(solution)/shard_map/finish/pallas_call | solution.py:583

commit v10 on v9

--- a/solution.py
+++ b/solution.py
@@ -44,7 +44,7 @@
 
 
 def attn_kernel(cu_hbm, valid, q, k, v, do, o_out, dq_out, dkv_out, lse_out, cu,
-                raw_q, raw_do, far_q, far_do, raw_k, raw_v, kv_hm, kv_all, kt, vt, qh, doh, st, pb, db,
+                raw_q, raw_do, far_q, far_do, raw_k, raw_v, kv_hm, kv_all, kt, vt, qh, doh, st0, st1, pb, db,
                 dkv_acc, dkv_in, o_st, dq_st, o_far, dq_far, dkv_st, back_st, lse_st, caps, valid_all,
                 in_sem, raw_ssem, raw_rsem, val_ssem, val_rsem, kv_ssem, kv_rsem,
                 part_ssem, part_rsem, swap_ssem, swap_rsem, back_ssem, back_rsem, res_ssem, res_rsem, dkv_ssem, dkv_rsem, lse_sem, lse_rsem):
@@ -257,13 +257,33 @@
         slots = [slot_of(ch, ti) for ti in range(4)]
         sent = [0, 1] if ch == 1 else [2, 3, 4, 5]
         kept = [0, 1] if ch == 0 else [2, 3, 4, 5]
-        order = [0, 1, 2, 3]
 
         def transposes(s):
             for src, dst in ((0, kt), (1, vt)):
                 dst[:, s * SLOT:(s + 1) * SLOT] = jnp.transpose(kv_slot(h_ref[0], s, src))
 
         h_ref = [None]
+        sts = (st0, st1)
+
+        def point(h, where):
+            if ch == 0:
+                return
+            kv = {(0, 3): 2, (1, 2): 3}
+            swaps = {(1, 4): (0, 1), (2, 4): (2,)}
+            parts = {(2, 2): (0,), (2, 4): (1,), (3, 4): (2, 3)}
+            for at in range(HC):
+                if not any((at, where) in d for d in (kv, swaps, parts)):
+                    continue
+
+                @pl.when(h == at)
+                def _():
+                    if (at, where) in kv:
+                        for to in (1, 2):
+                            kv_push(kv[at, where], to, True).start()
+                    for e in swaps.get((at, where), ()):
+                        swap_copy(e).start()
+                    for e in parts.get((at, where), ()):
+                        part_copy(e, 0, 2).start()
 
         def head(h, _):
             h_ref[0] = h
@@ -288,11 +308,15 @@
                     ready.add(u)
                     transposes(u)
 
-            for ti in order:
+            state = {}
+
+            def forward(ti):
+                point(h, ti)
                 s = slots[ti]
                 nk = s + 1
                 for u in range(nk):
                     wait_slot(u)
+                st = sts[ti % 2]
                 qt = qh[h, ti].reshape(TILE, HEAD)
                 dt = doh[h, ti].reshape(TILE, HEAD)
                 m8 = [None] * GROUP
@@ -334,58 +358,68 @@
                     inv.append(i_l)
                     o_st[h % 2, ti, g * SLOT:(g + 1) * SLOT, :] = jnp.transpose(og)
 
-                first = [u for u in range(nk) if u in sent] if (ch == 0 and ti >= 2) else []
-                rest = [u for u in range(nk) if u not in first]
-                dqt = None
-                for part in (first, rest):
-                    runs = []
-                    for u in part:
-                        if runs and runs[-1][1] == u and u - runs[-1][0] < 2:
-                            runs[-1][1] = u + 1
-                        else:
-                            runs.append([u, u + 1])
-                    for a, b in runs:
-                        n = b - a
-                        vb = kv_slots(h, a, b, 1)
-                        dp = mm(vb, dt, NT)
-                        for j in range(n):
-                            for g in range(GROUP):
-                                at = (slice((a + j) * SLOT, (a + j + 1) * SLOT), slice(g * SLOT, (g + 1) * SLOT))
-                                p = st[at] * inv[g]
-                                pb[at] = p.astype(BF16)
-                                ds = p * (dp[j * SLOT:(j + 1) * SLOT, g * SLOT:(g + 1) * SLOT] - dd[g])
-                                db[at] = ds.astype(BF16)
-                        dsb = db[a * SLOT:b * SLOT, :]
-                        dv = mm(pb[a * SLOT:b * SLOT, :], dt, NN)
-                        dk = mm(dsb, qt, NN) * SCALE
-                        dq = mm(kt[:, a * SLOT:b * SLOT], dsb, NN)
-                        dqt = dq if dqt is None else dqt + dq
-                        for j in range(n):
-                            u = a + j
-                            new = (dk[j * SLOT:(j + 1) * SLOT], dv[j * SLOT:(j + 1) * SLOT])
-                            for w in range(2):
-                                dkv_acc[h, u, w] = dkv_acc[h, u, w] + new[w] if u in seen else new[w]
-                            seen.add(u)
-                    if part is first and ti == 3 and ch == 0:
-                        part_run(0, h, lambda cp: cp.start())
+                state[ti] = [inv, dd, None]
+
+            def backward(ti, part):
+                inv, dd, dqt = state[ti]
+                qt = qh[h, ti].reshape(TILE, HEAD)
+                dt = doh[h, ti].reshape(TILE, HEAD)
+                st = sts[ti % 2]
+                runs = []
+                for u in part:
+                    if runs and runs[-1][1] == u and u - runs[-1][0] < 2:
+                        runs[-1][1] = u + 1
+                    else:
+                        runs.append([u, u + 1])
+                for a, b in runs:
+                    n = b - a
+                    vb = kv_slots(h, a, b, 1)
+                    dp = mm(vb, dt, NT)
+                    for j in range(n):
+                        for g in range(GROUP):
+                            at = (slice((a + j) * SLOT, (a + j + 1) * SLOT), slice(g * SLOT, (g + 1) * SLOT))
+                            p = st[at] * inv[g]
+                            pb[at] = p.astype(BF16)
+                            ds = p * (dp[j * SLOT:(j + 1) * SLOT, g * SLOT:(g + 1) * SLOT] - dd[g])
+                            db[at] = ds.astype(BF16)
+                    dsb = db[a * SLOT:b * SLOT, :]
+                    dv = mm(pb[a * SLOT:b * SLOT, :], dt, NN)
+                    dk = mm(dsb, qt, NN) * SCALE
+                    dq = mm(kt[:, a * SLOT:b * SLOT], dsb, NN)
+                    dqt = dq if dqt is None else dqt + dq
+                    for j in range(n):
+                        u = a + j
+                        new = (dk[j * SLOT:(j + 1) * SLOT], dv[j * SLOT:(j + 1) * SLOT])
+                        for w in range(2):
+                            dkv_acc[h, u, w] = dkv_acc[h, u, w] + new[w] if u in seen else new[w]
+                        seen.add(u)
+                state[ti][2] = dqt
+
+            def finish(ti):
+                dqt = state[ti][2]
                 for g in range(GROUP):
                     dqg = (dqt[:, g * SLOT:(g + 1) * SLOT] * SCALE).astype(BF16)
                     dq_st[h % 2, ti, g * SLOT:(g + 1) * SLOT, :] = jnp.transpose(dqg)
+
+            if ch == 0:
+                for ti in (0, 1):
+                    forward(ti)
+                    backward(ti, range(slots[ti] + 1))
+                    finish(ti)
+                for ti in (2, 3):
+                    forward(ti)
+                    backward(ti, sent)
+                part_run(0, h, lambda cp: cp.start())
+                for ti in (2, 3):
+                    backward(ti, [u for u in range(slots[ti] + 1) if u not in sent])
+                    finish(ti)
+            else:
+                for ti in range(4):
+                    forward(ti)
+                    backward(ti, range(slots[ti] + 1))
+                    finish(ti)
             if ch == 1:
-                @pl.when(h < HC - 2)
-                def _():
-                    for to in (1, 2):
-                        kv_push(h + 2, to, True).start()
-
-                @pl.when(h == HC - 2)
-                def _():
-                    for e in range(SWAP):
-                        swap_copy(e).start()
-
-                @pl.when(h == HC - 1)
-                def _():
-                    for e in range(HC):
-                        part_copy(e, 0, 2).start()
+                point(h, 4)
             else:
                 for ti in (2, 3):
                     dkv_put(h, ti, lambda w, ti=ti: dkv_acc[h, slots[ti], w])
@@ -506,6 +540,7 @@
             pltpu.VMEM((HC, 4, GROUP, SLOT, HEAD), BF16),
             pltpu.VMEM((HC, 4, GROUP, SLOT, HEAD), BF16),
             pltpu.VMEM((8 * SLOT, TILE), F32),
+            pltpu.VMEM((8 * SLOT, TILE), F32),
             pltpu.VMEM((8 * SLOT, TILE), BF16),
             pltpu.VMEM((8 * SLOT, TILE), BF16),
             pltpu.VMEM((HC, 8, 2, SLOT, HEAD), F32),

time: 69.4 us -> 65.3 us (0.941)
  Pallas kernels: 68.4 us -> 64.3 us
    pallas_call x1, Pallas kernels: 66 us -> 61.9 us  [attn_call(): pl.pallas_call(attn_kernel, out_shape=(pltpu.VMEM((2, SLOT, 32, HEAD), BF...]
where the time goes in v10:
time: 65.3 us; the launch traced here: 65.1 us
  Pallas kernels  64.3 us (98%)
  between operations  0.8 us (1%)
    pallas_call x1, Pallas kernels, attn_call(): pl.pallas_call(attn_kernel, out_shape=(pltpu.VMEM((2, SLOT, 32, HEAD), BF...  61.9 us
    pallas_call x1, Pallas kernels, finish_call(): pl.pallas_call(finish_kernel, out_shape=(jax.ShapeDtypeStruct((256, 32, H...  2.48 us

profile of v10, /device:TPU:0, one launch (start us, length us, event | category | flops | bytes accessed | tf_op | source)
XLA Modules:
  0.0 65.1 jit_solution(14162453162107320657)
XLA Ops:
  0.6 61.9 %attn.1 = (bf16[2,128,32,128]{3,2,1,0:T(8,128)(2,1)S(1)}, bf16[2,128,32,128]{3,2,1,0:T(8,128)(2,1)S(1)}, bf16[8,2,2,128,128]{4,3,2,1,0:T(8,128)(2,1)S(1)}, f32[2,32,128]{2,1,0:T(8,128)S(1)}, s32[3]{0:T(128)S(4)}) custom-call(s32[3]{0:T(128)} %cu_hbm.1, s32[1,256]{1,0:T(1,128)} %bitcast.2, bf16[256,32,128]{2,1,0:T(8,128)(2,1)} %q.1, bf16[256,8,128]{2,1,0:T(8,128)(2,1)} %k.1, ...), custom_call_target="tpu_custom_call" | custom-call | tf_op jit(solution)/shard_map/attn/pallas_call | solution.py:518
  62.5 2.5 %finish.1 = (bf16[256,32,128]{2,1,0:T(8,128)(2,1)}, bf16[256,32,128]{2,1,0:T(8,128)(2,1)}, bf16[256,8,128]{2,1,0:T(8,128)(2,1)}, bf16[256,8,128]{2,1,0:T(8,128)(2,1)}, f32[32,256]{1,0:T(8,128)}) custom-call(bf16[2,128,32,128]{3,2,1,0:T(8,128)(2,1)S(1)} %get-tuple-element.15.o_in, bf16[2,128,32,128]{3,2,1,0:T(8,128)(2,1)S(1)} %get-tuple-element.16.dq_in, ...), custom_call_target="tpu_custom_call" | custom-call | tf_op jit(solution)/shard_map/finish/pallas_call | solution.py:618

commit v11 on v10

--- a/solution.py
+++ b/solution.py
@@ -16,7 +16,7 @@
 TILE = 512
 GROUP = 4
 HC = 4
-SWAP = 3
+SW = (2, 2, 1, 0)
 SCALE = HEAD ** -0.5
 C2 = SCALE * math.log2(math.e)
 NT = (((1,), (1,)), ((), ()))
@@ -45,9 +45,9 @@
 
 def attn_kernel(cu_hbm, valid, q, k, v, do, o_out, dq_out, dkv_out, lse_out, cu,
                 raw_q, raw_do, far_q, far_do, raw_k, raw_v, kv_hm, kv_all, kt, vt, qh, doh, st0, st1, pb, db,
-                dkv_acc, dkv_in, o_st, dq_st, o_far, dq_far, dkv_st, back_st, lse_st, caps, valid_all,
+                dkv_acc, cross_in, near_in, swap_in, o_st, dq_st, o_far, dq_far, dkv_st, back_st, lse_st, caps, valid_all,
                 in_sem, raw_ssem, raw_rsem, val_ssem, val_rsem, kv_ssem, kv_rsem,
-                part_ssem, part_rsem, swap_ssem, swap_rsem, back_ssem, back_rsem, res_ssem, res_rsem, dkv_ssem, dkv_rsem, lse_sem, lse_rsem):
+                part_ssem, part_rsem, near_ssem, near_rsem, swap_ssem, swap_rsem, back_ssem, back_rsem, res_ssem, res_rsem, dkv_ssem, dkv_rsem, lse_sem, lse_rsem):
     r = lax.axis_index("cp")
     chip = r // 2
     c = r % 2
@@ -181,21 +181,38 @@
     push_do.wait_recv()
     q_relayout(pc, far_q, far_do)
 
-    def part_copy(h, i, n):
-        return remote(dkv_acc.at[h, pl.ds(i, n)], dkv_in.at[h, pl.ds(0, n)], part_ssem.at[h], part_rsem.at[h], cross)
-
-    def part_run(ch, h, act):
+    def part_copy(h, u, n=2):
+        up = int(u > 3)
+        i = u if u < 2 else u - 2
+        return remote(dkv_acc.at[h, pl.ds(2 * u, n)], cross_in.at[4 * c + h, up, pl.ds(0, n)], part_ssem.at[h, i],
+                      part_rsem.at[4 * c + h, up], min(u, 7 - u))
+
+    def part_wait(j, up, n=2):
+        remote(dkv_acc.at[0, pl.ds(0, n)], cross_in.at[j, up, pl.ds(0, n)], part_ssem.at[0, 0],
+               part_rsem.at[j, up], partner).wait_recv()
+
+    def near_copy(h, up, slot, n=2):
+        return remote(dkv_acc.at[h, pl.ds(2 * slot, n)], near_in.at[h, up, pl.ds(0, n)], near_ssem.at[h, up],
+                      near_rsem.at[h, up], partner)
+
+    def near_run(ch, h, act):
+        act(near_copy(h, 0, 2 * ch + pc))
         if ch == 1:
-            act(part_copy(h, 0, 2))
-        else:
-            pl.when(h < SWAP)(lambda: act(part_copy(h, 2, 3)))
-            pl.when(h >= SWAP)(lambda: act(part_copy(h, 2, 4)))
+            pl.when(c == 0)(lambda: act(near_copy(h, 1, 4)))
+            if SW[h] < 2:
+                pl.when(c == 1)(lambda: act(near_copy(h, 1, 5, 2 - SW[h])))
+
+    def near_wait(h, up, n=2):
+        near_copy(h, up, 0, n).wait_recv()
 
     def swap_copy(h):
-        return remote(dkv_acc.at[h, 5], dkv_in.at[h, 2], swap_ssem.at[h], swap_rsem.at[h], cross)
-
-    def swap_back(h):
-        return remote(back_st.at[h], dkv_out.at[4 * c + h, 1], back_ssem.at[h], back_rsem.at[4 * c + h], 2)
+        n = SW[h]
+        return remote(dkv_acc.at[h, pl.ds(12 - n, n)], swap_in.at[h, pl.ds(2 - n, n)], swap_ssem.at[h], swap_rsem.at[h], cross)
+
+    def swap_back(h, core):
+        at = pl.ds(2 - SW[h], SW[h])
+        j = 4 * core + h
+        return remote(back_st.at[h, at], dkv_out.at[j, 1, at], back_ssem.at[h], back_rsem.at[j], 2)
 
     def res_copy(p, ti, which):
         stage, out = ((o_far, o_out), (dq_far, dq_out))[which]
@@ -256,7 +273,6 @@
     def run_chip(ch):
         slots = [slot_of(ch, ti) for ti in range(4)]
         sent = [0, 1] if ch == 1 else [2, 3, 4, 5]
-        kept = [0, 1] if ch == 0 else [2, 3, 4, 5]
 
         def transposes(s):
             for src, dst in ((0, kt), (1, vt)):
@@ -283,7 +299,8 @@
                     for e in swaps.get((at, where), ()):
                         swap_copy(e).start()
                     for e in parts.get((at, where), ()):
-                        part_copy(e, 0, 2).start()
+                        for u in (0, 1):
+                            part_copy(e, u).start()
 
         def head(h, _):
             h_ref[0] = h
@@ -391,7 +408,7 @@
                         u = a + j
                         new = (dk[j * SLOT:(j + 1) * SLOT], dv[j * SLOT:(j + 1) * SLOT])
                         for w in range(2):
-                            dkv_acc[h, u, w] = dkv_acc[h, u, w] + new[w] if u in seen else new[w]
+                            dkv_acc[h, 2 * u + w] = dkv_acc[h, 2 * u + w] + new[w] if u in seen else new[w]
                         seen.add(u)
                 state[ti][2] = dqt
 
@@ -409,7 +426,11 @@
                 for ti in (2, 3):
                     forward(ti)
                     backward(ti, sent)
-                part_run(0, h, lambda cp: cp.start())
+                for u in (2, 3, 4):
+                    part_copy(h, u).start()
+                for at in range(HC):
+                    if SW[at] < 2:
+                        pl.when(h == at)(part_copy(at, 5, 2 - SW[at]).start)
                 for ti in (2, 3):
                     backward(ti, [u for u in range(slots[ti] + 1) if u not in sent])
                     finish(ti)
@@ -422,7 +443,9 @@
                 point(h, 4)
             else:
                 for ti in (2, 3):
-                    dkv_put(h, ti, lambda w, ti=ti: dkv_acc[h, slots[ti], w])
+                    dkv_put(h, ti, lambda w, ti=ti: dkv_acc[h, 2 * slots[ti] + w])
+            for at in range(HC):
+                pl.when(h == at)(functools.partial(near_run, ch, at, lambda cp: cp.start()))
             pl.when(h % 2 == 1)(lambda: res_put(h // 2))
             return 0
 
@@ -432,84 +455,78 @@
         lse_far.start()
 
         if ch == 0:
-            def swapped(h, _):
-                swap_copy(h).wait_recv()
-                for w in range(2):
-                    back_st[h, w] = (dkv_in[h, 2, w] + dkv_acc[h, 5, w]).astype(BF16)
-                swap_back(h).start()
-                return 0
-            lax.fori_loop(0, SWAP, swapped, 0)
-
-        def tail(h, _):
-            part_run(1 - ch, h, lambda cp: cp.wait_recv())
-            for i, u in enumerate(kept):
-                ti = slots.index(u)
-                put = functools.partial(dkv_put, h, ti, lambda w, u=u, i=i: dkv_acc[h, u, w] + dkv_in[h, i, w])
-                if u == 5:
-                    pl.when(h >= SWAP)(put)
+            for h in range(HC):
+                if SW[h]:
+                    swap_copy(h).wait_recv()
+                    for w in range(2 - SW[h], 2):
+                        back_st[h, w] = (swap_in[h, w] + dkv_acc[h, 10 + w]).astype(BF16)
+                    swap_back(h, c).start()
+
+        def early(h, _):
+            kv_push(h, 0, True).wait_send()
+            for to in (1, 2):
+                kv_push(h, to, ch == 1).wait_send()
+            if ch == 0:
+                for ti in (2, 3):
+                    pl.when(c != TILES[ti][0])(dkv_copy(h, ti).wait_send)
+                remote(dkv_st.at[h, 0], dkv_out.at[4 * pc + h, 1], dkv_ssem.at[h, 0], dkv_rsem.at[h, 1], partner).wait_recv()
+            return 0
+        lax.fori_loop(0, HC, early, 0)
+        for h in range(HC):
+            near_run(ch, h, lambda cp: cp.wait_send())
+        push_q.wait_send()
+        push_do.wait_send()
+        for cp in push_val:
+            cp.wait_send()
+        for p in range(2):
+            for which in range(2):
+                stage, out = ((o_far, o_out), (dq_far, dq_out))[which]
+                for ti in range(4):
+                    pl.when(c != TILES[ti][0])(res_copy(p, ti, which).wait_send)
+                for up in range(2):
+                    dst = out.at[up, :, pl.ds(pl.multiple_of(16 * pc + 8 * p, 8), 8), :]
+                    remote(stage.at[p, 0], dst, res_ssem.at[which, p, 0], res_rsem.at[which, p, up], partner).wait_recv()
+        lse_far.wait_send()
+        remote(lse_st.at[0], lse_out.at[:, oth_heads, :], lse_sem, lse_rsem, partner).wait_recv()
+
+        def add_up(h, up, slot, n):
+            if n == 0:
+                return
+            part_wait(4 * c + h, up, n)
+            for w in range(n):
+                dkv_out[4 * c + h, up, w] = (dkv_acc[h, 2 * slot + w] + cross_in[4 * c + h, up, w]).astype(BF16)
+            near_wait(h, up, n)
+            part_wait(4 * pc + h, up, n)
+            for w in range(n):
+                dkv_out[4 * pc + h, up, w] = (near_in[h, up, w] + cross_in[4 * pc + h, up, w]).astype(BF16)
+
+        for h in range(HC):
+            add_up(h, 0, 2 * ch + c, 2)
+            if ch == 1:
+                pl.when(c == 1)(functools.partial(add_up, h, 1, 4, 2))
+                pl.when(c == 0)(functools.partial(add_up, h, 1, 5, 2 - SW[h]))
+
+        for h in range(HC):
+            for u in sent:
+                n = 2 - SW[h] if u == 5 else 2
+                if n:
+                    part_copy(h, u, n).wait_send()
+            if SW[h]:
+                if ch == 0:
+                    swap_back(h, c).wait_send()
                 else:
-                    put()
-            return 0
-        lax.fori_loop(0, HC, tail, 0)
-
-        def drain(h, _):
-            part_run(ch, h, lambda cp: cp.wait_send())
-            return 0
-        lax.fori_loop(0, HC, drain, 0)
-
-        def drain_swap(h, _):
-            if ch == 0:
-                swap_back(h).wait_send()
-            else:
-                swap_copy(h).wait_send()
-            return 0
-        lax.fori_loop(0, SWAP, drain_swap, 0)
+                    swap_copy(h).wait_send()
 
         if ch == 1:
             @pl.when(c == 0)
             def _():
-                for core in range(2):
-                    for h in range(SWAP):
-                        remote(back_st.at[h], dkv_out.at[4 * core + h, 1], back_ssem.at[h], back_rsem.at[4 * core + h], 2).wait_recv()
+                for h in range(HC):
+                    if SW[h]:
+                        for core in range(2):
+                            swap_back(h, core).wait_recv()
 
     pl.when(chip == 0)(functools.partial(run_chip, 0))
     pl.when(chip == 1)(functools.partial(run_chip, 1))
-
-    push_q.wait_send()
-    push_do.wait_send()
-    for cp in push_val:
-        cp.wait_send()
-
-    def drain(h, _):
-        kv_push(h, 0, True).wait_send()
-        for ch in range(2):
-            @pl.when(chip == ch)
-            def _():
-                for to in (1, 2):
-                    kv_push(h, to, ch == 1).wait_send()
-        far = jnp.logical_and(chip == 1, h < SWAP)
-        for ti in range(4):
-            sent = c != TILES[ti][0]
-            pl.when(jnp.logical_and(sent, jnp.logical_not(far)) if ti == 3 else sent)(dkv_copy(h, ti).wait_send)
-        for up in range(2):
-            come = remote(dkv_st.at[h, 0], dkv_out.at[4 * pc + h, up], dkv_ssem.at[h, 0], dkv_rsem.at[h, up], partner)
-            if up:
-                pl.when(jnp.logical_not(jnp.logical_and(far, c == 0)))(come.wait_recv)
-            else:
-                come.wait_recv()
-        return 0
-    lax.fori_loop(0, HC, drain, 0)
-
-    for p in range(2):
-        for which in range(2):
-            stage, out = ((o_far, o_out), (dq_far, dq_out))[which]
-            for ti in range(4):
-                pl.when(c != TILES[ti][0])(res_copy(p, ti, which).wait_send)
-            for up in range(2):
-                dst = out.at[up, :, pl.ds(pl.multiple_of(16 * pc + 8 * p, 8), 8), :]
-                remote(stage.at[p, 0], dst, res_ssem.at[which, p, 0], res_rsem.at[which, p, up], partner).wait_recv()
-    lse_far.wait_send()
-    remote(lse_st.at[0], lse_out.at[:, oth_heads, :], lse_sem, lse_rsem, partner).wait_recv()
 
 
 def attn_call(cu, valid, q, k, v, do):
@@ -543,8 +560,10 @@
             pltpu.VMEM((8 * SLOT, TILE), F32),
             pltpu.VMEM((8 * SLOT, TILE), BF16),
             pltpu.VMEM((8 * SLOT, TILE), BF16),
-            pltpu.VMEM((HC, 8, 2, SLOT, HEAD), F32),
-            pltpu.VMEM((HC, 4, 2, SLOT, HEAD), F32),
+            pltpu.VMEM((HC, 16, SLOT, HEAD), F32),
+            pltpu.VMEM((8, 2, 2, SLOT, HEAD), F32),
+            pltpu.VMEM((HC, 2, 2, SLOT, HEAD), F32),
+            pltpu.VMEM((HC, 2, SLOT, HEAD), F32),
             pltpu.VMEM((2, 4, TILE, HEAD), BF16),
             pltpu.VMEM((2, 4, TILE, HEAD), BF16),
             pltpu.VMEM((2, 4, SLOT, 8, HEAD), BF16),
@@ -558,7 +577,7 @@
             dma((2,)), dma((2,)),
             dma((3,)), dma((4,)),
             dma((3, HC)), dma((HC, 4)),
-            dma((HC,)), dma((HC,)),
+            dma((HC, 4)), dma((8, 2)), dma((HC, 2)), dma((HC, 2)),
             dma((HC,)), dma((HC,)), dma((HC,)), dma((8,)),
             dma((2, 2, 4)), dma((2, 2, 2)),
             dma((HC, 4)), dma((HC, 2)),

time: 65.3 us -> 65.2 us (level)
  no operation moved by 1% of the time
where the time goes in v11:
time: 65.2 us; the launch traced here: 65.1 us
  Pallas kernels  64.3 us (99%)
  between operations  0.82 us (1%)
    pallas_call x1, Pallas kernels, attn_call(): pl.pallas_call(attn_kernel, out_shape=(pltpu.VMEM((2, SLOT, 32, HEAD), BF...  61.8 us
    pallas_call x1, Pallas kernels, finish_call(): pl.pallas_call(finish_kernel, out_shape=(jax.ShapeDtypeStruct((256, 32, H...  2.47 us

profile of v11, /device:TPU:0, one launch (start us, length us, event | category | flops | bytes accessed | tf_op | source)
XLA Modules:
  0.0 65.1 jit_solution(8408973959477050937)
XLA Ops:
  0.6 61.8 %attn.1 = (bf16[2,128,32,128]{3,2,1,0:T(8,128)(2,1)S(1)}, bf16[2,128,32,128]{3,2,1,0:T(8,128)(2,1)S(1)}, bf16[8,2,2,128,128]{4,3,2,1,0:T(8,128)(2,1)S(1)}, f32[2,32,128]{2,1,0:T(8,128)S(1)}, s32[3]{0:T(128)S(4)}) custom-call(s32[3]{0:T(128)} %cu_hbm.1, s32[1,256]{1,0:T(1,128)} %bitcast.2, bf16[256,32,128]{2,1,0:T(8,128)(2,1)} %q.1, bf16[256,8,128]{2,1,0:T(8,128)(2,1)} %k.1, ...), custom_call_target="tpu_custom_call" | custom-call | tf_op jit(solution)/shard_map/attn/pallas_call | solution.py:535
  62.5 2.5 %finish.1 = (bf16[256,32,128]{2,1,0:T(8,128)(2,1)}, bf16[256,32,128]{2,1,0:T(8,128)(2,1)}, bf16[256,8,128]{2,1,0:T(8,128)(2,1)}, bf16[256,8,128]{2,1,0:T(8,128)(2,1)}, f32[32,256]{1,0:T(8,128)}) custom-call(bf16[2,128,32,128]{3,2,1,0:T(8,128)(2,1)S(1)} %get-tuple-element.15.o_in, bf16[2,128,32,128]{3,2,1,0:T(8,128)(2,1)S(1)} %get-tuple-element.16.dq_in, ...), custom_call_target="tpu_custom_call" | custom-call | tf_op jit(solution)/shard_map/finish/pallas_call | solution.py:637

commit v12 on v11

--- a/solution.py
+++ b/solution.py
@@ -46,7 +46,7 @@
 def attn_kernel(cu_hbm, valid, q, k, v, do, o_out, dq_out, dkv_out, lse_out, cu,
                 raw_q, raw_do, far_q, far_do, raw_k, raw_v, kv_hm, kv_all, kt, vt, qh, doh, st0, st1, pb, db,
                 dkv_acc, cross_in, near_in, swap_in, o_st, dq_st, o_far, dq_far, dkv_st, back_st, lse_st, caps, valid_all,
-                in_sem, raw_ssem, raw_rsem, val_ssem, val_rsem, kv_ssem, kv_rsem,
+                in_sem, raw_ssem, raw_rsem, val_ssem, val_rsem, first_ssem, first_rsem, kv_ssem, kv_rsem,
                 part_ssem, part_rsem, near_ssem, near_rsem, swap_ssem, swap_rsem, back_ssem, back_rsem, res_ssem, res_rsem, dkv_ssem, dkv_rsem, lse_sem, lse_rsem):
     r = lax.axis_index("cp")
     chip = r // 2
@@ -68,7 +68,7 @@
     ld_do = pltpu.make_async_copy(do.at[:, own_heads, :], raw_do, in_sem.at[3])
     ld_val = pltpu.make_async_copy(valid, valid_all.at[r], in_sem.at[4])
     ld_cu = pltpu.make_async_copy(cu_hbm, cu, in_sem.at[5])
-    for cp in (ld_cu, ld_k, ld_v, ld_q, ld_do, ld_val):
+    for cp in (ld_cu, ld_k, ld_v, ld_val):
         cp.start()
 
     barrier = pltpu.get_barrier_semaphore()
@@ -83,8 +83,6 @@
     push_do = remote(do.at[:, oth_heads, :], far_do, raw_ssem.at[1], raw_rsem.at[1], partner)
     push_val = [remote(valid, valid_all.at[r], val_ssem.at[i], val_rsem.at[r], dev) for i, dev in enumerate(peers)]
 
-    push_q.start()
-    push_do.start()
 
     def kv_relayout(up):
         def body(i, _):
@@ -101,12 +99,25 @@
         ups = pl.ds(0, 2 if both else 1)
         return remote(kv_hm.at[head, ups], kv_all.at[h, r, ups], kv_ssem.at[to, h], kv_rsem.at[h, r], dev)
 
+    def kv_first(to, up):
+        head = 4 * c if to == 1 else 4 * pc
+        at = pl.ds(up, 1)
+        return remote(kv_hm.at[head, at], kv_all.at[0, r, at], first_ssem.at[to - 1, up], first_rsem.at[c, up],
+                      (cross, cross_o)[to - 1])
+
     def kv_wait(h, owner, both):
         ups = pl.ds(0, 2 if both else 1)
         remote(kv_hm.at[0, ups], kv_all.at[h, owner, ups], kv_ssem.at[0, h], kv_rsem.at[h, owner], partner).wait_recv()
 
+    def first_wait(owner):
+        for up in range(2):
+            at = pl.ds(up, 1)
+            remote(kv_hm.at[0, at], kv_all.at[0, owner, at], first_ssem.at[0, up], first_rsem.at[owner - 2, up], partner).wait_recv()
+
     ld_k.wait()
     ld_v.wait()
+    for cp in (ld_q, ld_do, push_q, push_do):
+        cp.start()
     kv_relayout(0)
 
     def cross_send(ch, h):
@@ -116,8 +127,16 @@
                 kv_push(h, to, ch == 1).start()
 
     cross_send(0, 0)
+
+    def send_first(up):
+        @pl.when(chip == 1)
+        def _():
+            for to in (1, 2):
+                kv_first(to, up).start()
+
+    send_first(0)
     kv_relayout(1)
-    cross_send(1, 0)
+    send_first(1)
     for h in range(HC):
         kv_push(h, 0, True).start()
     ld_val.wait()
@@ -319,7 +338,8 @@
                     new = [0, 1]
                 else:
                     for owner in (2, 3):
-                        kv_wait(h, owner, True)
+                        pl.when(h == 0)(functools.partial(first_wait, owner))
+                        pl.when(h > 0)(functools.partial(kv_wait, h, owner, True))
                     new = [2, 3, 4, 5]
                 for u in new:
                     ready.add(u)
@@ -425,9 +445,13 @@
                     finish(ti)
                 for ti in (2, 3):
                     forward(ti)
-                    backward(ti, sent)
-                for u in (2, 3, 4):
+                for ti in (2, 3):
+                    backward(ti, [2, 3])
+                for u in (2, 3):
                     part_copy(h, u).start()
+                for ti in (2, 3):
+                    backward(ti, [4, 5])
+                part_copy(h, 4).start()
                 for at in range(HC):
                     if SW[at] < 2:
                         pl.when(h == at)(part_copy(at, 5, 2 - SW[at]).start)
@@ -465,13 +489,20 @@
         def early(h, _):
             kv_push(h, 0, True).wait_send()
             for to in (1, 2):
-                kv_push(h, to, ch == 1).wait_send()
+                if ch == 0:
+                    kv_push(h, to, False).wait_send()
+                else:
+                    pl.when(h > 0)(kv_push(h, to, True).wait_send)
             if ch == 0:
                 for ti in (2, 3):
                     pl.when(c != TILES[ti][0])(dkv_copy(h, ti).wait_send)
                 remote(dkv_st.at[h, 0], dkv_out.at[4 * pc + h, 1], dkv_ssem.at[h, 0], dkv_rsem.at[h, 1], partner).wait_recv()
             return 0
         lax.fori_loop(0, HC, early, 0)
+        if ch == 1:
+            for to in (1, 2):
+                for up in range(2):
+                    kv_first(to, up).wait_send()
         for h in range(HC):
             near_run(ch, h, lambda cp: cp.wait_send())
         push_q.wait_send()
@@ -576,6 +607,7 @@
             dma((6,)),
             dma((2,)), dma((2,)),
             dma((3,)), dma((4,)),
+            dma((2, 2)), dma((2, 2)),
             dma((3, HC)), dma((HC, 4)),
             dma((HC, 4)), dma((8, 2)), dma((HC, 2)), dma((HC, 2)),
             dma((HC,)), dma((HC,)), dma((HC,)), dma((8,)),

time: 65.2 us -> 64.1 us (0.983)
  Pallas kernels: 64.3 us -> 63.1 us
    pallas_call x1, Pallas kernels: 61.8 us -> 60.7 us  [attn_call(): pl.pallas_call(attn_kernel, out_shape=(pltpu.VMEM((2, SLOT, 32, HEAD), BF...]
where the time goes in v12:
time: 64.1 us; the launch traced here: 63.9 us
  Pallas kernels  63.1 us (98%)
  between operations  0.82 us (1%)
    pallas_call x1, Pallas kernels, attn_call(): pl.pallas_call(attn_kernel, out_shape=(pltpu.VMEM((2, SLOT, 32, HEAD), BF...  60.7 us
    pallas_call x1, Pallas kernels, finish_call(): pl.pallas_call(finish_kernel, out_shape=(jax.ShapeDtypeStruct((256, 32, H...  2.47 us

profile of v12, /device:TPU:0, one launch (start us, length us, event | category | flops | bytes accessed | tf_op | source)
XLA Modules:
  0.0 63.9 jit_solution(2681685946297252881)
XLA Ops:
  0.6 60.7 %attn.1 = (bf16[2,128,32,128]{3,2,1,0:T(8,128)(2,1)S(1)}, bf16[2,128,32,128]{3,2,1,0:T(8,128)(2,1)S(1)}, bf16[8,2,2,128,128]{4,3,2,1,0:T(8,128)(2,1)S(1)}, f32[2,32,128]{2,1,0:T(8,128)S(1)}, s32[3]{0:T(128)S(4)}) custom-call(s32[3]{0:T(128)} %cu_hbm.1, s32[1,256]{1,0:T(1,128)} %bitcast.2, bf16[256,32,128]{2,1,0:T(8,128)(2,1)} %q.1, bf16[256,8,128]{2,1,0:T(8,128)(2,1)} %k.1, ...), custom_call_target="tpu_custom_call" | custom-call | tf_op jit(solution)/shard_map/attn/pallas_call | solution.py:566
  61.3 2.5 %finish.1 = (bf16[256,32,128]{2,1,0:T(8,128)(2,1)}, bf16[256,32,128]{2,1,0:T(8,128)(2,1)}, bf16[256,8,128]{2,1,0:T(8,128)(2,1)}, bf16[256,8,128]{2,1,0:T(8,128)(2,1)}, f32[32,256]{1,0:T(8,128)}) custom-call(bf16[2,128,32,128]{3,2,1,0:T(8,128)(2,1)S(1)} %get-tuple-element.15.o_in, bf16[2,128,32,128]{3,2,1,0:T(8,128)(2,1)S(1)} %get-tuple-element.16.dq_in, ...), custom_call_target="tpu_custom_call" | custom-call | tf_op jit(solution)/shard_map/finish/pallas_call | solution.py:669

commit v13 on v12

--- a/solution.py
+++ b/solution.py
@@ -16,7 +16,7 @@
 TILE = 512
 GROUP = 4
 HC = 4
-SW = (2, 2, 1, 0)
+SW = (2, 2, 2, 0)
 SCALE = HEAD ** -0.5
 C2 = SCALE * math.log2(math.e)
 NT = (((1,), (1,)), ((), ()))

time: 64.1 us -> 64.1 us (level); the launches traced: 63.9 us -> 63.2 us
  Pallas kernels: 63.1 us -> 62.4 us
    pallas_call x1, Pallas kernels: 60.7 us -> 60 us  [attn_call(): pl.pallas_call(attn_kernel, out_shape=(pltpu.VMEM((2, SLOT, 32, HEAD), BF...]
where the time goes in v13:
time: 64.1 us; the launch traced here: 63.2 us
  Pallas kernels  62.4 us (97%)
  between operations  0.82 us (1%)
    pallas_call x1, Pallas kernels, attn_call(): pl.pallas_call(attn_kernel, out_shape=(pltpu.VMEM((2, SLOT, 32, HEAD), BF...  60 us
    pallas_call x1, Pallas kernels, finish_call(): pl.pallas_call(finish_kernel, out_shape=(jax.ShapeDtypeStruct((256, 32, H...  2.46 us

profile of v13, /device:TPU:0, one launch (start us, length us, event | category | flops | bytes accessed | tf_op | source)
XLA Modules:
  0.0 63.2 jit_solution(9253850338647408733)
XLA Ops:
  0.6 60.0 %attn.1 = (bf16[2,128,32,128]{3,2,1,0:T(8,128)(2,1)S(1)}, bf16[2,128,32,128]{3,2,1,0:T(8,128)(2,1)S(1)}, bf16[8,2,2,128,128]{4,3,2,1,0:T(8,128)(2,1)S(1)}, f32[2,32,128]{2,1,0:T(8,128)S(1)}, s32[3]{0:T(128)S(4)}) custom-call(s32[3]{0:T(128)} %cu_hbm.1, s32[1,256]{1,0:T(1,128)} %bitcast.2, bf16[256,32,128]{2,1,0:T(8,128)(2,1)} %q.1, bf16[256,8,128]{2,1,0:T(8,128)(2,1)} %k.1, ...), custom_call_target="tpu_custom_call" | custom-call | tf_op jit(solution)/shard_map/attn/pallas_call | solution.py:566
  60.6 2.5 %finish.1 = (bf16[256,32,128]{2,1,0:T(8,128)(2,1)}, bf16[256,32,128]{2,1,0:T(8,128)(2,1)}, bf16[256,8,128]{2,1,0:T(8,128)(2,1)}, bf16[256,8,128]{2,1,0:T(8,128)(2,1)}, f32[32,256]{1,0:T(8,128)}) custom-call(bf16[2,128,32,128]{3,2,1,0:T(8,128)(2,1)S(1)} %get-tuple-element.15.o_in, bf16[2,128,32,128]{3,2,1,0:T(8,128)(2,1)S(1)} %get-tuple-element.16.dq_in, ...), custom_call_target="tpu_custom_call" | custom-call | tf_op jit(solution)/shard_map/finish/pallas_call | solution.py:669

commit v14 on v13

--- a/solution.py
+++ b/solution.py
@@ -45,9 +45,9 @@
 
 def attn_kernel(cu_hbm, valid, q, k, v, do, o_out, dq_out, dkv_out, lse_out, cu,
                 raw_q, raw_do, far_q, far_do, raw_k, raw_v, kv_hm, kv_all, kt, vt, qh, doh, st0, st1, pb, db,
-                dkv_acc, cross_in, near_in, swap_in, o_st, dq_st, o_far, dq_far, dkv_st, back_st, lse_st, caps, valid_all,
+                dkv_acc, cross_in, swap_in, o_st, dq_st, o_far, dq_far, dkv_st, back_st, lse_st, caps, valid_all,
                 in_sem, raw_ssem, raw_rsem, val_ssem, val_rsem, first_ssem, first_rsem, kv_ssem, kv_rsem,
-                part_ssem, part_rsem, near_ssem, near_rsem, swap_ssem, swap_rsem, back_ssem, back_rsem, res_ssem, res_rsem, dkv_ssem, dkv_rsem, lse_sem, lse_rsem):
+                part_ssem, part_rsem, swap_ssem, swap_rsem, back_ssem, back_rsem, res_ssem, res_rsem, dkv_ssem, dkv_rsem, lse_sem, lse_rsem):
     r = lax.axis_index("cp")
     chip = r // 2
     c = r % 2
@@ -200,29 +200,14 @@
     push_do.wait_recv()
     q_relayout(pc, far_q, far_do)
 
-    def part_copy(h, u, n=2):
-        up = int(u > 3)
-        i = u if u < 2 else u - 2
-        return remote(dkv_acc.at[h, pl.ds(2 * u, n)], cross_in.at[4 * c + h, up, pl.ds(0, n)], part_ssem.at[h, i],
-                      part_rsem.at[4 * c + h, up], min(u, 7 - u))
-
-    def part_wait(j, up, n=2):
-        remote(dkv_acc.at[0, pl.ds(0, n)], cross_in.at[j, up, pl.ds(0, n)], part_ssem.at[0, 0],
-               part_rsem.at[j, up], partner).wait_recv()
-
-    def near_copy(h, up, slot, n=2):
-        return remote(dkv_acc.at[h, pl.ds(2 * slot, n)], near_in.at[h, up, pl.ds(0, n)], near_ssem.at[h, up],
-                      near_rsem.at[h, up], partner)
-
-    def near_run(ch, h, act):
-        act(near_copy(h, 0, 2 * ch + pc))
+    def part_copy(h, i, first, n):
+        return remote(dkv_acc.at[h, pl.ds(first, n)], cross_in.at[h, pl.ds(4 * i, n)], part_ssem.at[h, i],
+                      part_rsem.at[h, i], cross)
+
+    def part_list(ch, h):
         if ch == 1:
-            pl.when(c == 0)(lambda: act(near_copy(h, 1, 4)))
-            if SW[h] < 2:
-                pl.when(c == 1)(lambda: act(near_copy(h, 1, 5, 2 - SW[h])))
-
-    def near_wait(h, up, n=2):
-        near_copy(h, up, 0, n).wait_recv()
+            return [part_copy(h, 0, 0, 4)]
+        return [part_copy(h, 0, 4, 4), part_copy(h, 1, 8, 4 - SW[h])]
 
     def swap_copy(h):
         n = SW[h]
@@ -238,9 +223,11 @@
         dst = out.at[TILES[ti][1], :, pl.ds(pl.multiple_of(16 * c + 8 * p, 8), 8), :]
         return remote(stage.at[p, ti], dst, res_ssem.at[which, p, ti], res_rsem.at[which, p, TILES[ti][1]], partner)
 
-    def dkv_copy(h, ti):
+    def dkv_copy(h, ti, n=2, j=None):
         up = TILES[ti][1]
-        return remote(dkv_st.at[h, ti], dkv_out.at[4 * c + h, up], dkv_ssem.at[h, ti], dkv_rsem.at[h, up], partner)
+        at = pl.ds(0, n)
+        return remote(dkv_st.at[h, ti, at], dkv_out.at[4 * c + h if j is None else j, up, at], dkv_ssem.at[h, ti],
+                      dkv_rsem.at[h, up], partner)
 
     def res_put(p):
         heads = pl.ds(pl.multiple_of(16 * c + 8 * p, 8), 8)
@@ -267,19 +254,19 @@
                 for which in range(2):
                     res_copy(p, ti, which).start()
 
-    def dkv_put(h, ti, parts):
+    def dkv_put(h, ti, parts, n=2):
         oc, up = TILES[ti]
 
         @pl.when(c == oc)
         def _():
-            for w in range(2):
+            for w in range(n):
                 dkv_out[4 * c + h, up, w] = parts(w).astype(BF16)
 
         @pl.when(c != oc)
         def _():
-            for w in range(2):
+            for w in range(n):
                 dkv_st[h, ti, w] = parts(w).astype(BF16)
-            dkv_copy(h, ti).start()
+            dkv_copy(h, ti, n).start()
 
     lse_far = remote(lse_st.at[pc], lse_out.at[:, own_heads, :], lse_sem, lse_rsem, partner)
 
@@ -318,8 +305,7 @@
                     for e in swaps.get((at, where), ()):
                         swap_copy(e).start()
                     for e in parts.get((at, where), ()):
-                        for u in (0, 1):
-                            part_copy(e, u).start()
+                        part_list(1, e)[0].start()
 
         def head(h, _):
             h_ref[0] = h
@@ -447,14 +433,11 @@
                     forward(ti)
                 for ti in (2, 3):
                     backward(ti, [2, 3])
-                for u in (2, 3):
-                    part_copy(h, u).start()
+                part_copy(h, 0, 4, 4).start()
                 for ti in (2, 3):
                     backward(ti, [4, 5])
-                part_copy(h, 4).start()
                 for at in range(HC):
-                    if SW[at] < 2:
-                        pl.when(h == at)(part_copy(at, 5, 2 - SW[at]).start)
+                    pl.when(h == at)(part_copy(at, 1, 8, 4 - SW[at]).start)
                 for ti in (2, 3):
                     backward(ti, [u for u in range(slots[ti] + 1) if u not in sent])
                     finish(ti)
@@ -468,8 +451,6 @@
             else:
                 for ti in (2, 3):
                     dkv_put(h, ti, lambda w, ti=ti: dkv_acc[h, 2 * slots[ti] + w])
-            for at in range(HC):
-                pl.when(h == at)(functools.partial(near_run, ch, at, lambda cp: cp.start()))
             pl.when(h % 2 == 1)(lambda: res_put(h // 2))
             return 0
 
@@ -503,8 +484,6 @@
             for to in (1, 2):
                 for up in range(2):
                     kv_first(to, up).wait_send()
-        for h in range(HC):
-            near_run(ch, h, lambda cp: cp.wait_send())
         push_q.wait_send()
         push_do.wait_send()
         for cp in push_val:
@@ -520,28 +499,25 @@
         lse_far.wait_send()
         remote(lse_st.at[0], lse_out.at[:, oth_heads, :], lse_sem, lse_rsem, partner).wait_recv()
 
-        def add_up(h, up, slot, n):
-            if n == 0:
-                return
-            part_wait(4 * c + h, up, n)
-            for w in range(n):
-                dkv_out[4 * c + h, up, w] = (dkv_acc[h, 2 * slot + w] + cross_in[4 * c + h, up, w]).astype(BF16)
-            near_wait(h, up, n)
-            part_wait(4 * pc + h, up, n)
-            for w in range(n):
-                dkv_out[4 * pc + h, up, w] = (near_in[h, up, w] + cross_in[4 * pc + h, up, w]).astype(BF16)
-
+        kept = [(i, ti) for i, ti in enumerate([0, 1] if ch == 0 else [0, 1, 2, 3])]
         for h in range(HC):
-            add_up(h, 0, 2 * ch + c, 2)
-            if ch == 1:
-                pl.when(c == 1)(functools.partial(add_up, h, 1, 4, 2))
-                pl.when(c == 0)(functools.partial(add_up, h, 1, 5, 2 - SW[h]))
-
+            for i, cp in enumerate(part_list(1 - ch, h)):
+                cp.wait_recv()
+                for k, ti in kept[2 * i:2 * i + 2]:
+                    u = slots[ti]
+                    n = 2 - SW[h] if u == 5 else 2
+                    if n:
+                        dkv_put(h, ti, lambda w, k=k, u=u: dkv_acc[h, 2 * u + w] + cross_in[h, 2 * k + w], n)
         for h in range(HC):
-            for u in sent:
-                n = 2 - SW[h] if u == 5 else 2
+            for k, ti in kept:
+                n = 2 - SW[h] if slots[ti] == 5 else 2
                 if n:
-                    part_copy(h, u, n).wait_send()
+                    pl.when(c != TILES[ti][0])(dkv_copy(h, ti, n).wait_send)
+                    pl.when(c == TILES[ti][0])(dkv_copy(h, ti, n, 4 * pc + h).wait_recv)
+
+        for h in range(HC):
+            for cp in part_list(ch, h):
+                cp.wait_send()
             if SW[h]:
                 if ch == 0:
                     swap_back(h, c).wait_send()
@@ -592,8 +568,7 @@
             pltpu.VMEM((8 * SLOT, TILE), BF16),
             pltpu.VMEM((8 * SLOT, TILE), BF16),
             pltpu.VMEM((HC, 16, SLOT, HEAD), F32),
-            pltpu.VMEM((8, 2, 2, SLOT, HEAD), F32),
-            pltpu.VMEM((HC, 2, 2, SLOT, HEAD), F32),
+            pltpu.VMEM((HC, 8, SLOT, HEAD), F32),
             pltpu.VMEM((HC, 2, SLOT, HEAD), F32),
             pltpu.VMEM((2, 4, TILE, HEAD), BF16),
             pltpu.VMEM((2, 4, TILE, HEAD), BF16),
@@ -609,7 +584,7 @@
             dma((3,)), dma((4,)),
             dma((2, 2)), dma((2, 2)),
             dma((3, HC)), dma((HC, 4)),
-            dma((HC, 4)), dma((8, 2)), dma((HC, 2)), dma((HC, 2)),
+            dma((HC, 2)), dma((HC, 2)),
             dma((HC,)), dma((HC,)), dma((HC,)), dma((8,)),
             dma((2, 2, 4)), dma((2, 2, 2)),
             dma((HC, 4)), dma((HC, 2)),

time: 64.1 us -> 65.6 us (1.023); the launches traced: 63.2 us -> 65.5 us
  Pallas kernels: 62.4 us -> 64.7 us
    pallas_call x1, Pallas kernels: 60 us -> 62.2 us  [attn_call(): pl.pallas_call(attn_kernel, out_shape=(pltpu.VMEM((2, SLOT, 32, HEAD), BF...]
where the time goes in v14:
time: 65.6 us; the launch traced here: 65.5 us
  Pallas kernels  64.7 us (99%)
  between operations  0.82 us (1%)
    pallas_call x1, Pallas kernels, attn_call(): pl.pallas_call(attn_kernel, out_shape=(pltpu.VMEM((2, SLOT, 32, HEAD), BF...  62.2 us
    pallas_call x1, Pallas kernels, finish_call(): pl.pallas_call(finish_kernel, out_shape=(jax.ShapeDtypeStruct((256, 32, H...  2.47 us

profile of v14, /device:TPU:0, one launch (start us, length us, event | category | flops | bytes accessed | tf_op | source)
XLA Modules:
  0.0 65.5 jit_solution(367075116351059756)
XLA Ops:
  0.6 62.2 %attn.1 = (bf16[2,128,32,128]{3,2,1,0:T(8,128)(2,1)S(1)}, bf16[2,128,32,128]{3,2,1,0:T(8,128)(2,1)S(1)}, bf16[8,2,2,128,128]{4,3,2,1,0:T(8,128)(2,1)S(1)}, f32[2,32,128]{2,1,0:T(8,128)S(1)}, s32[3]{0:T(128)S(4)}) custom-call(s32[3]{0:T(128)} %cu_hbm.1, s32[1,256]{1,0:T(1,128)} %bitcast.2, bf16[256,32,128]{2,1,0:T(8,128)(2,1)} %q.1, bf16[256,8,128]{2,1,0:T(8,128)(2,1)} %k.1, ...), custom_call_target="tpu_custom_call" | custom-call | tf_op jit(solution)/shard_map/attn/pallas_call | solution.py:542
  62.8 2.5 %finish.1 = (bf16[256,32,128]{2,1,0:T(8,128)(2,1)}, bf16[256,32,128]{2,1,0:T(8,128)(2,1)}, bf16[256,8,128]{2,1,0:T(8,128)(2,1)}, bf16[256,8,128]{2,1,0:T(8,128)(2,1)}, f32[32,256]{1,0:T(8,128)}) custom-call(bf16[2,128,32,128]{3,2,1,0:T(8,128)(2,1)S(1)} %get-tuple-element.15.o_in, bf16[2,128,32,128]{3,2,1,0:T(8,128)(2,1)S(1)} %get-tuple-element.16.dq_in, ...), custom_call_target="tpu_custom_call" | custom-call | tf_op jit(solution)/shard_map/finish/pallas_call | solution.py:644

commit v15 on v13

--- a/solution.py
+++ b/solution.py
@@ -74,7 +74,6 @@
     barrier = pltpu.get_barrier_semaphore()
     for dev in (partner, cross, cross_o):
         pl.semaphore_signal(barrier, inc=1, device_id={"cp": dev}, device_id_type=MESH)
-    pl.semaphore_wait(barrier, 3)
     ld_cu.wait()
     l0 = lax.shift_right_logical(cu[1], 3)
 
@@ -116,9 +115,8 @@
 
     ld_k.wait()
     ld_v.wait()
-    for cp in (ld_q, ld_do, push_q, push_do):
-        cp.start()
     kv_relayout(0)
+    pl.semaphore_wait(barrier, 3)
 
     def cross_send(ch, h):
         @pl.when(chip == ch)
@@ -135,6 +133,8 @@
                 kv_first(to, up).start()
 
     send_first(0)
+    for cp in (ld_q, ld_do, push_q, push_do):
+        cp.start()
     kv_relayout(1)
     send_first(1)
     for h in range(HC):
@@ -202,12 +202,11 @@
 
     def part_copy(h, u, n=2):
         up = int(u > 3)
-        i = u if u < 2 else u - 2
-        return remote(dkv_acc.at[h, pl.ds(2 * u, n)], cross_in.at[4 * c + h, up, pl.ds(0, n)], part_ssem.at[h, i],
+        return remote(dkv_acc.at[h, pl.ds(2 * u, n)], cross_in.at[4 * c + h, up, pl.ds(0, n)], part_ssem,
                       part_rsem.at[4 * c + h, up], min(u, 7 - u))
 
     def part_wait(j, up, n=2):
-        remote(dkv_acc.at[0, pl.ds(0, n)], cross_in.at[j, up, pl.ds(0, n)], part_ssem.at[0, 0],
+        remote(dkv_acc.at[0, pl.ds(0, n)], cross_in.at[j, up, pl.ds(0, n)], part_ssem,
                part_rsem.at[j, up], partner).wait_recv()
 
     def near_copy(h, up, slot, n=2):
@@ -537,11 +536,11 @@
                 pl.when(c == 1)(functools.partial(add_up, h, 1, 4, 2))
                 pl.when(c == 0)(functools.partial(add_up, h, 1, 5, 2 - SW[h]))
 
+        units = HC * 4 if ch == 1 else HC * 8 - sum(SW)
+        rows = next(a for a in (1, 2, 3, 4) if units % a == 0 and units // a <= 16)
+        block = dkv_acc.at[pl.ds(0, rows), pl.ds(0, units // rows)]
+        remote(block, block, part_ssem, part_rsem.at[0, 0], partner).wait_send()
         for h in range(HC):
-            for u in sent:
-                n = 2 - SW[h] if u == 5 else 2
-                if n:
-                    part_copy(h, u, n).wait_send()
             if SW[h]:
                 if ch == 0:
                     swap_back(h, c).wait_send()
@@ -609,7 +608,7 @@
             dma((3,)), dma((4,)),
             dma((2, 2)), dma((2, 2)),
             dma((3, HC)), dma((HC, 4)),
-            dma((HC, 4)), dma((8, 2)), dma((HC, 2)), dma((HC, 2)),
+            dma, dma((8, 2)), dma((HC, 2)), dma((HC, 2)),
             dma((HC,)), dma((HC,)), dma((HC,)), dma((8,)),
             dma((2, 2, 4)), dma((2, 2, 2)),
             dma((HC, 4)), dma((HC, 2)),

time: 64.1 us -> 63.6 us (level)
  no operation moved by 1% of the time
where the time goes in v15:
time: 63.6 us; the launch traced here: 63.1 us
  Pallas kernels  62.3 us (98%)
  between operations  0.82 us (1%)
    pallas_call x1, Pallas kernels, attn_call(): pl.pallas_call(attn_kernel, out_shape=(pltpu.VMEM((2, SLOT, 32, HEAD), BF...  59.8 us
    pallas_call x1, Pallas kernels, finish_call(): pl.pallas_call(finish_kernel, out_shape=(jax.ShapeDtypeStruct((256, 32, H...  2.46 us

profile of v15, /device:TPU:0, one launch (start us, length us, event | category | flops | bytes accessed | tf_op | source)
XLA Modules:
  0.0 63.1 jit_solution(11489742523031137286)
XLA Ops:
  0.6 59.8 %attn.1 = (bf16[2,128,32,128]{3,2,1,0:T(8,128)(2,1)S(1)}, bf16[2,128,32,128]{3,2,1,0:T(8,128)(2,1)S(1)}, bf16[8,2,2,128,128]{4,3,2,1,0:T(8,128)(2,1)S(1)}, f32[2,32,128]{2,1,0:T(8,128)S(1)}, s32[3]{0:T(128)S(4)}) custom-call(s32[3]{0:T(128)} %cu_hbm.1, s32[1,256]{1,0:T(1,128)} %bitcast.2, bf16[256,32,128]{2,1,0:T(8,128)(2,1)} %q.1, bf16[256,8,128]{2,1,0:T(8,128)(2,1)} %k.1, ...), custom_call_target="tpu_custom_call" | custom-call | tf_op jit(solution)/shard_map/attn/pallas_call | solution.py:565
  60.5 2.5 %finish.1 = (bf16[256,32,128]{2,1,0:T(8,128)(2,1)}, bf16[256,32,128]{2,1,0:T(8,128)(2,1)}, bf16[256,8,128]{2,1,0:T(8,128)(2,1)}, bf16[256,8,128]{2,1,0:T(8,128)(2,1)}, f32[32,256]{1,0:T(8,128)}) custom-call(bf16[2,128,32,128]{3,2,1,0:T(8,128)(2,1)S(1)} %get-tuple-element.15.o_in, bf16[2,128,32,128]{3,2,1,0:T(8,128)(2,1)S(1)} %get-tuple-element.16.dq_in, ...), custom_call_target="tpu_custom_call" | custom-call | tf_op jit(solution)/shard_map/finish/pallas_call | solution.py:668

commit v16 on v15

--- a/solution.py
+++ b/solution.py
@@ -504,6 +504,11 @@
                     kv_first(to, up).wait_send()
         for h in range(HC):
             near_run(ch, h, lambda cp: cp.wait_send())
+            near_wait(h, 0)
+            if ch == 1:
+                pl.when(c == 1)(functools.partial(near_wait, h, 1))
+                if SW[h] < 2:
+                    pl.when(c == 0)(functools.partial(near_wait, h, 1, 2 - SW[h]))
         push_q.wait_send()
         push_do.wait_send()
         for cp in push_val:
@@ -525,7 +530,6 @@
             part_wait(4 * c + h, up, n)
             for w in range(n):
                 dkv_out[4 * c + h, up, w] = (dkv_acc[h, 2 * slot + w] + cross_in[4 * c + h, up, w]).astype(BF16)
-            near_wait(h, up, n)
             part_wait(4 * pc + h, up, n)
             for w in range(n):
                 dkv_out[4 * pc + h, up, w] = (near_in[h, up, w] + cross_in[4 * pc + h, up, w]).astype(BF16)
@@ -625,11 +629,10 @@
 
     def copies(i, x, out):
         runs = ((0, 0, 0, l0), (1, 0, l0, l0), (0, l0, 2 * l0, rest), (1, l0, SLOT + l0, rest))
-        return [pltpu.make_async_copy(x.at[up, pl.ds(at, n)], out.at[pl.ds(to, n)], sem.at[i, j])
-                for j, (up, at, to, n) in enumerate(runs)]
-
-    moves = copies(0, o_in, o_out) + copies(1, dq_in, dq_out)
-    for cp in moves:
+        return [pltpu.make_async_copy(x.at[up, pl.ds(at, n)], out.at[pl.ds(to, n)], sem.at[i])
+                for up, at, to, n in runs]
+
+    for cp in copies(0, o_in, o_out) + copies(1, dq_in, dq_out):
         cp.start()
 
     for w, dst in ((0, dk_t), (1, dv_t)):
@@ -639,10 +642,8 @@
                 dst[up, at] = jnp.transpose(dkv_in[:, up, w, at, :], (1, 0, 2))
                 return 0
             lax.fori_loop(0, SLOT // 16, body, 0)
-        more = copies(2 + w, dst, (dk_out, dv_out)[w])
-        for cp in more:
+        for cp in copies(2 + w, dst, (dk_out, dv_out)[w]):
             cp.start()
-        moves += more
 
     row = lax.broadcasted_iota(jnp.int32, (2 * SLOT, SLOT), 0)
     col = lax.broadcasted_iota(jnp.int32, (2 * SLOT, SLOT), 1)
@@ -658,8 +659,9 @@
     lse_t[...] = acc
     lse_move = pltpu.make_async_copy(lse_t, lse_out, lse_sem)
     lse_move.start()
-    for cp in moves + [lse_move]:
-        cp.wait()
+    for i, out in enumerate((o_out, dq_out, dk_out, dv_out)):
+        pltpu.make_async_copy(out, out, sem.at[i]).wait()
+    lse_move.wait()
 
 
 def finish_call(o_t, dq_t, dkv_hm, lse_hm, cu):
@@ -680,7 +682,7 @@
             pltpu.VMEM((2, SLOT, 8, HEAD), BF16),
             pltpu.VMEM((2, SLOT, 8, HEAD), BF16),
             pltpu.VMEM((32, 256), F32),
-            pltpu.SemaphoreType.DMA((4, 4)),
+            pltpu.SemaphoreType.DMA((4,)),
             pltpu.SemaphoreType.DMA,
         ],
         compiler_params=pltpu.CompilerParams(vmem_limit_bytes=16 * 1024 * 1024),

time: 63.6 us -> 63.5 us (level)
  no operation moved by 1% of the time
where the time goes in v16:
time: 63.5 us; the launch traced here: 63 us
  Pallas kernels  62.2 us (98%)
  between operations  0.82 us (1%)
    pallas_call x1, Pallas kernels, attn_call(): pl.pallas_call(attn_kernel, out_shape=(pltpu.VMEM((2, SLOT, 32, HEAD), BF...  59.8 us
    pallas_call x1, Pallas kernels, finish_call(): pl.pallas_call(finish_kernel, out_shape=(jax.ShapeDtypeStruct((256, 32, H...  2.37 us

profile of v16, /device:TPU:0, one launch (start us, length us, event | category | flops | bytes accessed | tf_op | source)
XLA Modules:
  0.0 63.0 jit_solution(7109265332808856640)
XLA Ops:
  0.6 59.8 %attn.1 = (bf16[2,128,32,128]{3,2,1,0:T(8,128)(2,1)S(1)}, bf16[2,128,32,128]{3,2,1,0:T(8,128)(2,1)S(1)}, bf16[8,2,2,128,128]{4,3,2,1,0:T(8,128)(2,1)S(1)}, f32[2,32,128]{2,1,0:T(8,128)S(1)}, s32[3]{0:T(128)S(4)}) custom-call(s32[3]{0:T(128)} %cu_hbm.1, s32[1,256]{1,0:T(1,128)} %bitcast.2, bf16[256,32,128]{2,1,0:T(8,128)(2,1)} %q.1, bf16[256,8,128]{2,1,0:T(8,128)(2,1)} %k.1, ...), custom_call_target="tpu_custom_call" | custom-call | tf_op jit(solution)/shard_map/attn/pallas_call | solution.py:569
  60.5 2.4 %finish.1 = (bf16[256,32,128]{2,1,0:T(8,128)(2,1)}, bf16[256,32,128]{2,1,0:T(8,128)(2,1)}, bf16[256,8,128]{2,1,0:T(8,128)(2,1)}, bf16[256,8,128]{2,1,0:T(8,128)(2,1)}, f32[32,256]{1,0:T(8,128)}) custom-call(bf16[2,128,32,128]{3,2,1,0:T(8,128)(2,1)S(1)} %get-tuple-element.15.o_in, bf16[2,128,32,128]{3,2,1,0:T(8,128)(2,1)S(1)} %get-tuple-element.16.dq_in, ...), custom_call_target="tpu_custom_call" | custom-call | tf_op jit(solution)/shard_map/finish/pallas_call | solution.py:670

commit v17 on v16

--- a/solution.py
+++ b/solution.py
@@ -302,8 +302,8 @@
         def point(h, where):
             if ch == 0:
                 return
-            kv = {(0, 3): 2, (1, 2): 3}
-            swaps = {(1, 4): (0, 1), (2, 4): (2,)}
+            kv = {(0, 1): 2, (0, 4): 3}
+            swaps = {(1, 2): (0,), (1, 4): (1,), (2, 4): (2,)}
             parts = {(2, 2): (0,), (2, 4): (1,), (3, 4): (2, 3)}
             for at in range(HC):
                 if not any((at, where) in d for d in (kv, swaps, parts)):

time: 63.5 us -> 63.3 us (level)
  no operation moved by 1% of the time
where the time goes in v17:
time: 63.3 us; the launch traced here: 63 us
  Pallas kernels  62.2 us (98%)
  between operations  0.82 us (1%)
    pallas_call x1, Pallas kernels, attn_call(): pl.pallas_call(attn_kernel, out_shape=(pltpu.VMEM((2, SLOT, 32, HEAD), BF...  59.8 us
    pallas_call x1, Pallas kernels, finish_call(): pl.pallas_call(finish_kernel, out_shape=(jax.ShapeDtypeStruct((256, 32, H...  2.36 us

profile of v17, /device:TPU:0, one launch (start us, length us, event | category | flops | bytes accessed | tf_op | source)
XLA Modules:
  0.0 63.0 jit_solution(430760943865219947)
XLA Ops:
  0.6 59.8 %attn.1 = (bf16[2,128,32,128]{3,2,1,0:T(8,128)(2,1)S(1)}, bf16[2,128,32,128]{3,2,1,0:T(8,128)(2,1)S(1)}, bf16[8,2,2,128,128]{4,3,2,1,0:T(8,128)(2,1)S(1)}, f32[2,32,128]{2,1,0:T(8,128)S(1)}, s32[3]{0:T(128)S(4)}) custom-call(s32[3]{0:T(128)} %cu_hbm.1, s32[1,256]{1,0:T(1,128)} %bitcast.2, bf16[256,32,128]{2,1,0:T(8,128)(2,1)} %q.1, bf16[256,8,128]{2,1,0:T(8,128)(2,1)} %k.1, ...), custom_call_target="tpu_custom_call" | custom-call | tf_op jit(solution)/shard_map/attn/pallas_call | solution.py:569
  60.5 2.4 %finish.1 = (bf16[256,32,128]{2,1,0:T(8,128)(2,1)}, bf16[256,32,128]{2,1,0:T(8,128)(2,1)}, bf16[256,8,128]{2,1,0:T(8,128)(2,1)}, bf16[256,8,128]{2,1,0:T(8,128)(2,1)}, f32[32,256]{1,0:T(8,128)}) custom-call(bf16[2,128,32,128]{3,2,1,0:T(8,128)(2,1)S(1)} %get-tuple-element.15.o_in, bf16[2,128,32,128]{3,2,1,0:T(8,128)(2,1)S(1)} %get-tuple-element.16.dq_in, ...), custom_call_target="tpu_custom_call" | custom-call | tf_op jit(solution)/shard_map/finish/pallas_call | solution.py:670

commit v18 on v17

--- a/solution.py
+++ b/solution.py
@@ -133,10 +133,10 @@
                 kv_first(to, up).start()
 
     send_first(0)
+    kv_relayout(1)
+    send_first(1)
     for cp in (ld_q, ld_do, push_q, push_do):
         cp.start()
-    kv_relayout(1)
-    send_first(1)
     for h in range(HC):
         kv_push(h, 0, True).start()
     ld_val.wait()

time: 63.3 us -> 63.7 us (level)
  no operation moved by 1% of the time
where the time goes in v18:
time: 63.7 us; the launch traced here: 63 us
  Pallas kernels  62.2 us (98%)
  between operations  0.82 us (1%)
    pallas_call x1, Pallas kernels, attn_call(): pl.pallas_call(attn_kernel, out_shape=(pltpu.VMEM((2, SLOT, 32, HEAD), BF...  59.8 us
    pallas_call x1, Pallas kernels, finish_call(): pl.pallas_call(finish_kernel, out_shape=(jax.ShapeDtypeStruct((256, 32, H...  2.36 us

profile of v18, /device:TPU:0, one launch (start us, length us, event | category | flops | bytes accessed | tf_op | source)
XLA Modules:
  0.0 63.0 jit_solution(15366878668167703584)
XLA Ops:
  0.6 59.8 %attn.1 = (bf16[2,128,32,128]{3,2,1,0:T(8,128)(2,1)S(1)}, bf16[2,128,32,128]{3,2,1,0:T(8,128)(2,1)S(1)}, bf16[8,2,2,128,128]{4,3,2,1,0:T(8,128)(2,1)S(1)}, f32[2,32,128]{2,1,0:T(8,128)S(1)}, s32[3]{0:T(128)S(4)}) custom-call(s32[3]{0:T(128)} %cu_hbm.1, s32[1,256]{1,0:T(1,128)} %bitcast.2, bf16[256,32,128]{2,1,0:T(8,128)(2,1)} %q.1, bf16[256,8,128]{2,1,0:T(8,128)(2,1)} %k.1, ...), custom_call_target="tpu_custom_call" | custom-call | tf_op jit(solution)/shard_map/attn/pallas_call | solution.py:569
  60.5 2.4 %finish.1 = (bf16[256,32,128]{2,1,0:T(8,128)(2,1)}, bf16[256,32,128]{2,1,0:T(8,128)(2,1)}, bf16[256,8,128]{2,1,0:T(8,128)(2,1)}, bf16[256,8,128]{2,1,0:T(8,128)(2,1)}, f32[32,256]{1,0:T(8,128)}) custom-call(bf16[2,128,32,128]{3,2,1,0:T(8,128)(2,1)S(1)} %get-tuple-element.15.o_in, bf16[2,128,32,128]{3,2,1,0:T(8,128)(2,1)S(1)} %get-tuple-element.16.dq_in, ...), custom_call_target="tpu_custom_call" | custom-call | tf_op jit(solution)/shard_map/finish/pallas_call | solution.py:670
